TPU v7x, 256 devices: a whole 4x4x8 slice. The times are simulated.
256 devices in a mesh: row: 32 (over y, z), col: 8 (over x, core).
Axes of the slice: x: 4, y: 4, z: 8, core: 2. Of those that a mesh axis runs over, the one named last changes fastest.
Arguments:
- weights: bfloat16 [2, 8192, 8192], P(None, 'row', 'col'), may hold values from -0.0625 to 0.0625
- preact: float32 [2, 2, 8192], P(None, None, 'row'), may hold values from -2.5 to 2.5
- panel: bfloat16 [2, 64, 8192], P(None, None, 'col'), may hold values from -6 to 6
Outputs:
- basis_out: float32 [2, 64, 8192], P(None, None, 'col')
All inputs are finite; a program needn't handle non-finite values.
Results may differ from a plain program's by a relative error of at most 0.035.
Values may be sent and summed in bfloat16 or wider, within the bound.
No kernel may reach another device: no remote copies, remote signals or barrier semaphores. Data moves between devices by JAX's collectives and lax.ppermute only.
A program may use at most 64 MiB of HBM per device.

v0:
```python
from functools import partial

import jax
import jax.numpy as jnp
from jax import lax
from jax.sharding import PartitionSpec as P

WIDTH = 8192
ITERS = 2


def in_blocks(x, dim, length):
    lengths = x.shape
    tiles = x.reshape(*lengths[:dim], length, lengths[dim] // length, *lengths[dim + 1 :])
    return jnp.moveaxis(tiles, dim, 0)


def sum_at_owner(x, axis, dim):
    tiles = in_blocks(x, dim, lax.axis_size(axis))
    arrived = lax.all_to_all(tiles, axis, split_axis=0, concat_axis=0, tiled=True)
    return arrived.astype(jnp.float32).sum(axis=0)


def from_everyone(x, axis):
    length = lax.axis_size(axis)
    return lax.all_to_all(jnp.broadcast_to(x[None], (length, *x.shape)), axis, 0, 0, tiled=True)


def in_order(tiles, dim):
    tiles = jnp.moveaxis(tiles, 0, dim)
    lengths = tiles.shape
    return tiles.reshape(*lengths[:dim], lengths[dim] * lengths[dim + 1], *lengths[dim + 2 :])


def gathered_copies(x, axis, dim):
    tiles = from_everyone(x, axis)
    return in_order(tiles, dim)


def picked(x, axis, root):
    return lax.dynamic_index_in_dim(lax.all_gather(x, axis), root, 0, keepdims=False)


def over_copies(x, axis):
    everything = from_everyone(x, axis)
    return jnp.sum(everything.astype(jnp.float32), axis=0)


def on_device(weights, preact, panel):
    slopes = 1.0 - jnp.tanh(preact) ** 2
    layers = weights.shape[0]
    span_ratio = lax.axis_size("row") // lax.axis_size("col")
    row_index = lax.axis_index("row")
    current = panel
    basis_out = panel.astype(jnp.float32)
    for iteration in range(ITERS):
        cotangent = None
        for layer_at in range(layers):
            partial_out = jnp.einsum(
                "bki,oi->bko", current, weights[layer_at], preferred_element_type=jnp.float32
            )
            summed = sum_at_owner(partial_out.astype(jnp.bfloat16), "col", 1)
            scaled = (slopes[:, layer_at, None, :] * summed).astype(jnp.bfloat16)
            if layer_at + 1 < layers:
                spread = gathered_copies(scaled, "row", 2)
                current = lax.all_to_all(spread, "col", split_axis=2, concat_axis=1, tiled=True)
            else:
                cotangent = gathered_copies(scaled, "col", 1)
        image_panel = None
        for layer_at in reversed(range(layers)):
            weighted = (slopes[:, layer_at, None, :] * cotangent).astype(jnp.bfloat16)
            partial_in = jnp.einsum(
                "bko,oi->bki", weighted, weights[layer_at], preferred_element_type=jnp.float32
            )
            if layer_at == 0:
                pieces = sum_at_owner(partial_in.astype(jnp.bfloat16), "row", 2).astype(
                    jnp.bfloat16
                )
                image_panel = gathered_copies(pieces, "row", 2)
            else:
                pieces = sum_at_owner(partial_in.astype(jnp.bfloat16), "row", 2).astype(
                    jnp.bfloat16
                )
                gathered = gathered_copies(pieces, "row", 2)
                chosen = picked(gathered, "col", row_index // span_ratio)
                width_row = cotangent.shape[2]
                cotangent = lax.dynamic_slice_in_dim(
                    chosen, row_index % span_ratio * width_row, width_row, 2
                )
        local_gram = jnp.einsum(
            "bkw,bjw->bkj", image_panel, image_panel, preferred_element_type=jnp.float32
        )
        gram_sum = over_copies(local_gram.astype(jnp.bfloat16), "col").astype(jnp.float32)
        factor = jnp.linalg.cholesky(gram_sum / WIDTH)
        basis_out = jax.vmap(partial(jax.scipy.linalg.solve_triangular, lower=True))(
            factor, image_panel.astype(jnp.float32)
        )
        current = basis_out.astype(jnp.bfloat16)
    return basis_out


def solution(mesh):
    return jax.shard_map(
        on_device,
        mesh=mesh,
        in_specs=(P(None, "row", "col"), P(None, None, "row"), P(None, None, "col")),
        out_specs=P(None, None, "col"),
        check_vma=False,
    )
```

profile of v0, /device:TPU:1, one launch (start us, length us, event | category | flops | bytes accessed | tf_op | source)
XLA Modules:
  0.0 452.3 jit_solution(6569241820050055485)
XLA Ops:
  6.5 0.9 copy-done
  7.5 1.3 fusion
  8.8 0.6 copy.162
  9.5 6.5 %all-to-all-start = ((bf16[8,2,8,256]{3,2,1,0:T(8,128)(2,1)}), bf16[8,2,8,256]{3,2,1,0:T(8,128)(2,1)S(1)}, u32[]{:S(2)}, u32[]{:S(2)}) async-start(bf16[8,2,8,256]{3,2,1,0:T(8,128)(2,1)} %bitcast.159), calls=%async_computation | async-start | bytes 131072 | tf_op jit(solution)/shard_map/all_to_all | solution.py:20
  15.9 0.7 multiply_subtract_fusion
  16.6 4.2 all-to-all-done
  20.9 20.0 %all_to_all.126 = bf16[32,2,8,256]{3,2,1,0:T(8,128)(2,1)S(1)} all-to-all(bf16[32,2,8,256]{3,2,1,0:T(8,128)(2,1)S(1)} %broadcast_in_dim.24), channel_id=1, replica_groups=mesh['row'=32,'col'=8] {'row'}, dimensions={0} | all-to-all | bytes 524288 | tf_op jit(solution)/shard_map/all_to_all | solution.py:26
  40.8 6.8 %copy.135 = bf16[2,8,32,256]{1,0,3,2:T(2,128)(2,1)} copy(bf16[2,8,32,256]{3,1,0,2:T(8,128)(2,1)S(1)} %bitcast.184) | data formatting | bytes 524288 | tf_op jit(solution)/shard_map/reshape | solution.py:32
  47.7 5.8 %reshape.89 = bf16[8,2,8192]{2,1,0:T(2,128)(2,1)S(1)} reshape(bf16[8192,2,8]{2,1,0:T(2,128)(2,1)} %bitcast.166) | data formatting | bytes 524288
  53.4 12.6 %all_to_all.127 = bf16[8,2,8192]{2,1,0:T(2,128)(2,1)S(1)} all-to-all(bf16[8,2,8192]{2,1,0:T(2,128)(2,1)S(1)} %reshape.89), channel_id=1, replica_groups=mesh['row'=32,'col'=8] {'col'}, dimensions={0} | all-to-all | bytes 524288 | tf_op jit(solution)/shard_map/all_to_all | solution.py:66
  66.1 5.9 %reshape.90 = bf16[8192,2,8]{2,1,0:T(2,128)(2,1)} reshape(bf16[8,2,8192]{2,1,0:T(2,128)(2,1)S(1)} %all_to_all.127) | data formatting | bytes 524288
  72.0 9.0 %copy.94 = bf16[2,8,8,1024]{3,1,2,0:T(8,128)(2,1)S(1)} copy(bf16[2,8,8,1024]{1,0,3,2:T(2,128)(2,1)} %bitcast.167) | data formatting | bytes 524288 | tf_op jit(solution)/shard_map/all_to_all | solution.py:66
  81.3 0.6 copy.161
  81.9 4.3 all-to-all-start.3
  86.2 4.9 %all-to-all-done.3 = bf16[8,2,8,256]{3,2,1,0:T(8,128)(2,1)S(1)} async-done(((bf16[8,2,8,256]{3,2,1,0:T(8,128)(2,1)}), bf16[8,2,8,256]{3,2,1,0:T(8,128)(2,1)S(1)}, u32[]{:S(2)}, u32[]{:S(2)}) %all-to-all-start.3) | async-done | bytes 65568 | tf_op jit(solution)/shard_map/all_to_all | solution.py:20
  91.1 8.0 %all_to_all.128 = bf16[8,2,8,256]{3,2,1,0:T(8,128)(2,1)S(1)} all-to-all(bf16[8,2,8,256]{3,2,1,0:T(8,128)(2,1)S(1)} %broadcast_in_dim.25), channel_id=1, replica_groups=mesh['row'=32,'col'=8] {'col'}, dimensions={0} | all-to-all | bytes 131072 | tf_op jit(solution)/shard_map/all_to_all | solution.py:26
  99.7 0.4 reshape.91
  100.1 13.6 %all_to_all.129 = bf16[32,2,2048]{2,1,0:T(2,128)(2,1)S(1)} all-to-all(bf16[32,2,2048]{2,1,0:T(2,128)(2,1)S(1)} %reshape.91), channel_id=1, replica_groups=mesh['row'=32,'col'=8] {'row'}, dimensions={0} | all-to-all | bytes 524288 | tf_op jit(solution)/shard_map/all_to_all | solution.py:20
  113.7 0.4 reshape.92
  114.3 0.4 reshape.93
  114.7 15.7 %all_to_all.130 = bf16[32,2,2048]{2,1,0:T(2,128)(2,1)S(1)} all-to-all(bf16[32,2,2048]{2,1,0:T(2,128)(2,1)S(1)} %reshape.93), channel_id=1, replica_groups=mesh['row'=32,'col'=8] {'row'}, dimensions={0} | all-to-all | bytes 524288 | tf_op jit(solution)/shard_map/all_to_all | solution.py:26
  130.4 0.4 reshape.94
  130.8 0.9 copy.100
  131.8 25.4 %all-gather.3.cloned.1.call-done = bf16[8,2,64,1024]{3,2,1,0:T(8,128)(2,1)} async-done(((bf16[1,2,64,1024]{3,2,1,0:T(8,128)(2,1)}), bf16[8,2,64,1024]{3,2,1,0:T(8,128)(2,1)}) %all-gather.3.cloned.1.call-update) | async-done | bytes 2097168 | tf_op jit(solution)/shard_map/all_gather | solution.py:41
  157.2 1.2 convolution_convert_fusion.3
  158.7 0.4 reshape.95
  159.1 19.3 %all_to_all.131 = bf16[32,2,2048]{2,1,0:T(2,128)(2,1)S(1)} all-to-all(bf16[32,2,2048]{2,1,0:T(2,128)(2,1)S(1)} %reshape.95), channel_id=1, replica_groups=mesh['row'=32,'col'=8] {'row'}, dimensions={0} | all-to-all | bytes 524288 | tf_op jit(solution)/shard_map/all_to_all | solution.py:20
  178.5 0.4 reshape.96
  179.1 0.4 reshape.97
  179.5 16.1 %all_to_all.132 = bf16[32,2,2048]{2,1,0:T(2,128)(2,1)S(1)} all-to-all(bf16[32,2,2048]{2,1,0:T(2,128)(2,1)S(1)} %reshape.97), channel_id=1, replica_groups=mesh['row'=32,'col'=8] {'row'}, dimensions={0} | all-to-all | bytes 524288 | tf_op jit(solution)/shard_map/all_to_all | solution.py:26
  196.4 0.9 reshape.99
  197.3 7.1 %all-to-all-start.9 = ((bf16[8,2,4096]{2,1,0:T(2,128)(2,1)}), bf16[8,2,4096]{2,1,0:T(2,128)(2,1)S(1)}, u32[]{:S(2)}, u32[]{:S(2)}) async-start(bf16[8,2,4096]{2,1,0:T(2,128)(2,1)} %reshape.99), calls=%async_computation.9 | async-start | bytes 262144 | tf_op jit(solution)/shard_map/all_to_all | solution.py:26
  204.5 5.0 %all-to-all-done.9 = bf16[8,2,4096]{2,1,0:T(2,128)(2,1)S(1)} async-done(((bf16[8,2,4096]{2,1,0:T(2,128)(2,1)}), bf16[8,2,4096]{2,1,0:T(2,128)(2,1)S(1)}, u32[]{:S(2)}, u32[]{:S(2)}) %all-to-all-start.9) | async-done | bytes 131104 | tf_op jit(solution)/shard_map/all_to_all | solution.py:26
  210.0 11.7 %custom-call.8 = f32[2,64,64]{2,1,0:T(8,128)S(1)} custom-call(f32[2,64,64]{2,1,0:T(8,128)S(1)} %fusion.36), custom_call_target="Cholesky" | custom-call | tf_op jit(solution)/shard_map/jit(cholesky)/cholesky | solution.py:94
  222.0 9.8 %custom-call.9 = f32[2,1,64,64]{2,3,1,0:T(8,128)S(1)} custom-call(f32[2,1,64,64]{3,2,1,0:T(8,128)S(1)} %select_bitcast_fusion.1), custom_call_target="InvertDiagBlocksLowerTriangular" | custom-call | tf_op jit(solution)/shard_map/vmap(jit(_solve_triangular))/triangular_solve | solution.py:95
  231.8 0.6 convolution_convert_fusion.2
  232.8 8.1 %all_to_all.133 = bf16[8,2,8,256]{3,2,1,0:T(8,128)(2,1)S(1)} all-to-all(bf16[8,2,8,256]{3,2,1,0:T(8,128)(2,1)S(1)} %bitcast.186), channel_id=1, replica_groups=mesh['row'=32,'col'=8] {'col'}, dimensions={0} | all-to-all | bytes 131072 | tf_op jit(solution)/shard_map/all_to_all | solution.py:20
  241.0 13.7 %all_to_all.134 = bf16[32,2,8,256]{3,2,1,0:T(8,128)(2,1)S(1)} all-to-all(bf16[32,2,8,256]{3,2,1,0:T(8,128)(2,1)S(1)} %broadcast_in_dim.29), channel_id=1, replica_groups=mesh['row'=32,'col'=8] {'row'}, dimensions={0} | all-to-all | bytes 524288 | tf_op jit(solution)/shard_map/all_to_all | solution.py:26
  254.6 6.8 %copy.136 = bf16[2,8,32,256]{1,0,3,2:T(2,128)(2,1)} copy(bf16[2,8,32,256]{3,1,0,2:T(8,128)(2,1)S(1)} %bitcast.185) | data formatting | bytes 524288 | tf_op jit(solution)/shard_map/reshape | solution.py:32
  261.4 5.8 %reshape.101 = bf16[8,2,8192]{2,1,0:T(2,128)(2,1)S(1)} reshape(bf16[8192,2,8]{2,1,0:T(2,128)(2,1)} %bitcast.168) | data formatting | bytes 524288
  267.2 12.6 %all_to_all.135 = bf16[8,2,8192]{2,1,0:T(2,128)(2,1)S(1)} all-to-all(bf16[8,2,8192]{2,1,0:T(2,128)(2,1)S(1)} %reshape.101), channel_id=1, replica_groups=mesh['row'=32,'col'=8] {'col'}, dimensions={0} | all-to-all | bytes 524288 | tf_op jit(solution)/shard_map/all_to_all | solution.py:66
  279.8 5.9 %reshape.102 = bf16[8192,2,8]{2,1,0:T(2,128)(2,1)} reshape(bf16[8,2,8192]{2,1,0:T(2,128)(2,1)S(1)} %all_to_all.135) | data formatting | bytes 524288
  285.8 8.9 %copy.113 = bf16[2,8,8,1024]{3,1,2,0:T(8,128)(2,1)S(1)} copy(bf16[2,8,8,1024]{1,0,3,2:T(2,128)(2,1)} %bitcast.169) | data formatting | bytes 524288 | tf_op jit(solution)/shard_map/all_to_all | solution.py:66
  295.0 8.3 %all_to_all.136 = bf16[8,2,8,256]{3,2,1,0:T(8,128)(2,1)S(1)} all-to-all(bf16[8,2,8,256]{3,2,1,0:T(8,128)(2,1)S(1)} %bitcast.187), channel_id=1, replica_groups=mesh['row'=32,'col'=8] {'col'}, dimensions={0} | all-to-all | bytes 131072 | tf_op jit(solution)/shard_map/all_to_all | solution.py:20
  303.3 8.0 %all_to_all.137 = bf16[8,2,8,256]{3,2,1,0:T(8,128)(2,1)S(1)} all-to-all(bf16[8,2,8,256]{3,2,1,0:T(8,128)(2,1)S(1)} %broadcast_in_dim.30), channel_id=1, replica_groups=mesh['row'=32,'col'=8] {'col'}, dimensions={0} | all-to-all | bytes 131072 | tf_op jit(solution)/shard_map/all_to_all | solution.py:26
  311.9 0.4 reshape.103
  312.3 13.6 %all_to_all.138 = bf16[32,2,2048]{2,1,0:T(2,128)(2,1)S(1)} all-to-all(bf16[32,2,2048]{2,1,0:T(2,128)(2,1)S(1)} %reshape.103), channel_id=1, replica_groups=mesh['row'=32,'col'=8] {'row'}, dimensions={0} | all-to-all | bytes 524288 | tf_op jit(solution)/shard_map/all_to_all | solution.py:20
  325.9 0.4 reshape.104
  326.5 0.4 reshape.105
  326.9 15.7 %all_to_all.139 = bf16[32,2,2048]{2,1,0:T(2,128)(2,1)S(1)} all-to-all(bf16[32,2,2048]{2,1,0:T(2,128)(2,1)S(1)} %reshape.105), channel_id=1, replica_groups=mesh['row'=32,'col'=8] {'row'}, dimensions={0} | all-to-all | bytes 524288 | tf_op jit(solution)/shard_map/all_to_all | solution.py:26
  342.5 0.4 reshape.106
  343.0 0.9 copy.119
  343.9 25.5 %all-gather.5.cloned.1.call-done = bf16[8,2,64,1024]{3,2,1,0:T(8,128)(2,1)} async-done(((bf16[1,2,64,1024]{3,2,1,0:T(8,128)(2,1)}), bf16[8,2,64,1024]{3,2,1,0:T(8,128)(2,1)}) %all-gather.5.cloned.1.call-update) | async-done | bytes 2097168 | tf_op jit(solution)/shard_map/all_gather | solution.py:41
  369.4 1.2 convolution_convert_fusion
  370.9 0.4 reshape.107
  371.3 19.3 %all_to_all.140 = bf16[32,2,2048]{2,1,0:T(2,128)(2,1)S(1)} all-to-all(bf16[32,2,2048]{2,1,0:T(2,128)(2,1)S(1)} %reshape.107), channel_id=1, replica_groups=mesh['row'=32,'col'=8] {'row'}, dimensions={0} | all-to-all | bytes 524288 | tf_op jit(solution)/shard_map/all_to_all | solution.py:20
  391.2 0.4 reshape.109
  391.6 16.1 %all_to_all.141 = bf16[32,2,2048]{2,1,0:T(2,128)(2,1)S(1)} all-to-all(bf16[32,2,2048]{2,1,0:T(2,128)(2,1)S(1)} %reshape.109), channel_id=1, replica_groups=mesh['row'=32,'col'=8] {'row'}, dimensions={0} | all-to-all | bytes 524288 | tf_op jit(solution)/shard_map/all_to_all | solution.py:26
  408.5 0.9 reshape.111
  409.4 7.0 %all-to-all-start.19 = ((bf16[8,2,4096]{2,1,0:T(2,128)(2,1)}), bf16[8,2,4096]{2,1,0:T(2,128)(2,1)S(1)}, u32[]{:S(2)}, u32[]{:S(2)}) async-start(bf16[8,2,4096]{2,1,0:T(2,128)(2,1)} %reshape.111), calls=%async_computation.19 | async-start | bytes 262144 | tf_op jit(solution)/shard_map/all_to_all | solution.py:26
  416.7 5.0 %all-to-all-done.19 = bf16[8,2,4096]{2,1,0:T(2,128)(2,1)S(1)} async-done(((bf16[8,2,4096]{2,1,0:T(2,128)(2,1)}), bf16[8,2,4096]{2,1,0:T(2,128)(2,1)S(1)}, u32[]{:S(2)}, u32[]{:S(2)}) %all-to-all-start.19) | async-done | bytes 131104 | tf_op jit(solution)/shard_map/all_to_all | solution.py:26
  422.2 11.7 %custom-call.10 = f32[2,64,64]{2,1,0:T(8,128)S(1)} custom-call(f32[2,64,64]{2,1,0:T(8,128)S(1)} %fusion.34), custom_call_target="Cholesky" | custom-call | tf_op jit(solution)/shard_map/jit(cholesky)/cholesky | solution.py:94
  434.2 9.8 %custom-call.11 = f32[2,1,64,64]{2,3,1,0:T(8,128)S(1)} custom-call(f32[2,1,64,64]{3,2,1,0:T(8,128)S(1)} %select_bitcast_fusion), custom_call_target="InvertDiagBlocksLowerTriangular" | custom-call | tf_op jit(solution)/shard_map/vmap(jit(_solve_triangular))/triangular_solve | solution.py:95
  444.0 1.4 fusion.12
  (82 shorter events, 7.7 us)
Async XLA Ops:
  6.5 1.0 copy-start
  9.5 11.3 %all-to-all-start = ((bf16[8,2,8,256]{3,2,1,0:T(8,128)(2,1)}), bf16[8,2,8,256]{3,2,1,0:T(8,128)(2,1)S(1)}, u32[]{:S(2)}, u32[]{:S(2)}) async-start(bf16[8,2,8,256]{3,2,1,0:T(8,128)(2,1)} %bitcast.159), calls=%async_computation | async-start | bytes 131072 | tf_op jit(solution)/shard_map/all_to_all | solution.py:20
  72.0 9.0 %copy-start.1 = (bf16[2,256,1024]{2,1,0:T(8,128)(2,1)S(1)}, bf16[2,256,1024]{2,1,0:T(8,128)(2,1)}, u32[]{:S(2)}) copy-start(bf16[2,256,1024]{2,1,0:T(8,128)(2,1)} %param.6) | copy-start | bytes 3145732
  81.9 9.2 %all-to-all-start.3 = ((bf16[8,2,8,256]{3,2,1,0:T(8,128)(2,1)}), bf16[8,2,8,256]{3,2,1,0:T(8,128)(2,1)S(1)}, u32[]{:S(2)}, u32[]{:S(2)}) async-start(bf16[8,2,8,256]{3,2,1,0:T(8,128)(2,1)} %bitcast.158), calls=%async_computation.3 | async-start | bytes 131072 | tf_op jit(solution)/shard_map/all_to_all | solution.py:20
  86.2 71.0 %all-gather.3.cloned.1.call-start = ((), (), s32[]{:S(2)}) async-start(), calls=%async_computation.20 | async-start | bytes 2359296 | tf_op jit(solution)/shard_map/all_gather | solution.py:41
  197.3 12.3 %all-to-all-start.9 = ((bf16[8,2,4096]{2,1,0:T(2,128)(2,1)}), bf16[8,2,4096]{2,1,0:T(2,128)(2,1)S(1)}, u32[]{:S(2)}, u32[]{:S(2)}) async-start(bf16[8,2,4096]{2,1,0:T(2,128)(2,1)} %reshape.99), calls=%async_computation.9 | async-start | bytes 262144 | tf_op jit(solution)/shard_map/all_to_all | solution.py:26
  204.3 165.1 %all-gather.5.cloned.1.call-start = ((), (), s32[]{:S(2)}) async-start(), calls=%async_computation.21 | async-start | bytes 2359296 | tf_op jit(solution)/shard_map/all_gather | solution.py:41
  409.4 12.3 %all-to-all-start.19 = ((bf16[8,2,4096]{2,1,0:T(2,128)(2,1)}), bf16[8,2,4096]{2,1,0:T(2,128)(2,1)S(1)}, u32[]{:S(2)}, u32[]{:S(2)}) async-start(bf16[8,2,4096]{2,1,0:T(2,128)(2,1)} %reshape.111), calls=%async_computation.19 | async-start | bytes 262144 | tf_op jit(solution)/shard_map/all_to_all | solution.py:26
Sparse Core Ops, SparseCore 0:
  131.9 25.3 all-gather.2
  344.0 25.3 all-gather.4
where the time goes:
time: 454 us; the launch traced here: 452 us
  blocking collectives  221 us (49%)
  local copies, waits for them, and re-layouts  70 us (15%)
  waiting for transfers between devices  70 us (15%)
  other arithmetic  45 us (10%)
  starting transfers between devices  24.9 us (5%)
  between operations  14.1 us (3%)
  matrix products  7.79 us (2%)
    all_to_all x8, blocking collectives, from_everyone(): lax.all_to_all(jnp.broadcast_to(x[None], (length, *x.shape)), axis, 0, 0,...  113 us
    all_to_all x6, blocking collectives, sum_at_owner(): lax.all_to_all(tiles, axis, split_axis=0, concat_axis=0, tiled=True)  82.2 us
    all_gather x2, waiting for transfers between devices, picked(): lax.all_gather(x, axis)  50.9 us
    unnamed x34, local copies, waits for them, and re-layouts  32.9 us
    all_to_all x2, blocking collectives, on_device(): lax.all_to_all(spread, 'col', split_axis=2, concat_axis=1, tiled=True)  25.2 us
    another operation x7, other arithmetic, on_device(): factor = jnp.linalg.cholesky(gram_sum / WIDTH)  23.8 us
    another operation x5, other arithmetic, on_device(): jax.vmap(partial(jax.scipy.linalg.solve_triangular, lower=True))  19.8 us
    all_to_all x2, local copies, waits for them, and re-layouts, on_device(): lax.all_to_all(spread, 'col', split_axis=2, concat_axis=1, tiled=True)  17.9 us
  transfers between devices with their start and end apart: 6, of which 6 were waited for; matrix products, arithmetic and copies ran while one was open for 0% of the time, Pallas kernels for 0%

commit v1 on v0

v1 whole, which is shorter than its diff:
```python
import jax
import jax.numpy as jnp
from jax import lax
from jax.experimental import pallas as pl
from jax.experimental.pallas import tpu as pltpu
from jax.sharding import Mesh, PartitionSpec as P

WIDTH = 8192
ITERS = 2
BF16 = jnp.bfloat16
F32 = jnp.float32


def dot_t(a, w):
    return lax.dot_general(a, w, (((1,), (1,)), ((), ())), preferred_element_type=F32)


def dot_n(a, w):
    return lax.dot_general(a, w, (((1,), (0,)), ((), ())), preferred_element_type=F32)


def exchange(tiles, axis):
    return lax.all_to_all(tiles, axis, split_axis=0, concat_axis=0, tiled=True)


def to_all(x, axis, count):
    return exchange(jnp.broadcast_to(x[None], (count, *x.shape)), axis)


def total(tiles):
    return jnp.sum(tiles.astype(F32), axis=0)


def inverse_factor(gram):
    n = gram.shape[0]
    rows = lax.broadcasted_iota(jnp.int32, (n, n), 0)
    cols = lax.broadcasted_iota(jnp.int32, (n, n), 1)
    eye = (rows == cols).astype(F32)
    both = jnp.concatenate([eye, gram * (1.0 / WIDTH)], axis=1)
    row_of = lax.broadcasted_iota(jnp.int32, (n, 2 * n), 0)
    for j in range(n - 1):
        column = jnp.broadcast_to(both[:, n + j : n + j + 1], (n, 2 * n))
        pivot_row = both[j : j + 1, :] / column[j : j + 1, :]
        both = both - jnp.where(row_of > j, column, 0.0) * pivot_row
    pivots = jnp.sum(both[:, n:] * eye, axis=1, keepdims=True)
    return both[:, :n] / jnp.sqrt(pivots)


def exact_dot(a, b):
    return lax.dot_general(
        a, b, (((1,), (0,)), ((), ())), precision=lax.Precision.HIGHEST, preferred_element_type=F32
    )


def gram_of_parts(parts_ref, start, rank):
    parts = [parts_ref[i, :, start : start + 2 * rank].astype(F32) for i in range(parts_ref.shape[0])]
    summed = parts[0]
    for part in parts[1:]:
        summed = summed + part
    return summed[:, :rank] + summed[:, rank:]


def normalized_forward(arrived, slope, width):
    rank = arrived.shape[1]

    def kernel(arrived_ref, slope_ref, out_ref):
        inverse = inverse_factor(gram_of_parts(arrived_ref, width, rank))
        summed = arrived_ref[0, :, :width].astype(F32)
        for i in range(1, arrived_ref.shape[0]):
            summed = summed + arrived_ref[i, :, :width].astype(F32)
        out_ref[...] = (slope_ref[...] * exact_dot(inverse, summed)).astype(BF16)

    return pl.pallas_call(
        kernel, out_shape=jax.ShapeDtypeStruct((rank, width), BF16), name="normalized_forward"
    )(arrived, slope)


def normalized_panel(arrived, own, other):
    rank = arrived.shape[1]

    def kernel(arrived_ref, own_ref, other_ref, own_out, other_out):
        inverse = inverse_factor(gram_of_parts(arrived_ref, 0, rank))
        own_out[...] = exact_dot(inverse, own_ref[...].astype(F32))
        other_out[...] = exact_dot(inverse, other_ref[...].astype(F32))

    shape = jax.ShapeDtypeStruct(own.shape, F32)
    return pl.pallas_call(kernel, out_shape=(shape, shape), name="normalized_panel")(arrived, own, other)


def high_low(gram):
    high = lax.reduce_precision(gram, 8, 7)
    return jnp.concatenate([high.astype(BF16), (gram - high).astype(BF16)], axis=1)


def make(n_x, n_y, n_z):
    swap = [(i * n_x + j, j * n_x + i) for i in range(n_y) for j in range(n_x)]
    flip = [(0, 1), (1, 0)]

    def on_device(weights, preact, panel):
        core = lax.axis_index("core")
        first = core == 0
        inputs, rank, width_in = panel.shape
        width_row = weights.shape[1]
        w1_own, w2_own = weights[0], weights[1]

        partial_out = jnp.einsum("bki,oi->bko", panel, w1_own, preferred_element_type=F32)
        mine = jnp.where(first, partial_out[0], partial_out[1])
        theirs = jnp.where(first, partial_out[1], partial_out[0])
        summed_out = mine + lax.ppermute(theirs, "core", flip)

        slopes = 1.0 - jnp.tanh(jnp.where(first, preact[0], preact[1])) ** 2
        slope_1 = slopes[0:1]
        slope_2 = lax.ppermute(slopes[1:2], ("y", "x"), swap)
        w2_moved = lax.ppermute(w2_own, ("y", "x"), swap)
        w2_other = lax.ppermute(w2_moved, "core", flip)
        w2_low = jnp.where(first, w2_moved, w2_other)
        w2_high = jnp.where(first, w2_other, w2_moved)
        w2 = jnp.concatenate([w2_low, w2_high], axis=1)
        w1_other = lax.ppermute(w1_own, "core", flip)

        own = other = None
        for iteration in range(ITERS):
            if iteration == 0:
                forward = (slope_1 * total(to_all(summed_out.astype(BF16), "x", n_x))).astype(BF16)
            else:
                partial_out = dot_t(own, w1_own) + dot_t(other, w1_other)
                gram = dot_t(own, own) + dot_t(other, other)
                message = jnp.concatenate([partial_out.astype(BF16), high_low(gram)], axis=1)
                forward = normalized_forward(to_all(message, "x", n_x), slope_1, width_row)
            spread = to_all(forward, "z", n_z)
            spread = jnp.moveaxis(spread, 0, 1).reshape(rank, n_z * width_row)
            partial_out = dot_t(spread, w2)
            forward = (slope_2 * total(to_all(partial_out.astype(BF16), "y", n_y))).astype(BF16)
            weighted = (slope_2 * forward.astype(F32)).astype(BF16)
            partial_in = dot_n(weighted, w2).astype(BF16)
            blocks = jnp.moveaxis(partial_in.reshape(rank, n_z, width_row), 1, 0)
            summed = total(exchange(blocks, "z")).astype(BF16)
            cotangent = total(to_all(summed, "x", n_x)).astype(BF16)
            weighted = (slope_1 * cotangent.astype(F32)).astype(BF16)
            partial_in = jnp.concatenate([dot_n(weighted, w1_own), dot_n(weighted, w1_other)], axis=1)
            groups = rank // 8
            cuts = n_y * n_z // groups
            length = 2 * width_in // cuts
            pieces = partial_in.astype(BF16).reshape(groups, 8, cuts, length)
            pieces = jnp.moveaxis(pieces, 2, 1).reshape(groups * cuts, 8, length)
            piece = total(exchange(pieces, ("y", "z"))).astype(BF16)
            image = to_all(piece, ("y", "z"), groups * cuts).reshape(groups, cuts, 8, length)
            image = jnp.moveaxis(image, 1, 2).reshape(rank, 2 * width_in)
            own, other = image[:, :width_in], image[:, width_in:]
        gram = dot_t(own, own) + dot_t(other, other)
        basis_own, basis_other = normalized_panel(to_all(high_low(gram), "x", n_x), own, other)
        received = lax.ppermute(basis_other, "core", flip)
        return jnp.stack([jnp.where(first, basis_own, received), jnp.where(first, received, basis_own)])

    return on_device


def solution(mesh):
    n_x, n_y, n_z = 4, 4, 8
    fine = Mesh(mesh.devices.reshape(n_y, n_z, n_x, 2), ("y", "z", "x", "core"))
    return jax.shard_map(
        make(n_x, n_y, n_z),
        mesh=fine,
        in_specs=(P(None, ("y", "z"), ("x", "core")), P(None, None, ("y", "z")), P(None, None, ("x", "core"))),
        out_specs=P(None, None, ("x", "core")),
        check_vma=False,
    )
```

time: 454 us -> 244 us (0.54)
  blocking collectives: 221 us -> 135 us
  local copies, waits for them, and re-layouts: 70 us -> 7.33 us
  other arithmetic: 45 us -> 2.44 us
  waiting for transfers between devices: 70 us -> 38.4 us
  Pallas kernels: 0 us -> 15 us
  starting transfers between devices: 24.9 us -> 39.8 us
  between operations: 14.1 us -> 0.34 us
    all_to_all x16 -> x11, blocking collectives: 221 us -> 135 us  [exchange(): return lax.all_to_all(tiles, axis, split_axis=0, concat_axis=0, tiled=True)]
    all_gather x2 -> x0, waiting for transfers between devices: 50.9 us -> none  [picked(): lax.all_gather(x, axis)]
    another operation x12 -> x2, other arithmetic: 43.6 us -> 1.84 us  [on_device(): jnp.stack([jnp.where(first, basis_own, received), jnp.where(first, receiv...]
    unnamed x34 -> x8, local copies, waits for them, and re-layouts: 32.9 us -> 1.58 us
    ppermute x0 -> x6, starting transfers between devices: none -> 23.4 us  [the longest x1 15.6 us: on_device(): received = lax.ppermute(basis_other, 'core', flip)]
    all_to_all x4, waiting for transfers between devices: 19.1 us -> 37 us  [exchange(): return lax.all_to_all(tiles, axis, split_axis=0, concat_axis=0, tiled=True)]
    all_to_all x2 -> x0, local copies, waits for them, and re-layouts: 17.9 us -> none  [on_device(): lax.all_to_all(spread, 'col', split_axis=2, concat_axis=1, tiled=True)]
    pallas_call x0 -> x2, Pallas kernels: none -> 15 us  [the longest x1 7.76 us: normalized_panel(): pl.pallas_call(kernel, out_shape=(shape, shape), name='normalized_panel')]
  transfers between devices with their start and end apart: 6 -> 10, of which waited for: 6 -> 5; matrix products, arithmetic and copies ran while one was open for 0% -> 1% of each run, Pallas kernels for 0% -> 0%
where the time goes in v1:
time: 244 us; the launch traced here: 243 us
  blocking collectives  135 us (55%)
  starting transfers between devices  39.8 us (16%)
  waiting for transfers between devices  38.4 us (16%)
  Pallas kernels  15 us (6%)
  local copies, waits for them, and re-layouts  7.33 us (3%)
  matrix products  4.94 us (2%)
  other arithmetic  2.44 us (1%)
    all_to_all x11, blocking collectives, exchange(): return lax.all_to_all(tiles, axis, split_axis=0, concat_axis=0, tiled=True)  135 us
    all_to_all x4, waiting for transfers between devices, exchange(): return lax.all_to_all(tiles, axis, split_axis=0, concat_axis=0, tiled=True)  37 us
    all_to_all x4, starting transfers between devices, exchange(): return lax.all_to_all(tiles, axis, split_axis=0, concat_axis=0, tiled=True)  16.4 us
    ppermute x1, starting transfers between devices, on_device(): received = lax.ppermute(basis_other, 'core', flip)  15.6 us
    pallas_call x1, Pallas kernels, normalized_panel(): pl.pallas_call(kernel, out_shape=(shape, shape), name='normalized_panel')  7.76 us
    pallas_call x1, Pallas kernels, normalized_forward(): pl.pallas_call(kernel, out_shape=jax.ShapeDtypeStruct((rank, width), BF16...  7.25 us
  transfers between devices with their start and end apart: 10, of which 5 were waited for; matrix products, arithmetic and copies ran while one was open for 1% of the time, Pallas kernels for 0%

profile of v1, /device:TPU:1, one launch (start us, length us, event | category | flops | bytes accessed | tf_op | source)
XLA Modules:
  0.0 243.0 jit_solution(1031252837826181284)
XLA Ops:
  0.0 0.9 copy-done
  1.0 1.3 fusion.1
  2.3 0.0 copy-start.3
  2.3 3.3 %collective-permute-start.1 = (f32[64,256]{1,0:T(8,128)S(1)}, f32[64,256]{1,0:T(8,128)S(1)}, u32[]{:S(2)}, u32[]{:S(2)}) collective-permute-start(f32[64,256]{1,0:T(8,128)S(1)} %select_bitcast_fusion.2), channel_id=1, source_target_pairs={{0,1},{1,0},{2,3},{3,2},{4,5},{5,4},{6,7},{7,6},{8,9},{9,8},{10,11... | collective-permute-start | bytes 196616 | tf_op jit(solution)/shard_map/ppermute | solution.py:109
  5.6 0.9 slice_bitcast_fusion
  6.5 0.7 collective-permute-start.2
  7.2 0.6 broadcast_in_dim.22
  7.9 6.4 %all-to-all-start = ((bf16[4,64,256]{2,1,0:T(8,128)(2,1)}), bf16[4,64,256]{2,1,0:T(8,128)(2,1)S(1)}, u32[]{:S(2)}, u32[]{:S(2)}) async-start(bf16[4,64,256]{2,1,0:T(8,128)(2,1)} %broadcast_in_dim.22), calls=%async_computation | async-start | bytes 262144 | tf_op jit(solution)/shard_map/all_to_all | solution.py:23
  14.3 0.6 slice_bitcast_fusion.3
  14.8 21.3 %all-to-all-done = bf16[4,64,256]{2,1,0:T(8,128)(2,1)S(1)} async-done(((bf16[4,64,256]{2,1,0:T(8,128)(2,1)}), bf16[4,64,256]{2,1,0:T(8,128)(2,1)S(1)}, u32[]{:S(2)}, u32[]{:S(2)}) %all-to-all-start) | async-done | bytes 131104 | tf_op jit(solution)/shard_map/all_to_all | solution.py:23
  36.2 0.0 collective-permute-done.2
  36.2 1.3 collective-permute-start.3
  37.5 20.4 %all_to_all.75 = bf16[8,64,256]{2,1,0:T(8,128)(2,1)S(1)} all-to-all(bf16[8,64,256]{2,1,0:T(8,128)(2,1)S(1)} %broadcast_in_dim.23), channel_id=1, replica_groups=mesh['y'=4,'z'=8,'x'=4,'core'=2] {'z'}, dimensions={0} | all-to-all | bytes 524288 | tf_op jit(solution)/shard_map/all_to_all | solution.py:23
  57.8 0.0 collective-permute-done.3
  57.8 0.1 broadcast_select_fusion.1
  57.9 0.4 convolution_convert_fusion.7
  58.4 0.7 broadcast_in_dim.24
  59.0 3.3 %all-to-all-start.2 = ((bf16[4,64,256]{2,1,0:T(8,128)(2,1)}), bf16[4,64,256]{2,1,0:T(8,128)(2,1)S(1)}, u32[]{:S(2)}, u32[]{:S(2)}) async-start(bf16[4,64,256]{2,1,0:T(8,128)(2,1)} %broadcast_in_dim.24), calls=%async_computation.2 | async-start | bytes 262144 | tf_op jit(solution)/shard_map/all_to_all | solution.py:23
  62.4 0.7 collective-permute-start
  63.0 4.1 %all-to-all-done.2 = bf16[4,64,256]{2,1,0:T(8,128)(2,1)S(1)} async-done(((bf16[4,64,256]{2,1,0:T(8,128)(2,1)}), bf16[4,64,256]{2,1,0:T(8,128)(2,1)S(1)}, u32[]{:S(2)}, u32[]{:S(2)}) %all-to-all-start.2) | async-done | bytes 131104 | tf_op jit(solution)/shard_map/all_to_all | solution.py:23
  67.2 0.0 collective-permute-done
  67.2 0.3 convolution_convert_fusion.1
  67.5 0.7 copy.19
  68.2 3.4 %all-to-all-start.3 = ((bf16[8,64,256]{2,1,0:T(8,128)(2,1)}), bf16[8,64,256]{2,1,0:T(8,128)(2,1)S(1)}, u32[]{:S(2)}, u32[]{:S(2)}) async-start(bf16[8,64,256]{2,1,0:T(8,128)(2,1)} %bitcast.71), calls=%async_computation.3 | async-start | bytes 524288 | tf_op jit(solution)/shard_map/all_to_all | solution.py:23
  71.6 1.9 collective-permute-start.4
  73.5 7.7 %all-to-all-done.3 = bf16[8,64,256]{2,1,0:T(8,128)(2,1)S(1)} async-done(((bf16[8,64,256]{2,1,0:T(8,128)(2,1)}), bf16[8,64,256]{2,1,0:T(8,128)(2,1)S(1)}, u32[]{:S(2)}, u32[]{:S(2)}) %all-to-all-start.3) | async-done | bytes 262176 | tf_op jit(solution)/shard_map/all_to_all | solution.py:23
  81.3 10.6 %all_to_all.76 = bf16[4,64,256]{2,1,0:T(8,128)(2,1)S(1)} all-to-all(bf16[4,64,256]{2,1,0:T(8,128)(2,1)S(1)} %broadcast_in_dim.25), channel_id=1, replica_groups=mesh['y'=4,'z'=8,'x'=4,'core'=2] {'x'}, dimensions={0} | all-to-all | bytes 262144 | tf_op jit(solution)/shard_map/all_to_all | solution.py:23
  91.9 0.2 convolution_convert_fusion.5
  92.1 0.2 convolution_convert_fusion.4
  92.3 14.8 %all_to_all.77 = bf16[32,8,512]{2,1,0:T(8,128)(2,1)S(1)} all-to-all(bf16[32,8,512]{2,1,0:T(8,128)(2,1)S(1)} %bitcast.75), channel_id=1, replica_groups=mesh['y'=4,'z'=8,'x'=4,'core'=2] {'y','z'}, dimensions={0} | all-to-all | bytes 524288 | tf_op jit(solution)/shard_map/all_to_all | solution.py:23
  107.2 0.1 reduce_sum.103
  107.3 14.1 %all_to_all.78 = bf16[32,8,512]{2,1,0:T(8,128)(2,1)S(1)} all-to-all(bf16[32,8,512]{2,1,0:T(8,128)(2,1)S(1)} %broadcast_in_dim.26), channel_id=1, replica_groups=mesh['y'=4,'z'=8,'x'=4,'core'=2] {'y','z'}, dimensions={0} | all-to-all | bytes 524288 | tf_op jit(solution)/shard_map/all_to_all | solution.py:23
  121.4 0.2 fusion.6
  121.5 0.3 fusion.8
  121.8 0.2 reduce-precision_convert_fusion.1
  122.0 0.3 fusion
  122.3 0.1 pad_maximum_fusion.4
  122.4 8.2 %all_to_all.79.arrived_ref = bf16[4,64,384]{2,1,0:T(8,128)(2,1)} all-to-all(bf16[4,64,384]{2,1,0:T(8,128)(2,1)S(1)} %broadcast_in_dim.27), channel_id=1, replica_groups=mesh['y'=4,'z'=8,'x'=4,'core'=2] {'x'}, dimensions={0} | all-to-all | bytes 393216 | tf_op jit(solution)/shard_map/all_to_all | solution.py:23
  130.6 7.2 %normalized_forward.1 = bf16[64,256]{1,0:T(8,128)(2,1)} custom-call(bf16[4,64,384]{2,1,0:T(8,128)(2,1)} %all_to_all.79.arrived_ref, f32[1,256]{1,0:T(1,128)} %get-tuple-element.21.slope_ref), custom_call_target="tpu_custom_call" | custom-call | tf_op jit(solution)/shard_map/normalized_forward/pallas_call | solution.py:73
  137.9 0.8 broadcast_in_dim.28
  138.7 12.4 %all_to_all.80 = bf16[8,64,256]{2,1,0:T(8,128)(2,1)S(1)} all-to-all(bf16[8,64,256]{2,1,0:T(8,128)(2,1)S(1)} %broadcast_in_dim.28), channel_id=1, replica_groups=mesh['y'=4,'z'=8,'x'=4,'core'=2] {'z'}, dimensions={0} | all-to-all | bytes 524288 | tf_op jit(solution)/shard_map/all_to_all | solution.py:23
  151.0 0.4 convolution_convert_fusion.6
  151.5 7.5 %all_to_all.81 = bf16[4,64,256]{2,1,0:T(8,128)(2,1)S(1)} all-to-all(bf16[4,64,256]{2,1,0:T(8,128)(2,1)S(1)} %broadcast_in_dim.29), channel_id=1, replica_groups=mesh['y'=4,'z'=8,'x'=4,'core'=2] {'y'}, dimensions={0} | all-to-all | bytes 262144 | tf_op jit(solution)/shard_map/all_to_all | solution.py:23
  159.0 0.3 convolution_convert_fusion
  159.4 11.7 %all_to_all.82 = bf16[8,64,256]{2,1,0:T(8,128)(2,1)S(1)} all-to-all(bf16[8,64,256]{2,1,0:T(8,128)(2,1)S(1)} %bitcast.79), channel_id=1, replica_groups=mesh['y'=4,'z'=8,'x'=4,'core'=2] {'z'}, dimensions={0} | all-to-all | bytes 524288 | tf_op jit(solution)/shard_map/all_to_all | solution.py:23
  171.2 7.2 %all_to_all.83 = bf16[4,64,256]{2,1,0:T(8,128)(2,1)S(1)} all-to-all(bf16[4,64,256]{2,1,0:T(8,128)(2,1)S(1)} %broadcast_in_dim.30), channel_id=1, replica_groups=mesh['y'=4,'z'=8,'x'=4,'core'=2] {'x'}, dimensions={0} | all-to-all | bytes 262144 | tf_op jit(solution)/shard_map/all_to_all | solution.py:23
  178.4 0.2 convolution_convert_fusion.3
  178.6 0.2 convolution_convert_fusion.2
  178.9 12.6 %all_to_all.84 = bf16[32,8,512]{2,1,0:T(8,128)(2,1)S(1)} all-to-all(bf16[32,8,512]{2,1,0:T(8,128)(2,1)S(1)} %bitcast.76), channel_id=1, replica_groups=mesh['y'=4,'z'=8,'x'=4,'core'=2] {'y','z'}, dimensions={0} | all-to-all | bytes 524288 | tf_op jit(solution)/shard_map/all_to_all | solution.py:23
  191.5 0.1 reduce_sum.107
  191.6 15.2 %all_to_all.85 = bf16[32,8,512]{2,1,0:T(8,128)(2,1)S(1)} all-to-all(bf16[32,8,512]{2,1,0:T(8,128)(2,1)S(1)} %broadcast_in_dim.31), channel_id=1, replica_groups=mesh['y'=4,'z'=8,'x'=4,'core'=2] {'y','z'}, dimensions={0} | all-to-all | bytes 524288 | tf_op jit(solution)/shard_map/all_to_all | solution.py:23
  206.8 0.2 fusion.16
  207.0 0.2 reduce-precision_convert_fusion
  207.2 0.1 pad_maximum_fusion.5
  207.3 0.6 broadcast_in_dim.32
  207.9 3.3 %all-to-all-start.14 = ((bf16[4,64,128]{2,1,0:T(8,128)(2,1)}), bf16[4,64,128]{2,1,0:T(8,128)(2,1)S(1)}, u32[]{:S(2)}, u32[]{:S(2)}) async-start(bf16[4,64,128]{2,1,0:T(8,128)(2,1)} %broadcast_in_dim.32), calls=%async_computation.14 | async-start | bytes 131072 | tf_op jit(solution)/shard_map/all_to_all | solution.py:23
  211.2 0.7 fusion.18
  211.9 3.9 %all-to-all-done.14.arrived_ref = bf16[4,64,128]{2,1,0:T(8,128)(2,1)S(1)} async-done(((bf16[4,64,128]{2,1,0:T(8,128)(2,1)}), bf16[4,64,128]{2,1,0:T(8,128)(2,1)S(1)}, u32[]{:S(2)}, u32[]{:S(2)}) %all-to-all-start.14) | async-done | bytes 65568 | tf_op jit(solution)/shard_map/all_to_all | solution.py:23
  215.8 0.6 copy-done.2
  216.4 7.8 %normalized_panel.1 = (f32[64,1024]{1,0:T(8,128)}, f32[64,1024]{1,0:T(8,128)}) custom-call(bf16[4,64,128]{2,1,0:T(8,128)(2,1)} %copy-done.2, bf16[64,1024]{1,0:T(8,128)(2,1)} %get-tuple-element.16.own_ref, bf16[64,1024]{1,0:T(8,128)(2,1)} %get-tuple-element.15.other_ref), custom_call_target="tpu_custom_call" | custom-call | tf_op jit(solution)/shard_map/normalized_panel/pallas_call | solution.py:87
  224.2 15.6 %collective-permute-start.5 = (f32[64,1024]{1,0:T(8,128)}, f32[64,1024]{1,0:T(8,128)S(1)}, u32[]{:S(2)}, u32[]{:S(2)}) collective-permute-start(f32[64,1024]{1,0:T(8,128)} %get-tuple-element.8), channel_id=1, source_target_pairs={{0,1},{1,0},{2,3},{3,2},{4,5},{5,4},{6,7},{7,6},{8,9},{9,8},{10,11... | collective-permute-start | bytes 786440 | tf_op jit(solution)/shard_map/ppermute | solution.py:152
  239.8 1.4 collective-permute-done.5
  241.1 1.0 select_bitcast_fusion.1
  242.1 0.8 pad_maximum_fusion.1
  (30 shorter events, 0.4 us)
Async XLA Ops:
  0.0 1.0 copy-start
  0.0 5.6 %copy-start.1 = (bf16[2,256,1024]{2,1,0:T(8,128)(2,1)S(1)}, bf16[2,256,1024]{2,1,0:T(8,128)(2,1)}, u32[]{:S(2)}) copy-start(bf16[2,256,1024]{2,1,0:T(8,128)(2,1)} %param.3) | copy-start | bytes 3145732
  2.3 4.9 %copy-start.3 = (f32[2,2,256]{2,1,0:T(2,128)S(1)}, f32[2,2,256]{2,1,0:T(2,128)}, u32[]{:S(2)}) copy-start(f32[2,2,256]{2,1,0:T(2,128)} %param.4) | copy-start | bytes 12292
  2.3 4.9 %collective-permute-start.1 = (f32[64,256]{1,0:T(8,128)S(1)}, f32[64,256]{1,0:T(8,128)S(1)}, u32[]{:S(2)}, u32[]{:S(2)}) collective-permute-start(f32[64,256]{1,0:T(8,128)S(1)} %select_bitcast_fusion.2), channel_id=1, source_target_pairs={{0,1},{1,0},{2,3},{3,2},{4,5},{5,4},{6,7},{7,6},{8,9},{9,8},{10,11... | collective-permute-start | bytes 196616 | tf_op jit(solution)/shard_map/ppermute | solution.py:109
  6.5 29.7 %collective-permute-start.2 = (bf16[256,1024]{1,0:T(8,128)(2,1)S(1)}, bf16[256,1024]{1,0:T(8,128)(2,1)S(1)}, u32[]{:S(2)}, u32[]{:S(2)}) collective-permute-start(bf16[256,1024]{1,0:T(8,128)(2,1)S(1)} %get-tuple-element.11), channel_id=1, source_target_pairs={{0,0},{2,64},{4,128},{6,192},{64,2},{66,66},{68,130},{70,194},{128... | collective-permute-start | bytes 1572872 | tf_op jit(solution)/shard_map/ppermute | solution.py:114
  7.9 28.3 %all-to-all-start = ((bf16[4,64,256]{2,1,0:T(8,128)(2,1)}), bf16[4,64,256]{2,1,0:T(8,128)(2,1)S(1)}, u32[]{:S(2)}, u32[]{:S(2)}) async-start(bf16[4,64,256]{2,1,0:T(8,128)(2,1)} %broadcast_in_dim.22), calls=%async_computation | async-start | bytes 262144 | tf_op jit(solution)/shard_map/all_to_all | solution.py:23
  36.2 21.7 %collective-permute-start.3 = (bf16[256,1024]{1,0:T(8,128)(2,1)S(1)}, bf16[256,1024]{1,0:T(8,128)(2,1)S(1)}, u32[]{:S(2)}, u32[]{:S(2)}) collective-permute-start(bf16[256,1024]{1,0:T(8,128)(2,1)S(1)} %collective-permute-done.2), channel_id=1, source_target_pairs={{0,1},{1,0},{2,3},{3,2},{4,5},{5,4},{6,7},{7,6},{8,9},{9,8},{10,11... | collective-permute-start | bytes 1572872 | tf_op jit(solution)/shard_map/ppermute | solution.py:115
  59.0 8.1 %all-to-all-start.2 = ((bf16[4,64,256]{2,1,0:T(8,128)(2,1)}), bf16[4,64,256]{2,1,0:T(8,128)(2,1)S(1)}, u32[]{:S(2)}, u32[]{:S(2)}) async-start(bf16[4,64,256]{2,1,0:T(8,128)(2,1)} %broadcast_in_dim.24), calls=%async_computation.2 | async-start | bytes 262144 | tf_op jit(solution)/shard_map/all_to_all | solution.py:23
  62.4 4.8 %collective-permute-start = (f32[1,256]{1,0:T(1,128)S(1)}, f32[1,256]{1,0:T(1,128)S(1)}, u32[]{:S(2)}, u32[]{:S(2)}) collective-permute-start(f32[1,256]{1,0:T(1,128)S(1)} %get-tuple-element.22), channel_id=1, source_target_pairs={{0,0},{2,64},{4,128},{6,192},{64,2},{66,66},{68,130},{70,194},{128... | collective-permute-start | bytes 3080 | tf_op jit(solution)/shard_map/ppermute | solution.py:113
  68.2 13.0 %all-to-all-start.3 = ((bf16[8,64,256]{2,1,0:T(8,128)(2,1)}), bf16[8,64,256]{2,1,0:T(8,128)(2,1)S(1)}, u32[]{:S(2)}, u32[]{:S(2)}) async-start(bf16[8,64,256]{2,1,0:T(8,128)(2,1)} %bitcast.71), calls=%async_computation.3 | async-start | bytes 524288 | tf_op jit(solution)/shard_map/all_to_all | solution.py:23
  71.6 20.5 %collective-permute-start.4 = (bf16[256,1024]{1,0:T(8,128)(2,1)}, bf16[256,1024]{1,0:T(8,128)(2,1)S(1)}, u32[]{:S(2)}, u32[]{:S(2)}) collective-permute-start(bf16[256,1024]{1,0:T(8,128)(2,1)} %get-tuple-element.12), channel_id=1, source_target_pairs={{0,1},{1,0},{2,3},{3,2},{4,5},{5,4},{6,7},{7,6},{8,9},{9,8},{10,11... | collective-permute-start | bytes 1572872 | tf_op jit(solution)/shard_map/ppermute | solution.py:119
  207.9 7.9 %all-to-all-start.14 = ((bf16[4,64,128]{2,1,0:T(8,128)(2,1)}), bf16[4,64,128]{2,1,0:T(8,128)(2,1)S(1)}, u32[]{:S(2)}, u32[]{:S(2)}) async-start(bf16[4,64,128]{2,1,0:T(8,128)(2,1)} %broadcast_in_dim.32), calls=%async_computation.14 | async-start | bytes 131072 | tf_op jit(solution)/shard_map/all_to_all | solution.py:23
  215.8 0.6 copy-start.2
  224.2 17.0 %collective-permute-start.5 = (f32[64,1024]{1,0:T(8,128)}, f32[64,1024]{1,0:T(8,128)S(1)}, u32[]{:S(2)}, u32[]{:S(2)}) collective-permute-start(f32[64,1024]{1,0:T(8,128)} %get-tuple-element.8), channel_id=1, source_target_pairs={{0,1},{1,0},{2,3},{3,2},{4,5},{5,4},{6,7},{7,6},{8,9},{9,8},{10,11... | collective-permute-start | bytes 786440 | tf_op jit(solution)/shard_map/ppermute | solution.py:152

commit v2 on v1

--- a/solution.py
+++ b/solution.py
@@ -33,17 +33,34 @@
 
 def inverse_factor(gram):
     n = gram.shape[0]
+    count = n // 8
     rows = lax.broadcasted_iota(jnp.int32, (n, n), 0)
     cols = lax.broadcasted_iota(jnp.int32, (n, n), 1)
-    eye = (rows == cols).astype(F32)
-    both = jnp.concatenate([eye, gram * (1.0 / WIDTH)], axis=1)
-    row_of = lax.broadcasted_iota(jnp.int32, (n, 2 * n), 0)
-    for j in range(n - 1):
-        column = jnp.broadcast_to(both[:, n + j : n + j + 1], (n, 2 * n))
-        pivot_row = both[j : j + 1, :] / column[j : j + 1, :]
-        both = both - jnp.where(row_of > j, column, 0.0) * pivot_row
-    pivots = jnp.sum(both[:, n:] * eye, axis=1, keepdims=True)
-    return both[:, :n] / jnp.sqrt(pivots)
+    both = jnp.concatenate([(rows == cols).astype(F32), gram * (1.0 / WIDTH)], axis=1)
+    blocks = [both[8 * i : 8 * i + 8] for i in range(count)]
+    row_of = lax.broadcasted_iota(jnp.int32, (8, 2 * n), 0)
+    done = []
+    for k in range(count):
+        live = range(k, count)
+        columns = [
+            {i: jnp.broadcast_to(blocks[i][:, n + 8 * k + t : n + 8 * k + t + 1], (8, 2 * n)) for i in live}
+            for t in range(8)
+        ]
+        scale = jnp.zeros((8, 2 * n), F32)
+        for t in range(8):
+            inverse = 1.0 / columns[t][k][t : t + 1, :]
+            scale = jnp.where(row_of == t, inverse, scale)
+            factors = {i: columns[t][i] * inverse for i in live}
+            factors[k] = jnp.where(row_of > t, factors[k], 0.0)
+            for u in range(t + 1, 8):
+                entry = columns[u][k][t : t + 1, :]
+                for i in live:
+                    columns[u][i] = columns[u][i] - factors[i] * entry
+            pivot_row = blocks[k][t : t + 1, :]
+            for i in live:
+                blocks[i] = blocks[i] - factors[i] * pivot_row
+        done.append(blocks[k] * jnp.sqrt(scale))
+    return jnp.concatenate(done, axis=0)[:, :n]
 
 
 def exact_dot(a, b):
@@ -111,17 +128,22 @@
         slopes = 1.0 - jnp.tanh(jnp.where(first, preact[0], preact[1])) ** 2
         slope_1 = slopes[0:1]
         slope_2 = lax.ppermute(slopes[1:2], ("y", "x"), swap)
-        w2_moved = lax.ppermute(w2_own, ("y", "x"), swap)
-        w2_other = lax.ppermute(w2_moved, "core", flip)
-        w2_low = jnp.where(first, w2_moved, w2_other)
-        w2_high = jnp.where(first, w2_other, w2_moved)
-        w2 = jnp.concatenate([w2_low, w2_high], axis=1)
+
+        def moved(block):
+            here = lax.ppermute(block, ("y", "x"), swap)
+            there = lax.ppermute(here, "core", flip)
+            return jnp.concatenate([jnp.where(first, here, there), jnp.where(first, there, here)], axis=1)
+
+        half = width_row // 2
+        w2_top = moved(w2_own[:half])
         w1_other = lax.ppermute(w1_own, "core", flip)
 
         own = other = None
         for iteration in range(ITERS):
             if iteration == 0:
                 forward = (slope_1 * total(to_all(summed_out.astype(BF16), "x", n_x))).astype(BF16)
+                forward, w2_rest = lax.optimization_barrier((forward, w2_own[half:]))
+                w2 = jnp.concatenate([w2_top, moved(w2_rest)], axis=0)
             else:
                 partial_out = dot_t(own, w1_own) + dot_t(other, w1_other)
                 gram = dot_t(own, own) + dot_t(other, other)
@@ -150,7 +172,8 @@
         gram = dot_t(own, own) + dot_t(other, other)
         basis_own, basis_other = normalized_panel(to_all(high_low(gram), "x", n_x), own, other)
         received = lax.ppermute(basis_other, "core", flip)
-        return jnp.stack([jnp.where(first, basis_own, received), jnp.where(first, received, basis_own)])
+        at = lax.broadcasted_iota(jnp.int32, (inputs, rank, width_in), 0)
+        return jnp.where(at == core, basis_own[None], received[None])
 
     return on_device
 

time: 244 us -> 228 us (0.934)
  blocking collectives: 135 us -> 115 us
  starting transfers between devices: 39.8 us -> 50.5 us
  Pallas kernels: 15 us -> 8.01 us
    all_to_all x11 -> x10, blocking collectives: 135 us -> 115 us  [exchange(): return lax.all_to_all(tiles, axis, split_axis=0, concat_axis=0, tiled=True)]
    all_to_all x4 -> x5, starting transfers between devices: 16.4 us -> 25.7 us  [exchange(): return lax.all_to_all(tiles, axis, split_axis=0, concat_axis=0, tiled=True)]
    pallas_call x1, Pallas kernels: 7.25 us -> 3.75 us  [normalized_forward(): pl.pallas_call(kernel, out_shape=jax.ShapeDtypeStruct((rank, width), BF16...]
    pallas_call x1, Pallas kernels: 7.76 us -> 4.26 us  [normalized_panel(): pl.pallas_call(kernel, out_shape=(shape, shape), name='normalized_panel')]
    all_to_all x4 -> x5, waiting for transfers between devices: 37 us -> 37.1 us  [exchange(): return lax.all_to_all(tiles, axis, split_axis=0, concat_axis=0, tiled=True)]
  transfers between devices with their start and end apart: 10 -> 13, of which waited for: 5 -> 7; matrix products, arithmetic and copies ran while one was open for 1% -> 1% of each run, Pallas kernels for 0% -> 0%
where the time goes in v2:
time: 228 us; the launch traced here: 227 us
  blocking collectives  115 us (50%)
  starting transfers between devices  50.5 us (22%)
  waiting for transfers between devices  38.6 us (17%)
  Pallas kernels  8.01 us (4%)
  local copies, waits for them, and re-layouts  7.29 us (3%)
  matrix products  4.96 us (2%)
  other arithmetic  2.48 us (1%)
    all_to_all x10, blocking collectives, exchange(): return lax.all_to_all(tiles, axis, split_axis=0, concat_axis=0, tiled=True)  115 us
    all_to_all x5, waiting for transfers between devices, exchange(): return lax.all_to_all(tiles, axis, split_axis=0, concat_axis=0, tiled=True)  37.1 us
    all_to_all x5, starting transfers between devices, exchange(): return lax.all_to_all(tiles, axis, split_axis=0, concat_axis=0, tiled=True)  25.7 us
    ppermute x1, starting transfers between devices, on_device(): received = lax.ppermute(basis_other, 'core', flip)  15.9 us
  transfers between devices with their start and end apart: 13, of which 7 were waited for; matrix products, arithmetic and copies ran while one was open for 1% of the time, Pallas kernels for 0%

profile of v2, /device:TPU:1, one launch (start us, length us, event | category | flops | bytes accessed | tf_op | source)
XLA Modules:
  0.0 227.1 jit_solution(1317506087651544244)
XLA Ops:
  0.0 0.9 copy-done
  1.0 1.4 fusion.1
  2.3 3.3 %collective-permute-start.1 = (f32[64,256]{1,0:T(8,128)S(1)}, f32[64,256]{1,0:T(8,128)S(1)}, u32[]{:S(2)}, u32[]{:S(2)}) collective-permute-start(f32[64,256]{1,0:T(8,128)S(1)} %select_bitcast_fusion), channel_id=1, source_target_pairs={{0,1},{1,0},{2,3},{3,2},{4,5},{5,4},{6,7},{7,6},{8,9},{9,8},{10,11... | collective-permute-start | bytes 196616 | tf_op jit(solution)/shard_map/ppermute | solution.py:126
  5.7 0.7 collective-permute-start.2
  6.4 0.1 collective-permute-done.1
  6.5 0.7 broadcast_in_dim.32
  7.2 6.3 %all-to-all-start = ((bf16[4,64,256]{2,1,0:T(8,128)(2,1)}), bf16[4,64,256]{2,1,0:T(8,128)(2,1)S(1)}, u32[]{:S(2)}, u32[]{:S(2)}) async-start(bf16[4,64,256]{2,1,0:T(8,128)(2,1)} %broadcast_in_dim.32), calls=%async_computation | async-start | bytes 262144 | tf_op jit(solution)/shard_map/all_to_all | solution.py:23
  13.5 0.6 slice_bitcast_fusion.4
  14.1 10.0 %all-to-all-done = bf16[4,64,256]{2,1,0:T(8,128)(2,1)S(1)} async-done(((bf16[4,64,256]{2,1,0:T(8,128)(2,1)}), bf16[4,64,256]{2,1,0:T(8,128)(2,1)S(1)}, u32[]{:S(2)}, u32[]{:S(2)}) %all-to-all-start) | async-done | bytes 131104 | tf_op jit(solution)/shard_map/all_to_all | solution.py:23
  24.1 0.7 collective-permute-start.4
  24.8 0.0 collective-permute-done.2
  24.8 1.3 collective-permute-start.3
  26.1 0.7 broadcast_in_dim.33
  26.8 8.2 %all-to-all-start.1 = ((bf16[8,64,256]{2,1,0:T(8,128)(2,1)}), bf16[8,64,256]{2,1,0:T(8,128)(2,1)S(1)}, u32[]{:S(2)}, u32[]{:S(2)}) async-start(bf16[8,64,256]{2,1,0:T(8,128)(2,1)} %broadcast_in_dim.33), calls=%async_computation.1 | async-start | bytes 524288 | tf_op jit(solution)/shard_map/all_to_all | solution.py:23
  35.0 0.0 collective-permute-done.4
  35.0 0.4 collective-permute-start.5
  35.4 11.9 %all-to-all-done.1 = bf16[8,64,256]{2,1,0:T(8,128)(2,1)S(1)} async-done(((bf16[8,64,256]{2,1,0:T(8,128)(2,1)}), bf16[8,64,256]{2,1,0:T(8,128)(2,1)S(1)}, u32[]{:S(2)}, u32[]{:S(2)}) %all-to-all-start.1) | async-done | bytes 262176 | tf_op jit(solution)/shard_map/all_to_all | solution.py:23
  47.4 0.4 convolution_convert_fusion.7
  47.9 0.7 broadcast_in_dim.34
  48.6 4.5 %all-to-all-start.2 = ((bf16[4,64,256]{2,1,0:T(8,128)(2,1)}), bf16[4,64,256]{2,1,0:T(8,128)(2,1)S(1)}, u32[]{:S(2)}, u32[]{:S(2)}) async-start(bf16[4,64,256]{2,1,0:T(8,128)(2,1)} %broadcast_in_dim.34), calls=%async_computation.2 | async-start | bytes 262144 | tf_op jit(solution)/shard_map/all_to_all | solution.py:23
  53.1 0.6 collective-permute-start
  53.8 4.2 %all-to-all-done.2 = bf16[4,64,256]{2,1,0:T(8,128)(2,1)S(1)} async-done(((bf16[4,64,256]{2,1,0:T(8,128)(2,1)}), bf16[4,64,256]{2,1,0:T(8,128)(2,1)S(1)}, u32[]{:S(2)}, u32[]{:S(2)}) %all-to-all-start.2) | async-done | bytes 131104 | tf_op jit(solution)/shard_map/all_to_all | solution.py:23
  58.0 0.3 convolution_convert_fusion.1
  58.3 0.7 copy.19
  59.0 3.4 %all-to-all-start.3 = ((bf16[8,64,256]{2,1,0:T(8,128)(2,1)}), bf16[8,64,256]{2,1,0:T(8,128)(2,1)S(1)}, u32[]{:S(2)}, u32[]{:S(2)}) async-start(bf16[8,64,256]{2,1,0:T(8,128)(2,1)} %bitcast.69), calls=%async_computation.3 | async-start | bytes 524288 | tf_op jit(solution)/shard_map/all_to_all | solution.py:23
  62.5 2.0 collective-permute-start.6
  64.5 7.2 %all-to-all-done.3 = bf16[8,64,256]{2,1,0:T(8,128)(2,1)S(1)} async-done(((bf16[8,64,256]{2,1,0:T(8,128)(2,1)}), bf16[8,64,256]{2,1,0:T(8,128)(2,1)S(1)}, u32[]{:S(2)}, u32[]{:S(2)}) %all-to-all-start.3) | async-done | bytes 262176 | tf_op jit(solution)/shard_map/all_to_all | solution.py:23
  71.7 11.1 %all_to_all.75 = bf16[4,64,256]{2,1,0:T(8,128)(2,1)S(1)} all-to-all(bf16[4,64,256]{2,1,0:T(8,128)(2,1)S(1)} %broadcast_in_dim.35), channel_id=1, replica_groups=mesh['y'=4,'z'=8,'x'=4,'core'=2] {'x'}, dimensions={0} | all-to-all | bytes 262144 | tf_op jit(solution)/shard_map/all_to_all | solution.py:23
  82.8 0.2 convolution_convert_fusion.5
  83.1 0.2 convolution_convert_fusion.4
  83.3 14.5 %all_to_all.76 = bf16[32,8,512]{2,1,0:T(8,128)(2,1)S(1)} all-to-all(bf16[32,8,512]{2,1,0:T(8,128)(2,1)S(1)} %bitcast.74), channel_id=1, replica_groups=mesh['y'=4,'z'=8,'x'=4,'core'=2] {'y','z'}, dimensions={0} | all-to-all | bytes 524288 | tf_op jit(solution)/shard_map/all_to_all | solution.py:23
  97.8 0.1 reduce_sum.103
  97.9 14.1 %all_to_all.77 = bf16[32,8,512]{2,1,0:T(8,128)(2,1)S(1)} all-to-all(bf16[32,8,512]{2,1,0:T(8,128)(2,1)S(1)} %broadcast_in_dim.36), channel_id=1, replica_groups=mesh['y'=4,'z'=8,'x'=4,'core'=2] {'y','z'}, dimensions={0} | all-to-all | bytes 524288 | tf_op jit(solution)/shard_map/all_to_all | solution.py:23
  111.9 0.3 fusion.8
  112.2 0.2 fusion.6
  112.4 0.2 reduce-precision_convert_fusion.1
  112.6 0.3 fusion
  112.9 0.1 pad_maximum_fusion.2
  113.0 8.4 %all_to_all.78.arrived_ref = bf16[4,64,384]{2,1,0:T(8,128)(2,1)} all-to-all(bf16[4,64,384]{2,1,0:T(8,128)(2,1)S(1)} %broadcast_in_dim.37), channel_id=1, replica_groups=mesh['y'=4,'z'=8,'x'=4,'core'=2] {'x'}, dimensions={0} | all-to-all | bytes 393216 | tf_op jit(solution)/shard_map/all_to_all | solution.py:23
  121.4 3.7 %normalized_forward.1 = bf16[64,256]{1,0:T(8,128)(2,1)} custom-call(bf16[4,64,384]{2,1,0:T(8,128)(2,1)} %all_to_all.78.arrived_ref, f32[1,256]{1,0:T(1,128)} %get-tuple-element.25.slope_ref), custom_call_target="tpu_custom_call" | custom-call | tf_op jit(solution)/shard_map/normalized_forward/pallas_call | solution.py:90
  125.1 0.8 broadcast_in_dim.38
  125.9 12.4 %all_to_all.79 = bf16[8,64,256]{2,1,0:T(8,128)(2,1)S(1)} all-to-all(bf16[8,64,256]{2,1,0:T(8,128)(2,1)S(1)} %broadcast_in_dim.38), channel_id=1, replica_groups=mesh['y'=4,'z'=8,'x'=4,'core'=2] {'z'}, dimensions={0} | all-to-all | bytes 524288 | tf_op jit(solution)/shard_map/all_to_all | solution.py:23
  138.3 0.4 convolution_convert_fusion.6
  138.7 7.5 %all_to_all.80 = bf16[4,64,256]{2,1,0:T(8,128)(2,1)S(1)} all-to-all(bf16[4,64,256]{2,1,0:T(8,128)(2,1)S(1)} %broadcast_in_dim.39), channel_id=1, replica_groups=mesh['y'=4,'z'=8,'x'=4,'core'=2] {'y'}, dimensions={0} | all-to-all | bytes 262144 | tf_op jit(solution)/shard_map/all_to_all | solution.py:23
  146.3 0.3 convolution_convert_fusion
  146.6 11.7 %all_to_all.81 = bf16[8,64,256]{2,1,0:T(8,128)(2,1)S(1)} all-to-all(bf16[8,64,256]{2,1,0:T(8,128)(2,1)S(1)} %bitcast.77), channel_id=1, replica_groups=mesh['y'=4,'z'=8,'x'=4,'core'=2] {'z'}, dimensions={0} | all-to-all | bytes 524288 | tf_op jit(solution)/shard_map/all_to_all | solution.py:23
  158.4 7.2 %all_to_all.82 = bf16[4,64,256]{2,1,0:T(8,128)(2,1)S(1)} all-to-all(bf16[4,64,256]{2,1,0:T(8,128)(2,1)S(1)} %broadcast_in_dim.40), channel_id=1, replica_groups=mesh['y'=4,'z'=8,'x'=4,'core'=2] {'x'}, dimensions={0} | all-to-all | bytes 262144 | tf_op jit(solution)/shard_map/all_to_all | solution.py:23
  165.6 0.2 convolution_convert_fusion.3
  165.8 0.2 convolution_convert_fusion.2
  166.1 12.6 %all_to_all.83 = bf16[32,8,512]{2,1,0:T(8,128)(2,1)S(1)} all-to-all(bf16[32,8,512]{2,1,0:T(8,128)(2,1)S(1)} %bitcast.75), channel_id=1, replica_groups=mesh['y'=4,'z'=8,'x'=4,'core'=2] {'y','z'}, dimensions={0} | all-to-all | bytes 524288 | tf_op jit(solution)/shard_map/all_to_all | solution.py:23
  178.7 0.1 reduce_sum.107
  178.8 15.5 %all_to_all.84 = bf16[32,8,512]{2,1,0:T(8,128)(2,1)S(1)} all-to-all(bf16[32,8,512]{2,1,0:T(8,128)(2,1)S(1)} %broadcast_in_dim.41), channel_id=1, replica_groups=mesh['y'=4,'z'=8,'x'=4,'core'=2] {'y','z'}, dimensions={0} | all-to-all | bytes 524288 | tf_op jit(solution)/shard_map/all_to_all | solution.py:23
  194.3 0.2 fusion.16
  194.5 0.2 reduce-precision_convert_fusion
  194.7 0.1 pad_maximum_fusion.3
  194.7 0.6 broadcast_in_dim.42
  195.4 3.3 %all-to-all-start.14 = ((bf16[4,64,128]{2,1,0:T(8,128)(2,1)}), bf16[4,64,128]{2,1,0:T(8,128)(2,1)S(1)}, u32[]{:S(2)}, u32[]{:S(2)}) async-start(bf16[4,64,128]{2,1,0:T(8,128)(2,1)} %broadcast_in_dim.42), calls=%async_computation.14 | async-start | bytes 131072 | tf_op jit(solution)/shard_map/all_to_all | solution.py:23
  198.7 0.7 fusion.18
  199.4 3.8 %all-to-all-done.14.arrived_ref = bf16[4,64,128]{2,1,0:T(8,128)(2,1)S(1)} async-done(((bf16[4,64,128]{2,1,0:T(8,128)(2,1)}), bf16[4,64,128]{2,1,0:T(8,128)(2,1)S(1)}, u32[]{:S(2)}, u32[]{:S(2)}) %all-to-all-start.14) | async-done | bytes 65568 | tf_op jit(solution)/shard_map/all_to_all | solution.py:23
  203.2 0.6 copy-done.2
  203.8 4.3 %normalized_panel.1 = (f32[64,1024]{1,0:T(8,128)}, f32[64,1024]{1,0:T(8,128)}) custom-call(bf16[4,64,128]{2,1,0:T(8,128)(2,1)} %copy-done.2, bf16[64,1024]{1,0:T(8,128)(2,1)} %get-tuple-element.20.own_ref, bf16[64,1024]{1,0:T(8,128)(2,1)} %get-tuple-element.19.other_ref), custom_call_target="tpu_custom_call" | custom-call | tf_op jit(solution)/shard_map/normalized_panel/pallas_call | solution.py:104
  208.0 15.9 %collective-permute-start.7 = (f32[64,1024]{1,0:T(8,128)}, f32[64,1024]{1,0:T(8,128)S(1)}, u32[]{:S(2)}, u32[]{:S(2)}) collective-permute-start(f32[64,1024]{1,0:T(8,128)} %get-tuple-element.12), channel_id=1, source_target_pairs={{0,1},{1,0},{2,3},{3,2},{4,5},{5,4},{6,7},{7,6},{8,9},{9,8},{10,11... | collective-permute-start | bytes 786440 | tf_op jit(solution)/shard_map/ppermute | solution.py:174
  223.9 1.4 collective-permute-done.7
  225.3 1.9 broadcast_select_fusion
  (41 shorter events, 0.6 us)
Async XLA Ops:
  0.0 1.0 copy-start
  0.0 5.6 %copy-start.1 = (bf16[2,256,1024]{2,1,0:T(8,128)(2,1)S(1)}, bf16[2,256,1024]{2,1,0:T(8,128)(2,1)}, u32[]{:S(2)}) copy-start(bf16[2,256,1024]{2,1,0:T(8,128)(2,1)} %param.3) | copy-start | bytes 3145732
  1.0 5.4 %copy-start.5 = (f32[2,2,256]{2,1,0:T(2,128)S(1)}, f32[2,2,256]{2,1,0:T(2,128)}, u32[]{:S(2)}) copy-start(f32[2,2,256]{2,1,0:T(2,128)} %param.4) | copy-start | bytes 12292
  2.3 4.2 %collective-permute-start.1 = (f32[64,256]{1,0:T(8,128)S(1)}, f32[64,256]{1,0:T(8,128)S(1)}, u32[]{:S(2)}, u32[]{:S(2)}) collective-permute-start(f32[64,256]{1,0:T(8,128)S(1)} %select_bitcast_fusion), channel_id=1, source_target_pairs={{0,1},{1,0},{2,3},{3,2},{4,5},{5,4},{6,7},{7,6},{8,9},{9,8},{10,11... | collective-permute-start | bytes 196616 | tf_op jit(solution)/shard_map/ppermute | solution.py:126
  5.7 19.1 %collective-permute-start.2 = (bf16[128,1024]{1,0:T(8,128)(2,1)S(1)}, bf16[128,1024]{1,0:T(8,128)(2,1)S(1)}, u32[]{:S(2)}, u32[]{:S(2)}) collective-permute-start(bf16[128,1024]{1,0:T(8,128)(2,1)S(1)} %get-tuple-element.13), channel_id=1, source_target_pairs={{0,0},{2,64},{4,128},{6,192},{64,2},{66,66},{68,130},{70,194},{128... | collective-permute-start | bytes 786440 | tf_op jit(solution)/shard_map/ppermute | solution.py:133
  7.2 16.9 %all-to-all-start = ((bf16[4,64,256]{2,1,0:T(8,128)(2,1)}), bf16[4,64,256]{2,1,0:T(8,128)(2,1)S(1)}, u32[]{:S(2)}, u32[]{:S(2)}) async-start(bf16[4,64,256]{2,1,0:T(8,128)(2,1)} %broadcast_in_dim.32), calls=%async_computation | async-start | bytes 262144 | tf_op jit(solution)/shard_map/all_to_all | solution.py:23
  24.1 10.9 %collective-permute-start.4 = (bf16[128,1024]{1,0:T(8,128)(2,1)S(1)}, bf16[128,1024]{1,0:T(8,128)(2,1)S(1)}, u32[]{:S(2)}, u32[]{:S(2)}) collective-permute-start(bf16[128,1024]{1,0:T(8,128)(2,1)S(1)} %get-tuple-element.10), channel_id=1, source_target_pairs={{0,0},{2,64},{4,128},{6,192},{64,2},{66,66},{68,130},{70,194},{128... | collective-permute-start | bytes 786440 | tf_op jit(solution)/shard_map/ppermute | solution.py:133
  24.8 10.5 %collective-permute-start.3 = (bf16[128,1024]{1,0:T(8,128)(2,1)S(1)}, bf16[128,1024]{1,0:T(8,128)(2,1)S(1)}, u32[]{:S(2)}, u32[]{:S(2)}) collective-permute-start(bf16[128,1024]{1,0:T(8,128)(2,1)S(1)} %collective-permute-done.2), channel_id=1, source_target_pairs={{0,1},{1,0},{2,3},{3,2},{4,5},{5,4},{6,7},{7,6},{8,9},{9,8},{10,11... | collective-permute-start | bytes 786440 | tf_op jit(solution)/shard_map/ppermute | solution.py:134
  26.8 20.6 %all-to-all-start.1 = ((bf16[8,64,256]{2,1,0:T(8,128)(2,1)}), bf16[8,64,256]{2,1,0:T(8,128)(2,1)S(1)}, u32[]{:S(2)}, u32[]{:S(2)}) async-start(bf16[8,64,256]{2,1,0:T(8,128)(2,1)} %broadcast_in_dim.33), calls=%async_computation.1 | async-start | bytes 524288 | tf_op jit(solution)/shard_map/all_to_all | solution.py:23
  35.0 12.4 %collective-permute-start.5 = (bf16[128,1024]{1,0:T(8,128)(2,1)S(1)}, bf16[128,1024]{1,0:T(8,128)(2,1)S(1)}, u32[]{:S(2)}, u32[]{:S(2)}) collective-permute-start(bf16[128,1024]{1,0:T(8,128)(2,1)S(1)} %collective-permute-done.4), channel_id=1, source_target_pairs={{0,1},{1,0},{2,3},{3,2},{4,5},{5,4},{6,7},{7,6},{8,9},{9,8},{10,11... | collective-permute-start | bytes 786440 | tf_op jit(solution)/shard_map/ppermute | solution.py:134
  47.4 10.5 %copy-start.3 = (bf16[128,1024]{1,0:T(8,128)(2,1)}, bf16[128,1024]{1,0:T(8,128)(2,1)S(1)}, u32[]{:S(2)}) copy-start(bf16[128,1024]{1,0:T(8,128)(2,1)S(1)} %get-tuple-element.18) | copy-start | bytes 786436
  48.6 9.4 %all-to-all-start.2 = ((bf16[4,64,256]{2,1,0:T(8,128)(2,1)}), bf16[4,64,256]{2,1,0:T(8,128)(2,1)S(1)}, u32[]{:S(2)}, u32[]{:S(2)}) async-start(bf16[4,64,256]{2,1,0:T(8,128)(2,1)} %broadcast_in_dim.34), calls=%async_computation.2 | async-start | bytes 262144 | tf_op jit(solution)/shard_map/all_to_all | solution.py:23
  53.1 4.9 %collective-permute-start = (f32[1,256]{1,0:T(1,128)S(1)}, f32[1,256]{1,0:T(1,128)S(1)}, u32[]{:S(2)}, u32[]{:S(2)}) collective-permute-start(f32[1,256]{1,0:T(1,128)S(1)} %get-tuple-element.26), channel_id=1, source_target_pairs={{0,0},{2,64},{4,128},{6,192},{64,2},{66,66},{68,130},{70,194},{128... | collective-permute-start | bytes 3080 | tf_op jit(solution)/shard_map/ppermute | solution.py:130
  59.0 12.6 %all-to-all-start.3 = ((bf16[8,64,256]{2,1,0:T(8,128)(2,1)}), bf16[8,64,256]{2,1,0:T(8,128)(2,1)S(1)}, u32[]{:S(2)}, u32[]{:S(2)}) async-start(bf16[8,64,256]{2,1,0:T(8,128)(2,1)} %bitcast.69), calls=%async_computation.3 | async-start | bytes 524288 | tf_op jit(solution)/shard_map/all_to_all | solution.py:23
  62.5 20.6 %collective-permute-start.6 = (bf16[256,1024]{1,0:T(8,128)(2,1)S(1)}, bf16[256,1024]{1,0:T(8,128)(2,1)S(1)}, u32[]{:S(2)}, u32[]{:S(2)}) collective-permute-start(bf16[256,1024]{1,0:T(8,128)(2,1)S(1)} %slice_bitcast_fusion), channel_id=1, source_target_pairs={{0,1},{1,0},{2,3},{3,2},{4,5},{5,4},{6,7},{7,6},{8,9},{9,8},{10,11... | collective-permute-start | bytes 1572872 | tf_op jit(solution)/shard_map/ppermute | solution.py:139
  113.0 25.3 %copy-start.4 = (bf16[128,1024]{1,0:T(8,128)(2,1)S(1)}, bf16[128,1024]{1,0:T(8,128)(2,1)}, u32[]{:S(2)}) copy-start(bf16[128,1024]{1,0:T(8,128)(2,1)} %copy-done.3) | copy-start | bytes 786436
  195.4 7.8 %all-to-all-start.14 = ((bf16[4,64,128]{2,1,0:T(8,128)(2,1)}), bf16[4,64,128]{2,1,0:T(8,128)(2,1)S(1)}, u32[]{:S(2)}, u32[]{:S(2)}) async-start(bf16[4,64,128]{2,1,0:T(8,128)(2,1)} %broadcast_in_dim.42), calls=%async_computation.14 | async-start | bytes 131072 | tf_op jit(solution)/shard_map/all_to_all | solution.py:23
  203.1 0.6 copy-start.2
  208.0 17.2 %collective-permute-start.7 = (f32[64,1024]{1,0:T(8,128)}, f32[64,1024]{1,0:T(8,128)S(1)}, u32[]{:S(2)}, u32[]{:S(2)}) collective-permute-start(f32[64,1024]{1,0:T(8,128)} %get-tuple-element.12), channel_id=1, source_target_pairs={{0,1},{1,0},{2,3},{3,2},{4,5},{5,4},{6,7},{7,6},{8,9},{9,8},{10,11... | collective-permute-start | bytes 786440 | tf_op jit(solution)/shard_map/ppermute | solution.py:174

commit v3 on v2

--- a/solution.py
+++ b/solution.py
@@ -5,8 +5,10 @@
 from jax.experimental.pallas import tpu as pltpu
 from jax.sharding import Mesh, PartitionSpec as P
 
+
 WIDTH = 8192
 ITERS = 2
+EARLY = 96
 BF16 = jnp.bfloat16
 F32 = jnp.float32
 
@@ -77,31 +79,53 @@
     return summed[:, :rank] + summed[:, rank:]
 
 
-def normalized_forward(arrived, slope, width):
+def inverse_of(arrived, start):
     rank = arrived.shape[1]
 
-    def kernel(arrived_ref, slope_ref, out_ref):
-        inverse = inverse_factor(gram_of_parts(arrived_ref, width, rank))
-        summed = arrived_ref[0, :, :width].astype(F32)
-        for i in range(1, arrived_ref.shape[0]):
-            summed = summed + arrived_ref[i, :, :width].astype(F32)
-        out_ref[...] = (slope_ref[...] * exact_dot(inverse, summed)).astype(BF16)
+    def kernel(arrived_ref, out_ref):
+        out_ref[...] = inverse_factor(gram_of_parts(arrived_ref, start, rank))
 
     return pl.pallas_call(
-        kernel, out_shape=jax.ShapeDtypeStruct((rank, width), BF16), name="normalized_forward"
-    )(arrived, slope)
-
-
-def normalized_panel(arrived, own, other):
-    rank = arrived.shape[1]
-
-    def kernel(arrived_ref, own_ref, other_ref, own_out, other_out):
-        inverse = inverse_factor(gram_of_parts(arrived_ref, 0, rank))
-        own_out[...] = exact_dot(inverse, own_ref[...].astype(F32))
-        other_out[...] = exact_dot(inverse, other_ref[...].astype(F32))
-
-    shape = jax.ShapeDtypeStruct(own.shape, F32)
-    return pl.pallas_call(kernel, out_shape=(shape, shape), name="normalized_panel")(arrived, own, other)
+        kernel,
+        out_shape=jax.ShapeDtypeStruct((rank, rank), F32),
+        cost_estimate=pl.CostEstimate(flops=60_000_000, bytes_accessed=200_000, transcendentals=0),
+        name="inverse_of",
+    )(arrived)
+
+
+def normalized_weighted(arrived, inverse, slope):
+    count, rank, width = arrived.shape
+
+    def kernel(arrived_ref, inverse_ref, slope_ref, out_ref):
+        summed = arrived_ref[0].astype(F32)
+        for i in range(1, count):
+            summed = summed + arrived_ref[i].astype(F32)
+        forward = (slope_ref[...] * exact_dot(inverse_ref[...], summed)).astype(BF16)
+        out_ref[...] = (slope_ref[...] * forward.astype(F32)).astype(BF16)
+
+    return pl.pallas_call(
+        kernel, out_shape=jax.ShapeDtypeStruct((rank, width), BF16), name="normalized_weighted"
+    )(arrived, inverse, slope)
+
+
+def normalized_panels(core, inverse, inverse_there, image, there):
+    rank, width = there.shape
+
+    def kernel(core_ref, inverse_ref, inverse_there_ref, image_ref, there_ref, out_ref):
+        here_at = core_ref[0]
+        here = exact_dot(inverse_ref[...], image_ref[:, :width].astype(F32))
+        out_ref[pl.ds(here_at, 1)] = here[None]
+        away = exact_dot(inverse_there_ref[...], there_ref[...].astype(F32))
+        out_ref[pl.ds(1 - here_at, 1)] = away[None]
+
+    whole = pl.BlockSpec(memory_space=pltpu.VMEM)
+    return pl.pallas_call(
+        kernel,
+        in_specs=[pl.BlockSpec(memory_space=pltpu.SMEM), whole, whole, whole, whole],
+        out_specs=whole,
+        out_shape=jax.ShapeDtypeStruct((2, rank, width), F32),
+        name="normalized_panels",
+    )(core, inverse, inverse_there, image, there)
 
 
 def high_low(gram):
@@ -116,7 +140,7 @@
     def on_device(weights, preact, panel):
         core = lax.axis_index("core")
         first = core == 0
-        inputs, rank, width_in = panel.shape
+        _, rank, width_in = panel.shape
         width_row = weights.shape[1]
         w1_own, w2_own = weights[0], weights[1]
 
@@ -134,26 +158,30 @@
             there = lax.ppermute(here, "core", flip)
             return jnp.concatenate([jnp.where(first, here, there), jnp.where(first, there, here)], axis=1)
 
-        half = width_row // 2
-        w2_top = moved(w2_own[:half])
+        w2 = jnp.concatenate([moved(w2_own[:EARLY]), moved(w2_own[EARLY:])], axis=0)
         w1_other = lax.ppermute(w1_own, "core", flip)
 
-        own = other = None
+        image = inverse = None
         for iteration in range(ITERS):
             if iteration == 0:
-                forward = (slope_1 * total(to_all(summed_out.astype(BF16), "x", n_x))).astype(BF16)
-                forward, w2_rest = lax.optimization_barrier((forward, w2_own[half:]))
-                w2 = jnp.concatenate([w2_top, moved(w2_rest)], axis=0)
+                arrived = to_all(summed_out.astype(BF16), "x", n_x)
             else:
+                own, other = image[:, :width_in], image[:, width_in:]
                 partial_out = dot_t(own, w1_own) + dot_t(other, w1_other)
                 gram = dot_t(own, own) + dot_t(other, other)
                 message = jnp.concatenate([partial_out.astype(BF16), high_low(gram)], axis=1)
-                forward = normalized_forward(to_all(message, "x", n_x), slope_1, width_row)
+                arrived = to_all(message, "x", n_x)
+                inverse = inverse_of(arrived, width_row)
+            forward = (slope_1 * total(arrived[:, :, :width_row])).astype(BF16)
             spread = to_all(forward, "z", n_z)
             spread = jnp.moveaxis(spread, 0, 1).reshape(rank, n_z * width_row)
             partial_out = dot_t(spread, w2)
-            forward = (slope_2 * total(to_all(partial_out.astype(BF16), "y", n_y))).astype(BF16)
-            weighted = (slope_2 * forward.astype(F32)).astype(BF16)
+            arrived = to_all(partial_out.astype(BF16), "y", n_y)
+            if inverse is None:
+                forward = (slope_2 * total(arrived)).astype(BF16)
+                weighted = (slope_2 * forward.astype(F32)).astype(BF16)
+            else:
+                weighted = normalized_weighted(arrived, inverse, slope_2)
             partial_in = dot_n(weighted, w2).astype(BF16)
             blocks = jnp.moveaxis(partial_in.reshape(rank, n_z, width_row), 1, 0)
             summed = total(exchange(blocks, "z")).astype(BF16)
@@ -168,12 +196,11 @@
             piece = total(exchange(pieces, ("y", "z"))).astype(BF16)
             image = to_all(piece, ("y", "z"), groups * cuts).reshape(groups, cuts, 8, length)
             image = jnp.moveaxis(image, 1, 2).reshape(rank, 2 * width_in)
-            own, other = image[:, :width_in], image[:, width_in:]
-        gram = dot_t(own, own) + dot_t(other, other)
-        basis_own, basis_other = normalized_panel(to_all(high_low(gram), "x", n_x), own, other)
-        received = lax.ppermute(basis_other, "core", flip)
-        at = lax.broadcasted_iota(jnp.int32, (inputs, rank, width_in), 0)
-        return jnp.where(at == core, basis_own[None], received[None])
+        there = lax.ppermute(image[:, width_in:], "core", flip)
+        gram = dot_t(image, image)
+        inverse = inverse_of(to_all(high_low(gram), "x", n_x), 0)
+        inverse_there = lax.ppermute(inverse, "core", flip)
+        return normalized_panels(core.reshape(1).astype(jnp.int32), inverse, inverse_there, image, there)
 
     return on_device
 
@@ -181,8 +208,10 @@
 def solution(mesh):
     n_x, n_y, n_z = 4, 4, 8
     fine = Mesh(mesh.devices.reshape(n_y, n_z, n_x, 2), ("y", "z", "x", "core"))
+    on_device = make(n_x, n_y, n_z)
+
     return jax.shard_map(
-        make(n_x, n_y, n_z),
+        on_device,
         mesh=fine,
         in_specs=(P(None, ("y", "z"), ("x", "core")), P(None, None, ("y", "z")), P(None, None, ("x", "core"))),
         out_specs=P(None, None, ("x", "core")),

time: 228 us -> 235 us (1.031)
  starting transfers between devices: 50.5 us -> 59.3 us
  Pallas kernels: 8.01 us -> 11.2 us
  blocking collectives: 115 us -> 112 us
    ppermute x1 -> x2, starting transfers between devices: 15.9 us -> 20 us  [the longest x1 18.9 us: on_device(): there = lax.ppermute(image[:, width_in:], 'core', flip)]
    pallas_call x2 -> x4, Pallas kernels: 8.01 us -> 11.2 us  [the longest x2 7.04 us: inverse_of(): pl.pallas_call(kernel, out_shape=jax.ShapeDtypeStruct((rank, rank), F32),...]
    all_to_all x10, blocking collectives: 115 us -> 112 us  [exchange(): return lax.all_to_all(tiles, axis, split_axis=0, concat_axis=0, tiled=True)]
    all_to_all x5, starting transfers between devices: 25.7 us -> 28.4 us  [exchange(): return lax.all_to_all(tiles, axis, split_axis=0, concat_axis=0, tiled=True)]
  transfers between devices with their start and end apart: 13 -> 14, of which waited for: 7 -> 7; matrix products, arithmetic and copies ran while one was open for 1% -> 1% of each run, Pallas kernels for 0% -> 3%
where the time goes in v3:
time: 235 us; the launch traced here: 234 us
  blocking collectives  112 us (48%)
  starting transfers between devices  59.3 us (25%)
  waiting for transfers between devices  37 us (16%)
  Pallas kernels  11.2 us (5%)
  local copies, waits for them, and re-layouts  7.01 us (3%)
  matrix products  5.58 us (2%)
    all_to_all x10, blocking collectives, exchange(): return lax.all_to_all(tiles, axis, split_axis=0, concat_axis=0, tiled=True)  112 us
    all_to_all x5, waiting for transfers between devices, exchange(): return lax.all_to_all(tiles, axis, split_axis=0, concat_axis=0, tiled=True)  35 us
    all_to_all x5, starting transfers between devices, exchange(): return lax.all_to_all(tiles, axis, split_axis=0, concat_axis=0, tiled=True)  28.4 us
    ppermute x1, starting transfers between devices, on_device(): there = lax.ppermute(image[:, width_in:], 'core', flip)  18.9 us
    pallas_call x2, Pallas kernels, inverse_of(): pl.pallas_call(kernel, out_shape=jax.ShapeDtypeStruct((rank, rank), F32),...  7.04 us
  transfers between devices with their start and end apart: 14, of which 7 were waited for; matrix products, arithmetic and copies ran while one was open for 1% of the time, Pallas kernels for 3%

profile of v3, /device:TPU:1, one launch (start us, length us, event | category | flops | bytes accessed | tf_op | source)
XLA Modules:
  0.0 233.7 jit_solution(18108492020627959811)
XLA Ops:
  0.0 0.9 copy-done
  1.0 1.4 fusion.1
  2.3 3.3 %collective-permute-start.1 = (f32[64,256]{1,0:T(8,128)S(1)}, f32[64,256]{1,0:T(8,128)S(1)}, u32[]{:S(2)}, u32[]{:S(2)}) collective-permute-start(f32[64,256]{1,0:T(8,128)S(1)} %select_bitcast_fusion), channel_id=1, source_target_pairs={{0,1},{1,0},{2,3},{3,2},{4,5},{5,4},{6,7},{7,6},{8,9},{9,8},{10,11... | collective-permute-start | bytes 196616 | tf_op jit(solution)/shard_map/ppermute | solution.py:150
  5.7 0.7 collective-permute-start.2
  6.4 0.7 collective-permute-start.4
  7.1 0.7 broadcast_in_dim.22
  7.8 10.1 %all-to-all-start = ((bf16[4,64,256]{2,1,0:T(8,128)(2,1)}), bf16[4,64,256]{2,1,0:T(8,128)(2,1)S(1)}, u32[]{:S(2)}, u32[]{:S(2)}) async-start(bf16[4,64,256]{2,1,0:T(8,128)(2,1)} %broadcast_in_dim.22), calls=%async_computation | async-start | bytes 262144 | tf_op jit(solution)/shard_map/all_to_all | solution.py:25
  17.9 17.4 %all-to-all-done = bf16[4,64,256]{2,1,0:T(8,128)(2,1)S(1)} async-done(((bf16[4,64,256]{2,1,0:T(8,128)(2,1)}), bf16[4,64,256]{2,1,0:T(8,128)(2,1)S(1)}, u32[]{:S(2)}, u32[]{:S(2)}) %all-to-all-start) | async-done | bytes 131104 | tf_op jit(solution)/shard_map/all_to_all | solution.py:25
  35.3 0.7 broadcast_in_dim.23
  36.1 8.2 %all-to-all-start.1 = ((bf16[8,64,256]{2,1,0:T(8,128)(2,1)}), bf16[8,64,256]{2,1,0:T(8,128)(2,1)S(1)}, u32[]{:S(2)}, u32[]{:S(2)}) async-start(bf16[8,64,256]{2,1,0:T(8,128)(2,1)} %broadcast_in_dim.23), calls=%async_computation.1 | async-start | bytes 524288 | tf_op jit(solution)/shard_map/all_to_all | solution.py:25
  44.3 1.5 collective-permute-start.3
  45.8 0.1 collective-permute-start.5
  45.9 1.0 collective-permute-done.3
  46.9 0.7 broadcast_select_fusion.3
  47.6 6.8 %all-to-all-done.1 = bf16[8,64,256]{2,1,0:T(8,128)(2,1)S(1)} async-done(((bf16[8,64,256]{2,1,0:T(8,128)(2,1)}), bf16[8,64,256]{2,1,0:T(8,128)(2,1)S(1)}, u32[]{:S(2)}, u32[]{:S(2)}) %all-to-all-start.1) | async-done | bytes 262176 | tf_op jit(solution)/shard_map/all_to_all | solution.py:25
  54.5 0.8 copy-done.5
  55.3 0.4 convolution_convert_fusion.7
  55.8 0.7 broadcast_in_dim.24
  56.5 3.3 %all-to-all-start.2 = ((bf16[4,64,256]{2,1,0:T(8,128)(2,1)}), bf16[4,64,256]{2,1,0:T(8,128)(2,1)S(1)}, u32[]{:S(2)}, u32[]{:S(2)}) async-start(bf16[4,64,256]{2,1,0:T(8,128)(2,1)} %broadcast_in_dim.24), calls=%async_computation.2 | async-start | bytes 262144 | tf_op jit(solution)/shard_map/all_to_all | solution.py:25
  59.8 0.7 collective-permute-start
  60.5 4.1 %all-to-all-done.2 = bf16[4,64,256]{2,1,0:T(8,128)(2,1)S(1)} async-done(((bf16[4,64,256]{2,1,0:T(8,128)(2,1)}), bf16[4,64,256]{2,1,0:T(8,128)(2,1)S(1)}, u32[]{:S(2)}, u32[]{:S(2)}) %all-to-all-start.2) | async-done | bytes 131104 | tf_op jit(solution)/shard_map/all_to_all | solution.py:25
  64.6 0.3 convolution_convert_fusion.1
  64.9 0.2 copy-done.11
  65.2 0.7 copy.19
  65.9 3.4 %all-to-all-start.3 = ((bf16[8,64,256]{2,1,0:T(8,128)(2,1)}), bf16[8,64,256]{2,1,0:T(8,128)(2,1)S(1)}, u32[]{:S(2)}, u32[]{:S(2)}) async-start(bf16[8,64,256]{2,1,0:T(8,128)(2,1)} %bitcast.71), calls=%async_computation.3 | async-start | bytes 524288 | tf_op jit(solution)/shard_map/all_to_all | solution.py:25
  69.3 3.9 %collective-permute-start.6 = (bf16[256,1024]{1,0:T(8,128)(2,1)S(1)}, bf16[256,1024]{1,0:T(8,128)(2,1)S(1)}, u32[]{:S(2)}, u32[]{:S(2)}) collective-permute-start(bf16[256,1024]{1,0:T(8,128)(2,1)S(1)} %slice_bitcast_fusion), channel_id=1, source_target_pairs={{0,1},{1,0},{2,3},{3,2},{4,5},{5,4},{6,7},{7,6},{8,9},{9,8},{10,11... | collective-permute-start | bytes 1572872 | tf_op jit(solution)/shard_map/ppermute | solution.py:162
  73.2 5.4 %all-to-all-done.3 = bf16[8,64,256]{2,1,0:T(8,128)(2,1)S(1)} async-done(((bf16[8,64,256]{2,1,0:T(8,128)(2,1)}), bf16[8,64,256]{2,1,0:T(8,128)(2,1)S(1)}, u32[]{:S(2)}, u32[]{:S(2)}) %all-to-all-start.3) | async-done | bytes 262176 | tf_op jit(solution)/shard_map/all_to_all | solution.py:25
  78.7 9.5 %all_to_all.75 = bf16[4,64,256]{2,1,0:T(8,128)(2,1)S(1)} all-to-all(bf16[4,64,256]{2,1,0:T(8,128)(2,1)S(1)} %broadcast_in_dim.25), channel_id=1, replica_groups=mesh['y'=4,'z'=8,'x'=4,'core'=2] {'x'}, dimensions={0} | all-to-all | bytes 262144 | tf_op jit(solution)/shard_map/all_to_all | solution.py:25
  88.3 0.2 convolution_convert_fusion.5
  88.5 0.2 convolution_convert_fusion.4
  88.8 15.3 %all_to_all.76 = bf16[32,8,512]{2,1,0:T(8,128)(2,1)S(1)} all-to-all(bf16[32,8,512]{2,1,0:T(8,128)(2,1)S(1)} %bitcast.76), channel_id=1, replica_groups=mesh['y'=4,'z'=8,'x'=4,'core'=2] {'y','z'}, dimensions={0} | all-to-all | bytes 524288 | tf_op jit(solution)/shard_map/all_to_all | solution.py:25
  104.0 0.1 reduce_sum.103
  104.1 13.8 %all_to_all.77 = bf16[32,8,512]{2,1,0:T(8,128)(2,1)S(1)} all-to-all(bf16[32,8,512]{2,1,0:T(8,128)(2,1)S(1)} %broadcast_in_dim.26), channel_id=1, replica_groups=mesh['y'=4,'z'=8,'x'=4,'core'=2] {'y','z'}, dimensions={0} | all-to-all | bytes 524288 | tf_op jit(solution)/shard_map/all_to_all | solution.py:25
  117.9 0.2 fusion.6
  118.1 0.3 fusion.8
  118.4 0.2 reduce-precision_convert_fusion.1
  118.6 0.3 fusion
  118.9 0.1 pad_maximum_fusion.2
  119.0 7.7 %all_to_all.78.arrived_ref = bf16[4,64,384]{2,1,0:T(8,128)(2,1)S(1)} all-to-all(bf16[4,64,384]{2,1,0:T(8,128)(2,1)S(1)} %broadcast_in_dim.27), channel_id=1, replica_groups=mesh['y'=4,'z'=8,'x'=4,'core'=2] {'x'}, dimensions={0} | all-to-all | bytes 393216 | tf_op jit(solution)/shard_map/all_to_all | solution.py:25
  126.7 12.4 %all_to_all.79 = bf16[8,64,256]{2,1,0:T(8,128)(2,1)S(1)} all-to-all(bf16[8,64,256]{2,1,0:T(8,128)(2,1)S(1)} %broadcast_in_dim.28), channel_id=1, replica_groups=mesh['y'=4,'z'=8,'x'=4,'core'=2] {'z'}, dimensions={0} | all-to-all | bytes 524288 | tf_op jit(solution)/shard_map/all_to_all | solution.py:25
  139.1 0.4 convolution_convert_fusion.6
  139.6 0.7 broadcast_in_dim.29
  140.2 3.3 %all-to-all-start.9 = ((bf16[4,64,256]{2,1,0:T(8,128)(2,1)}), bf16[4,64,256]{2,1,0:T(8,128)(2,1)S(1)}, u32[]{:S(2)}, u32[]{:S(2)}) async-start(bf16[4,64,256]{2,1,0:T(8,128)(2,1)} %broadcast_in_dim.29), calls=%async_computation.9 | async-start | bytes 262144 | tf_op jit(solution)/shard_map/all_to_all | solution.py:25
  143.6 3.6 %inverse_of.2.inverse_ref = f32[64,64]{1,0:T(8,128)} custom-call(bf16[4,64,384]{2,1,0:T(8,128)(2,1)} %copy-done.3), custom_call_target="tpu_custom_call" | custom-call | flops 60000000 | bytes 200000 | tf_op jit(solution)/shard_map/inverse_of/pallas_call | solution.py:88
  147.1 1.2 all-to-all-done.9.arrived_ref
  148.4 0.7 copy-done.4
  149.0 1.7 normalized_weighted.1
  150.8 1.1 convolution_convert_fusion
  151.8 11.7 %all_to_all.80 = bf16[8,64,256]{2,1,0:T(8,128)(2,1)S(1)} all-to-all(bf16[8,64,256]{2,1,0:T(8,128)(2,1)S(1)} %bitcast.79), channel_id=1, replica_groups=mesh['y'=4,'z'=8,'x'=4,'core'=2] {'z'}, dimensions={0} | all-to-all | bytes 524288 | tf_op jit(solution)/shard_map/all_to_all | solution.py:25
  163.6 7.2 %all_to_all.81 = bf16[4,64,256]{2,1,0:T(8,128)(2,1)S(1)} all-to-all(bf16[4,64,256]{2,1,0:T(8,128)(2,1)S(1)} %broadcast_in_dim.30), channel_id=1, replica_groups=mesh['y'=4,'z'=8,'x'=4,'core'=2] {'x'}, dimensions={0} | all-to-all | bytes 262144 | tf_op jit(solution)/shard_map/all_to_all | solution.py:25
  170.9 0.2 convolution_convert_fusion.3
  171.1 0.2 convolution_convert_fusion.2
  171.3 12.9 %all_to_all.82 = bf16[32,8,512]{2,1,0:T(8,128)(2,1)S(1)} all-to-all(bf16[32,8,512]{2,1,0:T(8,128)(2,1)S(1)} %bitcast.77), channel_id=1, replica_groups=mesh['y'=4,'z'=8,'x'=4,'core'=2] {'y','z'}, dimensions={0} | all-to-all | bytes 524288 | tf_op jit(solution)/shard_map/all_to_all | solution.py:25
  184.3 0.1 reduce_sum.107
  184.3 13.8 %all_to_all.83 = bf16[32,8,512]{2,1,0:T(8,128)(2,1)S(1)} all-to-all(bf16[32,8,512]{2,1,0:T(8,128)(2,1)S(1)} %broadcast_in_dim.31), channel_id=1, replica_groups=mesh['y'=4,'z'=8,'x'=4,'core'=2] {'y','z'}, dimensions={0} | all-to-all | bytes 524288 | tf_op jit(solution)/shard_map/all_to_all | solution.py:25
  198.2 0.2 reduce-precision_convert_fusion
  198.4 18.9 %collective-permute-start.8 = (bf16[64,1024]{1,0:T(8,128)(2,1)S(1)}, bf16[64,1024]{1,0:T(8,128)(2,1)S(1)}, u32[]{:S(2)}, u32[]{:S(2)}) collective-permute-start(bf16[64,1024]{1,0:T(8,128)(2,1)S(1)} %slice.77), channel_id=1, source_target_pairs={{0,1},{1,0},{2,3},{3,2},{4,5},{5,4},{6,7},{7,6},{8,9},{9,8},{10,11... | collective-permute-start | bytes 393224 | tf_op jit(solution)/shard_map/ppermute | solution.py:199
  217.3 0.1 pad_maximum_fusion.3
  217.4 7.5 %all_to_all.84.arrived_ref = bf16[4,64,128]{2,1,0:T(8,128)(2,1)} all-to-all(bf16[4,64,128]{2,1,0:T(8,128)(2,1)S(1)} %broadcast_in_dim.32), channel_id=1, replica_groups=mesh['y'=4,'z'=8,'x'=4,'core'=2] {'x'}, dimensions={0} | all-to-all | bytes 131072 | tf_op jit(solution)/shard_map/all_to_all | solution.py:25
  225.0 3.5 %inverse_of.3.inverse_ref = f32[64,64]{1,0:T(8,128)} custom-call(bf16[4,64,128]{2,1,0:T(8,128)(2,1)} %all_to_all.84.arrived_ref), custom_call_target="tpu_custom_call" | custom-call | flops 60000000 | bytes 200000 | tf_op jit(solution)/shard_map/inverse_of/pallas_call | solution.py:88
  228.4 1.1 collective-permute-start.7
  229.6 1.1 collective-permute-done.7.inverse_there_ref
  230.7 0.6 copy-done.9
  231.3 2.4 %normalized_panels.1 = f32[2,64,1024]{2,1,0:T(8,128)} custom-call(s32[1]{0:T(128)} %bitcast.core_ref, f32[64,64]{1,0:T(8,128)} %inverse_of.3.inverse_ref, f32[64,64]{1,0:T(8,128)} %copy-done.9, bf16[64,2048]{1,0:T(8,128)(2,1)} %bitcast.74, bf16[64,1024]{1,0:T(8,128)(2,1)} %copy-done.8), custom_call_target="tpu_custom_call" | custom-call | tf_op jit(solution)/shard_map/normalized_panels/pallas_call | solution.py:122
  (56 shorter events, 0.7 us)
Async XLA Ops:
  0.0 1.0 copy-start
  0.0 5.6 %copy-start.1 = (bf16[2,256,1024]{2,1,0:T(8,128)(2,1)S(1)}, bf16[2,256,1024]{2,1,0:T(8,128)(2,1)}, u32[]{:S(2)}) copy-start(bf16[2,256,1024]{2,1,0:T(8,128)(2,1)} %param.3) | copy-start | bytes 3145732
  1.0 6.1 %copy-start.10 = (f32[2,2,256]{2,1,0:T(2,128)S(1)}, f32[2,2,256]{2,1,0:T(2,128)}, u32[]{:S(2)}) copy-start(f32[2,2,256]{2,1,0:T(2,128)} %param.4) | copy-start | bytes 12292
  2.3 4.7 %collective-permute-start.1 = (f32[64,256]{1,0:T(8,128)S(1)}, f32[64,256]{1,0:T(8,128)S(1)}, u32[]{:S(2)}, u32[]{:S(2)}) collective-permute-start(f32[64,256]{1,0:T(8,128)S(1)} %select_bitcast_fusion), channel_id=1, source_target_pairs={{0,1},{1,0},{2,3},{3,2},{4,5},{5,4},{6,7},{7,6},{8,9},{9,8},{10,11... | collective-permute-start | bytes 196616 | tf_op jit(solution)/shard_map/ppermute | solution.py:150
  5.7 38.6 %collective-permute-start.2 = (bf16[96,1024]{1,0:T(8,128)(2,1)S(1)}, bf16[96,1024]{1,0:T(8,128)(2,1)S(1)}, u32[]{:S(2)}, u32[]{:S(2)}) collective-permute-start(bf16[96,1024]{1,0:T(8,128)(2,1)S(1)} %slice_bitcast_fusion.2), channel_id=1, source_target_pairs={{0,0},{2,64},{4,128},{6,192},{64,2},{66,66},{68,130},{70,194},{128... | collective-permute-start | bytes 589832 | tf_op jit(solution)/shard_map/ppermute | solution.py:157
  6.4 39.4 %collective-permute-start.4 = (bf16[160,1024]{1,0:T(8,128)(2,1)S(1)}, bf16[160,1024]{1,0:T(8,128)(2,1)S(1)}, u32[]{:S(2)}, u32[]{:S(2)}) collective-permute-start(bf16[160,1024]{1,0:T(8,128)(2,1)S(1)} %slice_bitcast_fusion.1), channel_id=1, source_target_pairs={{0,0},{2,64},{4,128},{6,192},{64,2},{66,66},{68,130},{70,194},{128... | collective-permute-start | bytes 983048 | tf_op jit(solution)/shard_map/ppermute | solution.py:157
  7.8 27.5 %all-to-all-start = ((bf16[4,64,256]{2,1,0:T(8,128)(2,1)}), bf16[4,64,256]{2,1,0:T(8,128)(2,1)S(1)}, u32[]{:S(2)}, u32[]{:S(2)}) async-start(bf16[4,64,256]{2,1,0:T(8,128)(2,1)} %broadcast_in_dim.22), calls=%async_computation | async-start | bytes 262144 | tf_op jit(solution)/shard_map/all_to_all | solution.py:25
  36.1 18.3 %all-to-all-start.1 = ((bf16[8,64,256]{2,1,0:T(8,128)(2,1)}), bf16[8,64,256]{2,1,0:T(8,128)(2,1)S(1)}, u32[]{:S(2)}, u32[]{:S(2)}) async-start(bf16[8,64,256]{2,1,0:T(8,128)(2,1)} %broadcast_in_dim.23), calls=%async_computation.1 | async-start | bytes 524288 | tf_op jit(solution)/shard_map/all_to_all | solution.py:25
  44.3 2.6 %collective-permute-start.3 = (bf16[96,1024]{1,0:T(8,128)(2,1)S(1)}, bf16[96,1024]{1,0:T(8,128)(2,1)S(1)}, u32[]{:S(2)}, u32[]{:S(2)}) collective-permute-start(bf16[96,1024]{1,0:T(8,128)(2,1)S(1)} %collective-permute-done.2), channel_id=1, source_target_pairs={{0,1},{1,0},{2,3},{3,2},{4,5},{5,4},{6,7},{7,6},{8,9},{9,8},{10,11... | collective-permute-start | bytes 589832 | tf_op jit(solution)/shard_map/ppermute | solution.py:158
  45.8 8.6 %collective-permute-start.5 = (bf16[160,1024]{1,0:T(8,128)(2,1)S(1)}, bf16[160,1024]{1,0:T(8,128)(2,1)S(1)}, u32[]{:S(2)}, u32[]{:S(2)}) collective-permute-start(bf16[160,1024]{1,0:T(8,128)(2,1)S(1)} %collective-permute-done.4), channel_id=1, source_target_pairs={{0,1},{1,0},{2,3},{3,2},{4,5},{5,4},{6,7},{7,6},{8,9},{9,8},{10,11... | collective-permute-start | bytes 983048 | tf_op jit(solution)/shard_map/ppermute | solution.py:158
  54.4 0.9 copy-start.5
  55.3 9.3 %copy-start.6 = (bf16[96,1024]{1,0:T(8,128)(2,1)S(1)}, bf16[96,1024]{1,0:T(8,128)(2,1)}, u32[]{:S(2)}) copy-start(bf16[96,1024]{1,0:T(8,128)(2,1)} %get-tuple-element.8) | copy-start | bytes 589828
  56.5 8.1 %all-to-all-start.2 = ((bf16[4,64,256]{2,1,0:T(8,128)(2,1)}), bf16[4,64,256]{2,1,0:T(8,128)(2,1)S(1)}, u32[]{:S(2)}, u32[]{:S(2)}) async-start(bf16[4,64,256]{2,1,0:T(8,128)(2,1)} %broadcast_in_dim.24), calls=%async_computation.2 | async-start | bytes 262144 | tf_op jit(solution)/shard_map/all_to_all | solution.py:25
  59.8 4.8 %collective-permute-start = (f32[1,256]{1,0:T(1,128)S(1)}, f32[1,256]{1,0:T(1,128)S(1)}, u32[]{:S(2)}, u32[]{:S(2)}) collective-permute-start(f32[1,256]{1,0:T(1,128)S(1)} %get-tuple-element.13), channel_id=1, source_target_pairs={{0,0},{2,64},{4,128},{6,192},{64,2},{66,66},{68,130},{70,194},{128... | collective-permute-start | bytes 3080 | tf_op jit(solution)/shard_map/ppermute | solution.py:154
  64.6 0.5 copy-start.11
  65.9 12.8 %all-to-all-start.3 = ((bf16[8,64,256]{2,1,0:T(8,128)(2,1)}), bf16[8,64,256]{2,1,0:T(8,128)(2,1)S(1)}, u32[]{:S(2)}, u32[]{:S(2)}) async-start(bf16[8,64,256]{2,1,0:T(8,128)(2,1)} %bitcast.71), calls=%async_computation.3 | async-start | bytes 524288 | tf_op jit(solution)/shard_map/all_to_all | solution.py:25
  69.3 19.2 %collective-permute-start.6 = (bf16[256,1024]{1,0:T(8,128)(2,1)S(1)}, bf16[256,1024]{1,0:T(8,128)(2,1)S(1)}, u32[]{:S(2)}, u32[]{:S(2)}) collective-permute-start(bf16[256,1024]{1,0:T(8,128)(2,1)S(1)} %slice_bitcast_fusion), channel_id=1, source_target_pairs={{0,1},{1,0},{2,3},{3,2},{4,5},{5,4},{6,7},{7,6},{8,9},{9,8},{10,11... | collective-permute-start | bytes 1572872 | tf_op jit(solution)/shard_map/ppermute | solution.py:162
  119.0 20.1 %copy-start.7 = (bf16[96,1024]{1,0:T(8,128)(2,1)S(1)}, bf16[96,1024]{1,0:T(8,128)(2,1)}, u32[]{:S(2)}) copy-start(bf16[96,1024]{1,0:T(8,128)(2,1)} %get-tuple-element.8) | copy-start | bytes 589828
  126.7 12.9 %copy-start.3 = (bf16[4,64,384]{2,1,0:T(8,128)(2,1)}, bf16[4,64,384]{2,1,0:T(8,128)(2,1)S(1)}, u32[]{:S(2)}) copy-start(bf16[4,64,384]{2,1,0:T(8,128)(2,1)S(1)} %all_to_all.78.arrived_ref) | copy-start | bytes 589828
  140.2 8.1 %all-to-all-start.9 = ((bf16[4,64,256]{2,1,0:T(8,128)(2,1)}), bf16[4,64,256]{2,1,0:T(8,128)(2,1)S(1)}, u32[]{:S(2)}, u32[]{:S(2)}) async-start(bf16[4,64,256]{2,1,0:T(8,128)(2,1)} %broadcast_in_dim.29), calls=%async_computation.9 | async-start | bytes 262144 | tf_op jit(solution)/shard_map/all_to_all | solution.py:25
  148.3 0.7 copy-start.4
  198.2 32.5 %copy-start.2 = (bf16[32,8,512]{2,1,0:T(8,128)(2,1)}, bf16[32,8,512]{2,1,0:T(8,128)(2,1)S(1)}, u32[]{:S(2)}) copy-start(bf16[32,8,512]{2,1,0:T(8,128)(2,1)S(1)} %all_to_all.83) | copy-start | bytes 786436
  198.4 32.2 %collective-permute-start.8 = (bf16[64,1024]{1,0:T(8,128)(2,1)S(1)}, bf16[64,1024]{1,0:T(8,128)(2,1)S(1)}, u32[]{:S(2)}, u32[]{:S(2)}) collective-permute-start(bf16[64,1024]{1,0:T(8,128)(2,1)S(1)} %slice.77), channel_id=1, source_target_pairs={{0,1},{1,0},{2,3},{3,2},{4,5},{5,4},{6,7},{7,6},{8,9},{9,8},{10,11... | collective-permute-start | bytes 393224 | tf_op jit(solution)/shard_map/ppermute | solution.py:199
  228.4 2.2 collective-permute-start.7
  230.7 0.6 copy-start.9
  230.7 0.6 copy-start.8

commit v4 on v3

--- a/solution.py
+++ b/solution.py
@@ -8,9 +8,13 @@
 
 WIDTH = 8192
 ITERS = 2
-EARLY = 96
 BF16 = jnp.bfloat16
 F32 = jnp.float32
+WHOLE = pl.BlockSpec(memory_space=pltpu.VMEM)
+
+
+def on_chip(x):
+    return pltpu.with_memory_space_constraint(x, pltpu.VMEM)
 
 
 def dot_t(a, w):
@@ -87,10 +91,12 @@
 
     return pl.pallas_call(
         kernel,
-        out_shape=jax.ShapeDtypeStruct((rank, rank), F32),
+        in_specs=[WHOLE],
+        out_specs=WHOLE,
+        out_shape=pltpu.VMEM((rank, rank), F32),
         cost_estimate=pl.CostEstimate(flops=60_000_000, bytes_accessed=200_000, transcendentals=0),
         name="inverse_of",
-    )(arrived)
+    )(on_chip(arrived))
 
 
 def normalized_weighted(arrived, inverse, slope):
@@ -104,8 +110,12 @@
         out_ref[...] = (slope_ref[...] * forward.astype(F32)).astype(BF16)
 
     return pl.pallas_call(
-        kernel, out_shape=jax.ShapeDtypeStruct((rank, width), BF16), name="normalized_weighted"
-    )(arrived, inverse, slope)
+        kernel,
+        in_specs=[WHOLE] * 3,
+        out_specs=WHOLE,
+        out_shape=pltpu.VMEM((rank, width), BF16),
+        name="normalized_weighted",
+    )(on_chip(arrived), on_chip(inverse), on_chip(slope))
 
 
 def normalized_panels(core, inverse, inverse_there, image, there):
@@ -118,14 +128,19 @@
         away = exact_dot(inverse_there_ref[...], there_ref[...].astype(F32))
         out_ref[pl.ds(1 - here_at, 1)] = away[None]
 
-    whole = pl.BlockSpec(memory_space=pltpu.VMEM)
     return pl.pallas_call(
         kernel,
-        in_specs=[pl.BlockSpec(memory_space=pltpu.SMEM), whole, whole, whole, whole],
-        out_specs=whole,
+        in_specs=[pl.BlockSpec(memory_space=pltpu.SMEM)] + [WHOLE] * 4,
+        out_specs=WHOLE,
         out_shape=jax.ShapeDtypeStruct((2, rank, width), F32),
         name="normalized_panels",
-    )(core, inverse, inverse_there, image, there)
+    )(core, on_chip(inverse), on_chip(inverse_there), on_chip(image), on_chip(there))
+
+
+def three_parts(x):
+    high = lax.reduce_precision(x, 8, 7)
+    middle = lax.reduce_precision(x - high, 8, 7)
+    return high.astype(BF16), middle.astype(BF16), (x - high - middle).astype(BF16)
 
 
 def high_low(gram):
@@ -134,7 +149,10 @@
 
 
 def make(n_x, n_y, n_z):
-    swap = [(i * n_x + j, j * n_x + i) for i in range(n_y) for j in range(n_x)]
+    turns = [
+        [(i * n_x + j, j * n_x + (i + turn) % n_x) for i in range(n_y) for j in range(n_x)]
+        for turn in range(n_x)
+    ]
     flip = [(0, 1), (1, 0)]
 
     def on_device(weights, preact, panel):
@@ -151,14 +169,23 @@
 
         slopes = 1.0 - jnp.tanh(jnp.where(first, preact[0], preact[1])) ** 2
         slope_1 = slopes[0:1]
-        slope_2 = lax.ppermute(slopes[1:2], ("y", "x"), swap)
-
-        def moved(block):
-            here = lax.ppermute(block, ("y", "x"), swap)
-            there = lax.ppermute(here, "core", flip)
-            return jnp.concatenate([jnp.where(first, here, there), jnp.where(first, there, here)], axis=1)
-
-        w2 = jnp.concatenate([moved(w2_own[:EARLY]), moved(w2_own[EARLY:])], axis=0)
+
+        cut = width_row // n_x
+        high, middle, low = three_parts(slopes[1:2])
+        pad = jnp.zeros((8 - 3, width_in), BF16)
+        extra = jnp.concatenate([jnp.pad(p, ((0, 0), (0, width_in - width_row))) for p in (high, middle, low)] + [pad])
+        y_at, x_at = lax.axis_index("y"), lax.axis_index("x")
+        moved = []
+        for turn in range(n_x):
+            start = lax.rem(y_at + turn, n_x) * cut
+            piece = lax.dynamic_slice(w2_own, (start, 0), (cut, width_in), allow_negative_indices=False)
+            moved.append(lax.ppermute(jnp.concatenate([piece, extra]), ("y", "x"), turns[turn]))
+        here = jnp.concatenate([block[:cut] for block in moved])
+        sent = jnp.concatenate([block[cut : cut + 3].astype(F32).sum(0, keepdims=True)[:, :width_row] for block in moved])
+        slope_2 = lax.dynamic_slice(sent, (0, x_at * cut), (n_x, cut), allow_negative_indices=False).reshape(1, width_row)
+        there = lax.ppermute(here, "core", flip)
+        w2 = jnp.concatenate([jnp.where(first, here, there), jnp.where(first, there, here)], axis=1)
+        w2, slope_2 = lax.optimization_barrier((w2, slope_2))
         w1_other = lax.ppermute(w1_own, "core", flip)
 
         image = inverse = None

time: 235 us -> 214 us (0.911)
  waiting for transfers between devices: 37 us -> 18.6 us
  blocking collectives: 112 us -> 123 us
  starting transfers between devices: 59.3 us -> 51.6 us
  Pallas kernels: 11.2 us -> 5.6 us
    all_to_all x5 -> x4, waiting for transfers between devices: 35 us -> 16.2 us  [exchange(): return lax.all_to_all(tiles, axis, split_axis=0, concat_axis=0, tiled=True)]
    all_to_all x10 -> x11, blocking collectives: 112 us -> 123 us  [exchange(): return lax.all_to_all(tiles, axis, split_axis=0, concat_axis=0, tiled=True)]
    all_to_all x5 -> x4, starting transfers between devices: 28.4 us -> 18.2 us  [exchange(): return lax.all_to_all(tiles, axis, split_axis=0, concat_axis=0, tiled=True)]
    ppermute x5, starting transfers between devices: 3.66 us -> 9.96 us  [the longest x4 9.02 us: on_device(): lax.ppermute(jnp.concatenate([piece, extra]), ('y', 'x'), turns[turn])]
    pallas_call x4, Pallas kernels: 11.2 us -> 5.6 us  [the longest x2 4.03 us: inverse_of(): pl.pallas_call(kernel, in_specs=[WHOLE], out_specs=WHOLE, out_shape=pltpu...]
    ppermute x1, starting transfers between devices: 18.9 us -> 14.7 us  [on_device(): there = lax.ppermute(image[:, width_in:], 'core', flip)]
  transfers between devices with their start and end apart: 14 -> 13, of which waited for: 7 -> 6; matrix products, arithmetic and copies ran while one was open for 1% -> 3% of each run, Pallas kernels for 3% -> 2%
where the time goes in v4:
time: 214 us; the launch traced here: 213 us
  blocking collectives  123 us (57%)
  starting transfers between devices  51.6 us (24%)
  waiting for transfers between devices  18.6 us (9%)
  local copies, waits for them, and re-layouts  6.66 us (3%)
  Pallas kernels  5.6 us (3%)
  matrix products  4.81 us (2%)
  other arithmetic  2.47 us (1%)
    all_to_all x11, blocking collectives, exchange(): return lax.all_to_all(tiles, axis, split_axis=0, concat_axis=0, tiled=True)  123 us
    all_to_all x4, starting transfers between devices, exchange(): return lax.all_to_all(tiles, axis, split_axis=0, concat_axis=0, tiled=True)  18.2 us
    all_to_all x4, waiting for transfers between devices, exchange(): return lax.all_to_all(tiles, axis, split_axis=0, concat_axis=0, tiled=True)  16.2 us
    ppermute x1, starting transfers between devices, on_device(): there = lax.ppermute(image[:, width_in:], 'core', flip)  14.7 us
    ppermute x4, starting transfers between devices, on_device(): lax.ppermute(jnp.concatenate([piece, extra]), ('y', 'x'), turns[turn])  9.02 us
  transfers between devices with their start and end apart: 13, of which 6 were waited for; matrix products, arithmetic and copies ran while one was open for 3% of the time, Pallas kernels for 2%

profile of v4, /device:TPU:1, one launch (start us, length us, event | category | flops | bytes accessed | tf_op | source)
XLA Modules:
  0.0 212.9 jit_solution(12629744527500325271)
XLA Ops:
  0.0 0.9 copy-done
  1.0 1.3 fusion.1
  2.3 3.3 %collective-permute-start.5 = (f32[64,256]{1,0:T(8,128)S(1)}, f32[64,256]{1,0:T(8,128)S(1)}, u32[]{:S(2)}, u32[]{:S(2)}) collective-permute-start(f32[64,256]{1,0:T(8,128)S(1)} %select_bitcast_fusion), channel_id=1, source_target_pairs={{0,1},{1,0},{2,3},{3,2},{4,5},{5,4},{6,7},{7,6},{8,9},{9,8},{10,11... | collective-permute-start | bytes 196616 | tf_op jit(solution)/shard_map/ppermute | solution.py:168
  5.6 0.9 fusion.18
  6.7 0.7 collective-permute-start
  7.4 2.1 collective-permute-start.1
  9.5 4.3 %collective-permute-start.2 = (bf16[72,1024]{1,0:T(8,128)(2,1)S(1)}, bf16[72,1024]{1,0:T(8,128)(2,1)}, u32[]{:S(2)}, u32[]{:S(2)}) collective-permute-start(bf16[72,1024]{1,0:T(8,128)(2,1)S(1)} %concatenate.42), channel_id=1, source_target_pairs={{0,4},{2,68},{4,132},{6,196},{64,6},{66,70},{68,134},{70,198},{128... | collective-permute-start | bytes 442376 | tf_op jit(solution)/shard_map/ppermute | solution.py:182
  13.9 1.9 collective-permute-start.3
  15.9 0.6 broadcast_in_dim.37
  16.5 3.3 %all-to-all-start = ((bf16[4,64,256]{2,1,0:T(8,128)(2,1)}), bf16[4,64,256]{2,1,0:T(8,128)(2,1)S(1)}, u32[]{:S(2)}, u32[]{:S(2)}) async-start(bf16[4,64,256]{2,1,0:T(8,128)(2,1)} %broadcast_in_dim.37), calls=%async_computation | async-start | bytes 262144 | tf_op jit(solution)/shard_map/all_to_all | solution.py:29
  19.9 1.6 collective-permute-done.2
  21.5 0.9 slice.107
  22.4 0.6 copy-done.2
  23.1 0.9 collective-permute-start.4
  24.0 0.6 all-to-all-done
  24.7 0.7 broadcast_in_dim.38
  25.4 8.2 %all-to-all-start.1 = ((bf16[8,64,256]{2,1,0:T(8,128)(2,1)}), bf16[8,64,256]{2,1,0:T(8,128)(2,1)S(1)}, u32[]{:S(2)}, u32[]{:S(2)}) async-start(bf16[8,64,256]{2,1,0:T(8,128)(2,1)} %broadcast_in_dim.38), calls=%async_computation.1 | async-start | bytes 524288 | tf_op jit(solution)/shard_map/all_to_all | solution.py:29
  33.6 0.7 convert_reduce_fusion.4
  34.4 0.7 convert_reduce_fusion.3
  35.1 0.1 fusion.16
  35.2 0.1 reshape.109.slope_ref
  35.3 7.7 %all-to-all-done.1 = bf16[8,64,256]{2,1,0:T(8,128)(2,1)S(1)} async-done(((bf16[8,64,256]{2,1,0:T(8,128)(2,1)}), bf16[8,64,256]{2,1,0:T(8,128)(2,1)S(1)}, u32[]{:S(2)}, u32[]{:S(2)}) %all-to-all-start.1) | async-done | bytes 262176 | tf_op jit(solution)/shard_map/all_to_all | solution.py:29
  43.0 0.2 broadcast_select_fusion.1
  43.3 0.1 pad_maximum_fusion
  43.4 0.4 convolution_convert_fusion.7
  43.8 8.7 %all_to_all.75 = bf16[4,64,256]{2,1,0:T(8,128)(2,1)S(1)} all-to-all(bf16[4,64,256]{2,1,0:T(8,128)(2,1)S(1)} %broadcast_in_dim.39), channel_id=1, replica_groups=mesh['y'=4,'z'=8,'x'=4,'core'=2] {'y'}, dimensions={0} | all-to-all | bytes 262144 | tf_op jit(solution)/shard_map/all_to_all | solution.py:29
  52.5 0.3 convolution_convert_fusion.1
  52.8 0.7 copy.19
  53.5 3.4 %all-to-all-start.3 = ((bf16[8,64,256]{2,1,0:T(8,128)(2,1)}), bf16[8,64,256]{2,1,0:T(8,128)(2,1)S(1)}, u32[]{:S(2)}, u32[]{:S(2)}) async-start(bf16[8,64,256]{2,1,0:T(8,128)(2,1)} %bitcast.91), calls=%async_computation.3 | async-start | bytes 524288 | tf_op jit(solution)/shard_map/all_to_all | solution.py:29
  56.9 4.2 %collective-permute-start.6 = (bf16[256,1024]{1,0:T(8,128)(2,1)}, bf16[256,1024]{1,0:T(8,128)(2,1)S(1)}, u32[]{:S(2)}, u32[]{:S(2)}) collective-permute-start(bf16[256,1024]{1,0:T(8,128)(2,1)} %get-tuple-element.12), channel_id=1, source_target_pairs={{0,1},{1,0},{2,3},{3,2},{4,5},{5,4},{6,7},{7,6},{8,9},{9,8},{10,11... | collective-permute-start | bytes 1572872 | tf_op jit(solution)/shard_map/ppermute | solution.py:189
  61.1 5.1 %all-to-all-done.3 = bf16[8,64,256]{2,1,0:T(8,128)(2,1)S(1)} async-done(((bf16[8,64,256]{2,1,0:T(8,128)(2,1)}), bf16[8,64,256]{2,1,0:T(8,128)(2,1)S(1)}, u32[]{:S(2)}, u32[]{:S(2)}) %all-to-all-start.3) | async-done | bytes 262176 | tf_op jit(solution)/shard_map/all_to_all | solution.py:29
  66.3 12.3 %all_to_all.76 = bf16[4,64,256]{2,1,0:T(8,128)(2,1)S(1)} all-to-all(bf16[4,64,256]{2,1,0:T(8,128)(2,1)S(1)} %broadcast_in_dim.40), channel_id=1, replica_groups=mesh['y'=4,'z'=8,'x'=4,'core'=2] {'x'}, dimensions={0} | all-to-all | bytes 262144 | tf_op jit(solution)/shard_map/all_to_all | solution.py:29
  78.5 0.2 convolution_convert_fusion.5
  78.8 0.2 convolution_convert_fusion.4
  79.0 14.1 %all_to_all.77 = bf16[32,8,512]{2,1,0:T(8,128)(2,1)S(1)} all-to-all(bf16[32,8,512]{2,1,0:T(8,128)(2,1)S(1)} %bitcast.97), channel_id=1, replica_groups=mesh['y'=4,'z'=8,'x'=4,'core'=2] {'y','z'}, dimensions={0} | all-to-all | bytes 524288 | tf_op jit(solution)/shard_map/all_to_all | solution.py:29
  93.2 13.9 %all_to_all.78 = bf16[32,8,512]{2,1,0:T(8,128)(2,1)S(1)} all-to-all(bf16[32,8,512]{2,1,0:T(8,128)(2,1)S(1)} %broadcast_in_dim.41), channel_id=1, replica_groups=mesh['y'=4,'z'=8,'x'=4,'core'=2] {'y','z'}, dimensions={0} | all-to-all | bytes 524288 | tf_op jit(solution)/shard_map/all_to_all | solution.py:29
  107.1 0.3 fusion.8
  107.4 0.2 fusion.6
  107.6 0.2 reduce-precision_convert_fusion.1
  107.8 0.3 fusion
  108.1 0.1 pad_maximum_fusion.4
  108.2 7.5 %all_to_all.79.arrived_ref = bf16[4,64,384]{2,1,0:T(8,128)(2,1)S(1)} all-to-all(bf16[4,64,384]{2,1,0:T(8,128)(2,1)S(1)} %broadcast_in_dim.42), channel_id=1, replica_groups=mesh['y'=4,'z'=8,'x'=4,'core'=2] {'x'}, dimensions={0} | all-to-all | bytes 393216 | tf_op jit(solution)/shard_map/all_to_all | solution.py:29
  115.8 12.4 %all_to_all.80 = bf16[8,64,256]{2,1,0:T(8,128)(2,1)S(1)} all-to-all(bf16[8,64,256]{2,1,0:T(8,128)(2,1)S(1)} %broadcast_in_dim.43), channel_id=1, replica_groups=mesh['y'=4,'z'=8,'x'=4,'core'=2] {'z'}, dimensions={0} | all-to-all | bytes 524288 | tf_op jit(solution)/shard_map/all_to_all | solution.py:29
  128.2 0.4 convolution_convert_fusion.6
  128.6 0.7 broadcast_in_dim.44
  129.3 3.3 %all-to-all-start.9 = ((bf16[4,64,256]{2,1,0:T(8,128)(2,1)}), bf16[4,64,256]{2,1,0:T(8,128)(2,1)S(1)}, u32[]{:S(2)}, u32[]{:S(2)}) async-start(bf16[4,64,256]{2,1,0:T(8,128)(2,1)} %broadcast_in_dim.44), calls=%async_computation.9 | async-start | bytes 262144 | tf_op jit(solution)/shard_map/all_to_all | solution.py:29
  132.6 2.0 inverse_of.2.inverse_ref
  134.6 2.8 %all-to-all-done.9.arrived_ref = bf16[4,64,256]{2,1,0:T(8,128)(2,1)S(1)} async-done(((bf16[4,64,256]{2,1,0:T(8,128)(2,1)}), bf16[4,64,256]{2,1,0:T(8,128)(2,1)S(1)}, u32[]{:S(2)}, u32[]{:S(2)}) %all-to-all-start.9) | async-done | bytes 131104 | tf_op jit(solution)/shard_map/all_to_all | solution.py:29
  137.4 0.2 normalized_weighted.1
  137.6 0.3 convolution_convert_fusion
  138.0 11.7 %all_to_all.81 = bf16[8,64,256]{2,1,0:T(8,128)(2,1)S(1)} all-to-all(bf16[8,64,256]{2,1,0:T(8,128)(2,1)S(1)} %bitcast.100), channel_id=1, replica_groups=mesh['y'=4,'z'=8,'x'=4,'core'=2] {'z'}, dimensions={0} | all-to-all | bytes 524288 | tf_op jit(solution)/shard_map/all_to_all | solution.py:29
  149.8 7.2 %all_to_all.82 = bf16[4,64,256]{2,1,0:T(8,128)(2,1)S(1)} all-to-all(bf16[4,64,256]{2,1,0:T(8,128)(2,1)S(1)} %broadcast_in_dim.45), channel_id=1, replica_groups=mesh['y'=4,'z'=8,'x'=4,'core'=2] {'x'}, dimensions={0} | all-to-all | bytes 262144 | tf_op jit(solution)/shard_map/all_to_all | solution.py:29
  157.0 0.2 convolution_convert_fusion.3
  157.2 0.2 convolution_convert_fusion.2
  157.5 12.6 %all_to_all.83 = bf16[32,8,512]{2,1,0:T(8,128)(2,1)S(1)} all-to-all(bf16[32,8,512]{2,1,0:T(8,128)(2,1)S(1)} %bitcast.98), channel_id=1, replica_groups=mesh['y'=4,'z'=8,'x'=4,'core'=2] {'y','z'}, dimensions={0} | all-to-all | bytes 524288 | tf_op jit(solution)/shard_map/all_to_all | solution.py:29
  170.2 15.4 %all_to_all.84 = bf16[32,8,512]{2,1,0:T(8,128)(2,1)S(1)} all-to-all(bf16[32,8,512]{2,1,0:T(8,128)(2,1)S(1)} %broadcast_in_dim.46), channel_id=1, replica_groups=mesh['y'=4,'z'=8,'x'=4,'core'=2] {'y','z'}, dimensions={0} | all-to-all | bytes 524288 | tf_op jit(solution)/shard_map/all_to_all | solution.py:29
  185.6 0.2 reduce-precision_convert_fusion
  185.8 14.7 %collective-permute-start.8 = (bf16[64,1024]{1,0:T(8,128)(2,1)S(1)}, bf16[64,1024]{1,0:T(8,128)(2,1)S(1)}, u32[]{:S(2)}, u32[]{:S(2)}) collective-permute-start(bf16[64,1024]{1,0:T(8,128)(2,1)S(1)} %slice.122), channel_id=1, source_target_pairs={{0,1},{1,0},{2,3},{3,2},{4,5},{5,4},{6,7},{7,6},{8,9},{9,8},{10,11... | collective-permute-start | bytes 393224 | tf_op jit(solution)/shard_map/ppermute | solution.py:226
  200.5 0.1 pad_maximum_fusion.5
  200.6 6.9 %all_to_all.85.arrived_ref = bf16[4,64,128]{2,1,0:T(8,128)(2,1)S(1)} all-to-all(bf16[4,64,128]{2,1,0:T(8,128)(2,1)S(1)} %broadcast_in_dim.47), channel_id=1, replica_groups=mesh['y'=4,'z'=8,'x'=4,'core'=2] {'x'}, dimensions={0} | all-to-all | bytes 131072 | tf_op jit(solution)/shard_map/all_to_all | solution.py:29
  207.4 2.0 inverse_of.3.inverse_ref
  209.4 1.2 collective-permute-start.7
  210.7 0.9 collective-permute-done.7.inverse_there_ref
  211.5 1.4 normalized_panels.1
  (62 shorter events, 1.0 us)
Async XLA Ops:
  0.0 1.0 copy-start
  0.0 5.6 %copy-start.1 = (bf16[2,256,1024]{2,1,0:T(8,128)(2,1)S(1)}, bf16[2,256,1024]{2,1,0:T(8,128)(2,1)}, u32[]{:S(2)}) copy-start(bf16[2,256,1024]{2,1,0:T(8,128)(2,1)} %param.3) | copy-start | bytes 3145732
  2.3 13.5 %collective-permute-start.5 = (f32[64,256]{1,0:T(8,128)S(1)}, f32[64,256]{1,0:T(8,128)S(1)}, u32[]{:S(2)}, u32[]{:S(2)}) collective-permute-start(f32[64,256]{1,0:T(8,128)S(1)} %select_bitcast_fusion), channel_id=1, source_target_pairs={{0,1},{1,0},{2,3},{3,2},{4,5},{5,4},{6,7},{7,6},{8,9},{9,8},{10,11... | collective-permute-start | bytes 196616 | tf_op jit(solution)/shard_map/ppermute | solution.py:168
  5.6 0.9 copy-start.3
  6.7 13.2 %collective-permute-start = (bf16[72,1024]{1,0:T(8,128)(2,1)S(1)}, bf16[72,1024]{1,0:T(8,128)(2,1)S(1)}, u32[]{:S(2)}, u32[]{:S(2)}) collective-permute-start(bf16[72,1024]{1,0:T(8,128)(2,1)S(1)} %concatenate.40), channel_id=1, source_target_pairs={{0,0},{2,64},{4,128},{6,192},{64,2},{66,66},{68,130},{70,194},{128... | collective-permute-start | bytes 442376 | tf_op jit(solution)/shard_map/ppermute | solution.py:182
  7.4 12.5 %collective-permute-start.1 = (bf16[72,1024]{1,0:T(8,128)(2,1)S(1)}, bf16[72,1024]{1,0:T(8,128)(2,1)S(1)}, u32[]{:S(2)}, u32[]{:S(2)}) collective-permute-start(bf16[72,1024]{1,0:T(8,128)(2,1)S(1)} %concatenate.41), channel_id=1, source_target_pairs={{0,2},{2,66},{4,130},{6,194},{64,4},{66,68},{68,132},{70,196},{128... | collective-permute-start | bytes 442376 | tf_op jit(solution)/shard_map/ppermute | solution.py:182
  9.5 11.9 %collective-permute-start.2 = (bf16[72,1024]{1,0:T(8,128)(2,1)S(1)}, bf16[72,1024]{1,0:T(8,128)(2,1)}, u32[]{:S(2)}, u32[]{:S(2)}) collective-permute-start(bf16[72,1024]{1,0:T(8,128)(2,1)S(1)} %concatenate.42), channel_id=1, source_target_pairs={{0,4},{2,68},{4,132},{6,196},{64,6},{66,70},{68,134},{70,198},{128... | collective-permute-start | bytes 442376 | tf_op jit(solution)/shard_map/ppermute | solution.py:182
  13.9 8.5 %collective-permute-start.3 = (bf16[72,1024]{1,0:T(8,128)(2,1)S(1)}, bf16[72,1024]{1,0:T(8,128)(2,1)S(1)}, u32[]{:S(2)}, u32[]{:S(2)}) collective-permute-start(bf16[72,1024]{1,0:T(8,128)(2,1)S(1)} %concatenate.43), channel_id=1, source_target_pairs={{0,6},{2,70},{4,134},{6,198},{64,0},{66,64},{68,128},{70,192},{128... | collective-permute-start | bytes 442376 | tf_op jit(solution)/shard_map/ppermute | solution.py:182
  16.5 8.1 %all-to-all-start = ((bf16[4,64,256]{2,1,0:T(8,128)(2,1)}), bf16[4,64,256]{2,1,0:T(8,128)(2,1)S(1)}, u32[]{:S(2)}, u32[]{:S(2)}) async-start(bf16[4,64,256]{2,1,0:T(8,128)(2,1)} %broadcast_in_dim.37), calls=%async_computation | async-start | bytes 262144 | tf_op jit(solution)/shard_map/all_to_all | solution.py:29
  22.4 0.6 copy-start.2
  23.1 19.9 %collective-permute-start.4 = (bf16[256,1024]{1,0:T(8,128)(2,1)S(1)}, bf16[256,1024]{1,0:T(8,128)(2,1)S(1)}, u32[]{:S(2)}, u32[]{:S(2)}) collective-permute-start(bf16[256,1024]{1,0:T(8,128)(2,1)S(1)} %pad_maximum_fusion.1), channel_id=1, source_target_pairs={{0,1},{1,0},{2,3},{3,2},{4,5},{5,4},{6,7},{7,6},{8,9},{9,8},{10,11... | collective-permute-start | bytes 1572872 | tf_op jit(solution)/shard_map/ppermute | solution.py:186
  25.4 17.6 %all-to-all-start.1 = ((bf16[8,64,256]{2,1,0:T(8,128)(2,1)}), bf16[8,64,256]{2,1,0:T(8,128)(2,1)S(1)}, u32[]{:S(2)}, u32[]{:S(2)}) async-start(bf16[8,64,256]{2,1,0:T(8,128)(2,1)} %broadcast_in_dim.38), calls=%async_computation.1 | async-start | bytes 524288 | tf_op jit(solution)/shard_map/all_to_all | solution.py:29
  53.5 12.7 %all-to-all-start.3 = ((bf16[8,64,256]{2,1,0:T(8,128)(2,1)}), bf16[8,64,256]{2,1,0:T(8,128)(2,1)S(1)}, u32[]{:S(2)}, u32[]{:S(2)}) async-start(bf16[8,64,256]{2,1,0:T(8,128)(2,1)} %bitcast.91), calls=%async_computation.3 | async-start | bytes 524288 | tf_op jit(solution)/shard_map/all_to_all | solution.py:29
  56.9 21.8 %collective-permute-start.6 = (bf16[256,1024]{1,0:T(8,128)(2,1)}, bf16[256,1024]{1,0:T(8,128)(2,1)S(1)}, u32[]{:S(2)}, u32[]{:S(2)}) collective-permute-start(bf16[256,1024]{1,0:T(8,128)(2,1)} %get-tuple-element.12), channel_id=1, source_target_pairs={{0,1},{1,0},{2,3},{3,2},{4,5},{5,4},{6,7},{7,6},{8,9},{9,8},{10,11... | collective-permute-start | bytes 1572872 | tf_op jit(solution)/shard_map/ppermute | solution.py:189
  129.3 8.1 %all-to-all-start.9 = ((bf16[4,64,256]{2,1,0:T(8,128)(2,1)}), bf16[4,64,256]{2,1,0:T(8,128)(2,1)S(1)}, u32[]{:S(2)}, u32[]{:S(2)}) async-start(bf16[4,64,256]{2,1,0:T(8,128)(2,1)} %broadcast_in_dim.44), calls=%async_computation.9 | async-start | bytes 262144 | tf_op jit(solution)/shard_map/all_to_all | solution.py:29
  185.8 25.7 %collective-permute-start.8 = (bf16[64,1024]{1,0:T(8,128)(2,1)S(1)}, bf16[64,1024]{1,0:T(8,128)(2,1)S(1)}, u32[]{:S(2)}, u32[]{:S(2)}) collective-permute-start(bf16[64,1024]{1,0:T(8,128)(2,1)S(1)} %slice.122), channel_id=1, source_target_pairs={{0,1},{1,0},{2,3},{3,2},{4,5},{5,4},{6,7},{7,6},{8,9},{9,8},{10,11... | collective-permute-start | bytes 393224 | tf_op jit(solution)/shard_map/ppermute | solution.py:226
  209.4 2.1 collective-permute-start.7

commit v5 on v4

--- a/solution.py
+++ b/solution.py
@@ -99,23 +99,23 @@
     )(on_chip(arrived))
 
 
-def normalized_weighted(arrived, inverse, slope):
-    count, rank, width = arrived.shape
-
-    def kernel(arrived_ref, inverse_ref, slope_ref, out_ref):
-        summed = arrived_ref[0].astype(F32)
+def normalized_forward(arrived, slope, width):
+    count, rank, _ = arrived.shape
+
+    def kernel(arrived_ref, slope_ref, out_ref):
+        inverse = inverse_factor(gram_of_parts(arrived_ref, width, rank))
+        summed = arrived_ref[0, :, :width].astype(F32)
         for i in range(1, count):
-            summed = summed + arrived_ref[i].astype(F32)
-        forward = (slope_ref[...] * exact_dot(inverse_ref[...], summed)).astype(BF16)
-        out_ref[...] = (slope_ref[...] * forward.astype(F32)).astype(BF16)
+            summed = summed + arrived_ref[i, :, :width].astype(F32)
+        out_ref[...] = (slope_ref[...] * exact_dot(inverse, summed)).astype(BF16)
 
     return pl.pallas_call(
         kernel,
-        in_specs=[WHOLE] * 3,
+        in_specs=[WHOLE] * 2,
         out_specs=WHOLE,
         out_shape=pltpu.VMEM((rank, width), BF16),
-        name="normalized_weighted",
-    )(on_chip(arrived), on_chip(inverse), on_chip(slope))
+        name="normalized_forward",
+    )(on_chip(arrived), on_chip(slope))
 
 
 def normalized_panels(core, inverse, inverse_there, image, there):
@@ -185,30 +185,27 @@
         slope_2 = lax.dynamic_slice(sent, (0, x_at * cut), (n_x, cut), allow_negative_indices=False).reshape(1, width_row)
         there = lax.ppermute(here, "core", flip)
         w2 = jnp.concatenate([jnp.where(first, here, there), jnp.where(first, there, here)], axis=1)
-        w2, slope_2 = lax.optimization_barrier((w2, slope_2))
         w1_other = lax.ppermute(w1_own, "core", flip)
-
-        image = inverse = None
+        w2, slope_2, w1_other = lax.optimization_barrier((w2, slope_2, w1_other))
+
+        image = None
         for iteration in range(ITERS):
             if iteration == 0:
                 arrived = to_all(summed_out.astype(BF16), "x", n_x)
+                forward = (slope_1 * total(arrived)).astype(BF16)
             else:
                 own, other = image[:, :width_in], image[:, width_in:]
                 partial_out = dot_t(own, w1_own) + dot_t(other, w1_other)
                 gram = dot_t(own, own) + dot_t(other, other)
                 message = jnp.concatenate([partial_out.astype(BF16), high_low(gram)], axis=1)
                 arrived = to_all(message, "x", n_x)
-                inverse = inverse_of(arrived, width_row)
-            forward = (slope_1 * total(arrived[:, :, :width_row])).astype(BF16)
+                forward = normalized_forward(arrived, slope_1, width_row)
             spread = to_all(forward, "z", n_z)
             spread = jnp.moveaxis(spread, 0, 1).reshape(rank, n_z * width_row)
             partial_out = dot_t(spread, w2)
             arrived = to_all(partial_out.astype(BF16), "y", n_y)
-            if inverse is None:
-                forward = (slope_2 * total(arrived)).astype(BF16)
-                weighted = (slope_2 * forward.astype(F32)).astype(BF16)
-            else:
-                weighted = normalized_weighted(arrived, inverse, slope_2)
+            forward = (slope_2 * total(arrived)).astype(BF16)
+            weighted = (slope_2 * forward.astype(F32)).astype(BF16)
             partial_in = dot_n(weighted, w2).astype(BF16)
             blocks = jnp.moveaxis(partial_in.reshape(rank, n_z, width_row), 1, 0)
             summed = total(exchange(blocks, "z")).astype(BF16)

time: 214 us -> 210 us (0.981)
  blocking collectives: 123 us -> 133 us
  starting transfers between devices: 51.6 us -> 45.5 us
  waiting for transfers between devices: 18.6 us -> 13.2 us
    all_to_all x11 -> x13, blocking collectives: 123 us -> 133 us  [exchange(): return lax.all_to_all(tiles, axis, split_axis=0, concat_axis=0, tiled=True)]
    all_to_all x4 -> x2, starting transfers between devices: 18.2 us -> 11.5 us  [exchange(): return lax.all_to_all(tiles, axis, split_axis=0, concat_axis=0, tiled=True)]
    all_to_all x4 -> x2, waiting for transfers between devices: 16.2 us -> 11.5 us  [exchange(): return lax.all_to_all(tiles, axis, split_axis=0, concat_axis=0, tiled=True)]
    ppermute x1, starting transfers between devices: 14.7 us -> 18.9 us  [on_device(): there = lax.ppermute(image[:, width_in:], 'core', flip)]
    ppermute x1, starting transfers between devices: 4.16 us -> 0.35 us  [on_device(): w1_other = lax.ppermute(w1_own, 'core', flip)]
    ppermute x4, starting transfers between devices: 9.02 us -> 11.7 us  [on_device(): lax.ppermute(jnp.concatenate([piece, extra]), ('y', 'x'), turns[turn])]
  transfers between devices with their start and end apart: 13 -> 11, of which waited for: 6 -> 4; matrix products, arithmetic and copies ran while one was open for 3% -> 2% of each run, Pallas kernels for 2% -> 1%
where the time goes in v5:
time: 210 us; the launch traced here: 209 us
  blocking collectives  133 us (63%)
  starting transfers between devices  45.5 us (22%)
  waiting for transfers between devices  13.2 us (6%)
  Pallas kernels  5.57 us (3%)
  local copies, waits for them, and re-layouts  4.73 us (2%)
  matrix products  3.77 us (2%)
  other arithmetic  3.25 us (2%)
    all_to_all x13, blocking collectives, exchange(): return lax.all_to_all(tiles, axis, split_axis=0, concat_axis=0, tiled=True)  133 us
    ppermute x1, starting transfers between devices, on_device(): there = lax.ppermute(image[:, width_in:], 'core', flip)  18.9 us
    ppermute x4, starting transfers between devices, on_device(): lax.ppermute(jnp.concatenate([piece, extra]), ('y', 'x'), turns[turn])  11.7 us
    all_to_all x2, starting transfers between devices, exchange(): return lax.all_to_all(tiles, axis, split_axis=0, concat_axis=0, tiled=True)  11.5 us
    all_to_all x2, waiting for transfers between devices, exchange(): return lax.all_to_all(tiles, axis, split_axis=0, concat_axis=0, tiled=True)  11.5 us
  transfers between devices with their start and end apart: 11, of which 4 were waited for; matrix products, arithmetic and copies ran while one was open for 2% of the time, Pallas kernels for 1%

profile of v5, /device:TPU:1, one launch (start us, length us, event | category | flops | bytes accessed | tf_op | source)
XLA Modules:
  0.0 209.4 jit_solution(1714448722478417032)
XLA Ops:
  0.0 2.1 %slice_bitcast_fusion = (bf16[256,1024]{1,0:T(8,128)(2,1)}, bf16[1,256,1024]{2,1,0:T(8,128)(2,1)S(1)}) fusion(bf16[2,256,1024]{2,1,0:T(8,128)(2,1)} %param.3), kind=kLoop, calls=%fused_computation.18 | loop fusion | bytes 2097152 | tf_op jit(solution)/shard_map/squeeze | solution.py:163
  2.2 0.0 copy-start.1
  2.3 0.8 collective-permute-start
  3.2 4.6 %collective-permute-start.1 = (bf16[72,1024]{1,0:T(8,128)(2,1)S(1)}, bf16[72,1024]{1,0:T(8,128)(2,1)S(1)}, u32[]{:S(2)}, u32[]{:S(2)}) collective-permute-start(bf16[72,1024]{1,0:T(8,128)(2,1)S(1)} %concatenate.41), channel_id=1, source_target_pairs={{0,2},{2,66},{4,130},{6,194},{64,4},{66,68},{68,132},{70,196},{128... | collective-permute-start | bytes 442376 | tf_op jit(solution)/shard_map/ppermute | solution.py:182
  7.8 4.3 %collective-permute-start.2 = (bf16[72,1024]{1,0:T(8,128)(2,1)S(1)}, bf16[72,1024]{1,0:T(8,128)(2,1)S(1)}, u32[]{:S(2)}, u32[]{:S(2)}) collective-permute-start(bf16[72,1024]{1,0:T(8,128)(2,1)S(1)} %concatenate.42), channel_id=1, source_target_pairs={{0,4},{2,68},{4,132},{6,196},{64,6},{66,70},{68,134},{70,198},{128... | collective-permute-start | bytes 442376 | tf_op jit(solution)/shard_map/ppermute | solution.py:182
  12.2 1.9 collective-permute-start.3
  14.2 0.3 fusion.1
  14.5 1.7 collective-permute-start.6
  16.2 0.9 collective-permute-done.6
  17.1 0.4 collective-permute-start.5
  17.5 0.7 broadcast_in_dim.37
  18.1 3.3 %all-to-all-start = ((bf16[4,64,256]{2,1,0:T(8,128)(2,1)}), bf16[4,64,256]{2,1,0:T(8,128)(2,1)S(1)}, u32[]{:S(2)}, u32[]{:S(2)}) async-start(bf16[4,64,256]{2,1,0:T(8,128)(2,1)} %broadcast_in_dim.37), calls=%async_computation | async-start | bytes 262144 | tf_op jit(solution)/shard_map/all_to_all | solution.py:29
  21.4 0.0 collective-permute-done
  21.5 0.0 collective-permute-done.2
  21.6 0.6 copy-done.2
  22.2 0.8 pad_maximum_fusion.1
  23.0 0.2 collective-permute-start.4
  23.2 3.2 %all-to-all-done = bf16[4,64,256]{2,1,0:T(8,128)(2,1)S(1)} async-done(((bf16[4,64,256]{2,1,0:T(8,128)(2,1)}), bf16[4,64,256]{2,1,0:T(8,128)(2,1)S(1)}, u32[]{:S(2)}, u32[]{:S(2)}) %all-to-all-start) | async-done | bytes 131104 | tf_op jit(solution)/shard_map/all_to_all | solution.py:29
  26.4 0.7 broadcast_in_dim.38
  27.1 8.2 %all-to-all-start.1 = ((bf16[8,64,256]{2,1,0:T(8,128)(2,1)}), bf16[8,64,256]{2,1,0:T(8,128)(2,1)S(1)}, u32[]{:S(2)}, u32[]{:S(2)}) async-start(bf16[8,64,256]{2,1,0:T(8,128)(2,1)} %broadcast_in_dim.38), calls=%async_computation.1 | async-start | bytes 524288 | tf_op jit(solution)/shard_map/all_to_all | solution.py:29
  35.3 0.7 convert_reduce_fusion.4
  36.1 0.7 convert_reduce_fusion.3
  36.8 0.1 fusion.17
  36.9 0.1 reshape.90
  37.0 8.3 %all-to-all-done.1 = bf16[8,64,256]{2,1,0:T(8,128)(2,1)S(1)} async-done(((bf16[8,64,256]{2,1,0:T(8,128)(2,1)}), bf16[8,64,256]{2,1,0:T(8,128)(2,1)S(1)}, u32[]{:S(2)}, u32[]{:S(2)}) %all-to-all-start.1) | async-done | bytes 262176 | tf_op jit(solution)/shard_map/all_to_all | solution.py:29
  45.3 0.0 collective-permute-done.4
  45.3 0.2 broadcast_select_fusion.1
  45.6 0.1 pad_maximum_fusion
  45.7 0.4 convolution_convert_fusion.7
  46.1 7.7 %all_to_all.75 = bf16[4,64,256]{2,1,0:T(8,128)(2,1)S(1)} all-to-all(bf16[4,64,256]{2,1,0:T(8,128)(2,1)S(1)} %broadcast_in_dim.39), channel_id=1, replica_groups=mesh['y'=4,'z'=8,'x'=4,'core'=2] {'y'}, dimensions={0} | all-to-all | bytes 262144 | tf_op jit(solution)/shard_map/all_to_all | solution.py:29
  53.9 0.3 convolution_convert_fusion.1
  54.2 12.1 %all_to_all.76 = bf16[8,64,256]{2,1,0:T(8,128)(2,1)S(1)} all-to-all(bf16[8,64,256]{2,1,0:T(8,128)(2,1)S(1)} %bitcast.99), channel_id=1, replica_groups=mesh['y'=4,'z'=8,'x'=4,'core'=2] {'z'}, dimensions={0} | all-to-all | bytes 524288 | tf_op jit(solution)/shard_map/all_to_all | solution.py:29
  66.4 7.2 %all_to_all.77 = bf16[4,64,256]{2,1,0:T(8,128)(2,1)S(1)} all-to-all(bf16[4,64,256]{2,1,0:T(8,128)(2,1)S(1)} %broadcast_in_dim.40), channel_id=1, replica_groups=mesh['y'=4,'z'=8,'x'=4,'core'=2] {'x'}, dimensions={0} | all-to-all | bytes 262144 | tf_op jit(solution)/shard_map/all_to_all | solution.py:29
  73.6 0.2 convolution_convert_fusion.5
  73.8 0.2 convolution_convert_fusion.4
  74.1 12.6 %all_to_all.78 = bf16[32,8,512]{2,1,0:T(8,128)(2,1)S(1)} all-to-all(bf16[32,8,512]{2,1,0:T(8,128)(2,1)S(1)} %bitcast.97), channel_id=1, replica_groups=mesh['y'=4,'z'=8,'x'=4,'core'=2] {'y','z'}, dimensions={0} | all-to-all | bytes 524288 | tf_op jit(solution)/shard_map/all_to_all | solution.py:29
  86.7 0.1 reduce_sum.143
  86.8 13.8 %all_to_all.79 = bf16[32,8,512]{2,1,0:T(8,128)(2,1)S(1)} all-to-all(bf16[32,8,512]{2,1,0:T(8,128)(2,1)S(1)} %broadcast_in_dim.41), channel_id=1, replica_groups=mesh['y'=4,'z'=8,'x'=4,'core'=2] {'y','z'}, dimensions={0} | all-to-all | bytes 524288 | tf_op jit(solution)/shard_map/all_to_all | solution.py:29
  100.6 0.3 fusion.8
  100.9 0.2 fusion.6
  101.1 0.3 fusion
  101.3 0.2 reduce-precision_convert_fusion.1
  101.5 0.1 pad_maximum_fusion.4
  101.6 7.5 %all_to_all.80.arrived_ref = bf16[4,64,384]{2,1,0:T(8,128)(2,1)S(1)} all-to-all(bf16[4,64,384]{2,1,0:T(8,128)(2,1)S(1)} %broadcast_in_dim.42), channel_id=1, replica_groups=mesh['y'=4,'z'=8,'x'=4,'core'=2] {'x'}, dimensions={0} | all-to-all | bytes 393216 | tf_op jit(solution)/shard_map/all_to_all | solution.py:29
  109.2 2.2 %normalized_forward.1 = bf16[64,256]{1,0:T(8,128)(2,1)S(1)} custom-call(bf16[4,64,384]{2,1,0:T(8,128)(2,1)S(1)} %all_to_all.80.arrived_ref, f32[1,256]{1,0:T(1,128)S(1)} %get-tuple-element.23.slope_ref), custom_call_target="tpu_custom_call" | custom-call | tf_op jit(solution)/shard_map/normalized_forward/pallas_call | solution.py:112
  111.4 12.4 %all_to_all.81 = bf16[8,64,256]{2,1,0:T(8,128)(2,1)S(1)} all-to-all(bf16[8,64,256]{2,1,0:T(8,128)(2,1)S(1)} %broadcast_in_dim.43), channel_id=1, replica_groups=mesh['y'=4,'z'=8,'x'=4,'core'=2] {'z'}, dimensions={0} | all-to-all | bytes 524288 | tf_op jit(solution)/shard_map/all_to_all | solution.py:29
  123.8 0.4 convolution_convert_fusion.6
  124.3 7.2 %all_to_all.82 = bf16[4,64,256]{2,1,0:T(8,128)(2,1)S(1)} all-to-all(bf16[4,64,256]{2,1,0:T(8,128)(2,1)S(1)} %broadcast_in_dim.44), channel_id=1, replica_groups=mesh['y'=4,'z'=8,'x'=4,'core'=2] {'y'}, dimensions={0} | all-to-all | bytes 262144 | tf_op jit(solution)/shard_map/all_to_all | solution.py:29
  131.5 0.3 convolution_convert_fusion
  131.8 11.7 %all_to_all.83 = bf16[8,64,256]{2,1,0:T(8,128)(2,1)S(1)} all-to-all(bf16[8,64,256]{2,1,0:T(8,128)(2,1)S(1)} %bitcast.101), channel_id=1, replica_groups=mesh['y'=4,'z'=8,'x'=4,'core'=2] {'z'}, dimensions={0} | all-to-all | bytes 524288 | tf_op jit(solution)/shard_map/all_to_all | solution.py:29
  143.6 7.2 %all_to_all.84 = bf16[4,64,256]{2,1,0:T(8,128)(2,1)S(1)} all-to-all(bf16[4,64,256]{2,1,0:T(8,128)(2,1)S(1)} %broadcast_in_dim.45), channel_id=1, replica_groups=mesh['y'=4,'z'=8,'x'=4,'core'=2] {'x'}, dimensions={0} | all-to-all | bytes 262144 | tf_op jit(solution)/shard_map/all_to_all | solution.py:29
  150.9 0.2 convolution_convert_fusion.3
  151.1 0.2 convolution_convert_fusion.2
  151.3 12.6 %all_to_all.85 = bf16[32,8,512]{2,1,0:T(8,128)(2,1)S(1)} all-to-all(bf16[32,8,512]{2,1,0:T(8,128)(2,1)S(1)} %bitcast.98), channel_id=1, replica_groups=mesh['y'=4,'z'=8,'x'=4,'core'=2] {'y','z'}, dimensions={0} | all-to-all | bytes 524288 | tf_op jit(solution)/shard_map/all_to_all | solution.py:29
  164.0 0.1 reduce_sum.147
  164.0 13.8 %all_to_all.86 = bf16[32,8,512]{2,1,0:T(8,128)(2,1)S(1)} all-to-all(bf16[32,8,512]{2,1,0:T(8,128)(2,1)S(1)} %broadcast_in_dim.46), channel_id=1, replica_groups=mesh['y'=4,'z'=8,'x'=4,'core'=2] {'y','z'}, dimensions={0} | all-to-all | bytes 524288 | tf_op jit(solution)/shard_map/all_to_all | solution.py:29
  177.9 0.2 reduce-precision_convert_fusion
  178.1 18.9 %collective-permute-start.8 = (bf16[64,1024]{1,0:T(8,128)(2,1)S(1)}, bf16[64,1024]{1,0:T(8,128)(2,1)S(1)}, u32[]{:S(2)}, u32[]{:S(2)}) collective-permute-start(bf16[64,1024]{1,0:T(8,128)(2,1)S(1)} %slice.120), channel_id=1, source_target_pairs={{0,1},{1,0},{2,3},{3,2},{4,5},{5,4},{6,7},{7,6},{8,9},{9,8},{10,11... | collective-permute-start | bytes 393224 | tf_op jit(solution)/shard_map/ppermute | solution.py:223
  197.0 0.1 pad_maximum_fusion.5
  197.1 6.9 %all_to_all.87.arrived_ref = bf16[4,64,128]{2,1,0:T(8,128)(2,1)S(1)} all-to-all(bf16[4,64,128]{2,1,0:T(8,128)(2,1)S(1)} %broadcast_in_dim.47), channel_id=1, replica_groups=mesh['y'=4,'z'=8,'x'=4,'core'=2] {'x'}, dimensions={0} | all-to-all | bytes 131072 | tf_op jit(solution)/shard_map/all_to_all | solution.py:29
  204.0 2.0 inverse_of.1.inverse_ref
  206.0 1.2 collective-permute-start.7
  207.2 0.9 collective-permute-done.7.inverse_there_ref
  208.1 1.4 normalized_panels.1
  (60 shorter events, 0.9 us)
Async XLA Ops:
  0.0 14.1 %copy-start = (bf16[2,64,1024]{2,1,0:T(8,128)(2,1)S(1)}, bf16[2,64,1024]{2,1,0:T(8,128)(2,1)}, u32[]{:S(2)}) copy-start(bf16[2,64,1024]{2,1,0:T(8,128)(2,1)} %param.5) | copy-start | bytes 786436
  0.0 2.1 %copy-start.4 = (f32[2,2,256]{2,1,0:T(2,128)S(1)}, f32[2,2,256]{2,1,0:T(2,128)}, u32[]{:S(2)}) copy-start(f32[2,2,256]{2,1,0:T(2,128)} %param.4) | copy-start | bytes 12292
  2.2 12.0 %copy-start.1 = (bf16[2,256,1024]{2,1,0:T(8,128)(2,1)S(1)}, bf16[2,256,1024]{2,1,0:T(8,128)(2,1)}, u32[]{:S(2)}) copy-start(bf16[2,256,1024]{2,1,0:T(8,128)(2,1)} %param.3) | copy-start | bytes 3145732
  2.3 19.1 %collective-permute-start = (bf16[72,1024]{1,0:T(8,128)(2,1)S(1)}, bf16[72,1024]{1,0:T(8,128)(2,1)S(1)}, u32[]{:S(2)}, u32[]{:S(2)}) collective-permute-start(bf16[72,1024]{1,0:T(8,128)(2,1)S(1)} %concatenate.40), channel_id=1, source_target_pairs={{0,0},{2,64},{4,128},{6,192},{64,2},{66,66},{68,130},{70,194},{128... | collective-permute-start | bytes 442376 | tf_op jit(solution)/shard_map/ppermute | solution.py:182
  3.2 18.3 %collective-permute-start.1 = (bf16[72,1024]{1,0:T(8,128)(2,1)S(1)}, bf16[72,1024]{1,0:T(8,128)(2,1)S(1)}, u32[]{:S(2)}, u32[]{:S(2)}) collective-permute-start(bf16[72,1024]{1,0:T(8,128)(2,1)S(1)} %concatenate.41), channel_id=1, source_target_pairs={{0,2},{2,66},{4,130},{6,194},{64,4},{66,68},{68,132},{70,196},{128... | collective-permute-start | bytes 442376 | tf_op jit(solution)/shard_map/ppermute | solution.py:182
  7.8 13.7 %collective-permute-start.2 = (bf16[72,1024]{1,0:T(8,128)(2,1)S(1)}, bf16[72,1024]{1,0:T(8,128)(2,1)S(1)}, u32[]{:S(2)}, u32[]{:S(2)}) collective-permute-start(bf16[72,1024]{1,0:T(8,128)(2,1)S(1)} %concatenate.42), channel_id=1, source_target_pairs={{0,4},{2,68},{4,132},{6,196},{64,6},{66,70},{68,134},{70,198},{128... | collective-permute-start | bytes 442376 | tf_op jit(solution)/shard_map/ppermute | solution.py:182
  12.2 9.3 %collective-permute-start.3 = (bf16[72,1024]{1,0:T(8,128)(2,1)S(1)}, bf16[72,1024]{1,0:T(8,128)(2,1)S(1)}, u32[]{:S(2)}, u32[]{:S(2)}) collective-permute-start(bf16[72,1024]{1,0:T(8,128)(2,1)S(1)} %concatenate.43), channel_id=1, source_target_pairs={{0,6},{2,70},{4,134},{6,198},{64,0},{66,64},{68,128},{70,192},{128... | collective-permute-start | bytes 442376 | tf_op jit(solution)/shard_map/ppermute | solution.py:182
  14.5 2.6 %collective-permute-start.6 = (f32[64,256]{1,0:T(8,128)S(1)}, f32[64,256]{1,0:T(8,128)S(1)}, u32[]{:S(2)}, u32[]{:S(2)}) collective-permute-start(f32[64,256]{1,0:T(8,128)S(1)} %select_bitcast_fusion), channel_id=1, source_target_pairs={{0,1},{1,0},{2,3},{3,2},{4,5},{5,4},{6,7},{7,6},{8,9},{9,8},{10,11... | collective-permute-start | bytes 196616 | tf_op jit(solution)/shard_map/ppermute | solution.py:168
  17.1 28.6 %collective-permute-start.5 = (bf16[256,1024]{1,0:T(8,128)(2,1)}, bf16[256,1024]{1,0:T(8,128)(2,1)S(1)}, u32[]{:S(2)}, u32[]{:S(2)}) collective-permute-start(bf16[256,1024]{1,0:T(8,128)(2,1)} %get-tuple-element.11), channel_id=1, source_target_pairs={{0,1},{1,0},{2,3},{3,2},{4,5},{5,4},{6,7},{7,6},{8,9},{9,8},{10,11... | collective-permute-start | bytes 1572872 | tf_op jit(solution)/shard_map/ppermute | solution.py:188
  18.1 8.2 %all-to-all-start = ((bf16[4,64,256]{2,1,0:T(8,128)(2,1)}), bf16[4,64,256]{2,1,0:T(8,128)(2,1)S(1)}, u32[]{:S(2)}, u32[]{:S(2)}) async-start(bf16[4,64,256]{2,1,0:T(8,128)(2,1)} %broadcast_in_dim.37), calls=%async_computation | async-start | bytes 262144 | tf_op jit(solution)/shard_map/all_to_all | solution.py:29
  21.5 0.7 copy-start.2
  21.6 5.5 %copy-start.3 = (bf16[72,1024]{1,0:T(8,128)(2,1)}, bf16[72,1024]{1,0:T(8,128)(2,1)S(1)}, u32[]{:S(2)}) copy-start(bf16[72,1024]{1,0:T(8,128)(2,1)S(1)} %collective-permute-done.3) | copy-start | bytes 442372
  23.0 22.3 %collective-permute-start.4 = (bf16[256,1024]{1,0:T(8,128)(2,1)}, bf16[256,1024]{1,0:T(8,128)(2,1)S(1)}, u32[]{:S(2)}, u32[]{:S(2)}) collective-permute-start(bf16[256,1024]{1,0:T(8,128)(2,1)} %pad_maximum_fusion.1), channel_id=1, source_target_pairs={{0,1},{1,0},{2,3},{3,2},{4,5},{5,4},{6,7},{7,6},{8,9},{9,8},{10,11... | collective-permute-start | bytes 1572872 | tf_op jit(solution)/shard_map/ppermute | solution.py:186
  27.1 18.2 %all-to-all-start.1 = ((bf16[8,64,256]{2,1,0:T(8,128)(2,1)}), bf16[8,64,256]{2,1,0:T(8,128)(2,1)S(1)}, u32[]{:S(2)}, u32[]{:S(2)}) async-start(bf16[8,64,256]{2,1,0:T(8,128)(2,1)} %broadcast_in_dim.38), calls=%async_computation.1 | async-start | bytes 524288 | tf_op jit(solution)/shard_map/all_to_all | solution.py:29
  178.1 30.0 %collective-permute-start.8 = (bf16[64,1024]{1,0:T(8,128)(2,1)S(1)}, bf16[64,1024]{1,0:T(8,128)(2,1)S(1)}, u32[]{:S(2)}, u32[]{:S(2)}) collective-permute-start(bf16[64,1024]{1,0:T(8,128)(2,1)S(1)} %slice.120), channel_id=1, source_target_pairs={{0,1},{1,0},{2,3},{3,2},{4,5},{5,4},{6,7},{7,6},{8,9},{9,8},{10,11... | collective-permute-start | bytes 393224 | tf_op jit(solution)/shard_map/ppermute | solution.py:223
  206.0 2.1 %collective-permute-start.7 = (f32[64,64]{1,0:T(8,128)S(1)}, f32[64,64]{1,0:T(8,128)S(1)}, u32[]{:S(2)}, u32[]{:S(2)}) collective-permute-start(f32[64,64]{1,0:T(8,128)S(1)} %inverse_of.1.inverse_ref), channel_id=1, source_target_pairs={{0,1},{1,0},{2,3},{3,2},{4,5},{5,4},{6,7},{7,6},{8,9},{9,8},{10,11... | collective-permute-start | bytes 49160 | tf_op jit(solution)/shard_map/ppermute | solution.py:226

commit v6 on v5

--- a/solution.py
+++ b/solution.py
@@ -171,22 +171,22 @@
         slope_1 = slopes[0:1]
 
         cut = width_row // n_x
-        high, middle, low = three_parts(slopes[1:2])
-        pad = jnp.zeros((8 - 3, width_in), BF16)
-        extra = jnp.concatenate([jnp.pad(p, ((0, 0), (0, width_in - width_row))) for p in (high, middle, low)] + [pad])
         y_at, x_at = lax.axis_index("y"), lax.axis_index("x")
-        moved = []
+        slope_piece = lax.dynamic_slice(slopes[1:2], (0, x_at * cut), (1, cut), allow_negative_indices=False)
+        spot = lax.rem(x_at - y_at + n_x, n_x)
+        at_turn = lax.broadcasted_iota(jnp.int32, (1, n_x, cut), 1) == spot
+        slope_spread = jnp.where(at_turn, slope_piece[:, None], 0.0).reshape(1, width_row)
+        slope_rows = jnp.concatenate([*three_parts(slope_spread), jnp.zeros((8 - 3, width_row), BF16)])
+
+        blocks = []
         for turn in range(n_x):
             start = lax.rem(y_at + turn, n_x) * cut
             piece = lax.dynamic_slice(w2_own, (start, 0), (cut, width_in), allow_negative_indices=False)
-            moved.append(lax.ppermute(jnp.concatenate([piece, extra]), ("y", "x"), turns[turn]))
-        here = jnp.concatenate([block[:cut] for block in moved])
-        sent = jnp.concatenate([block[cut : cut + 3].astype(F32).sum(0, keepdims=True)[:, :width_row] for block in moved])
-        slope_2 = lax.dynamic_slice(sent, (0, x_at * cut), (n_x, cut), allow_negative_indices=False).reshape(1, width_row)
-        there = lax.ppermute(here, "core", flip)
-        w2 = jnp.concatenate([jnp.where(first, here, there), jnp.where(first, there, here)], axis=1)
+            here = lax.ppermute(piece, ("y", "x"), turns[turn])
+            there = lax.ppermute(here, "core", flip)
+            blocks.append(jnp.concatenate([jnp.where(first, here, there), jnp.where(first, there, here)], axis=1))
         w1_other = lax.ppermute(w1_own, "core", flip)
-        w2, slope_2, w1_other = lax.optimization_barrier((w2, slope_2, w1_other))
+        w2, w1_other = lax.optimization_barrier((jnp.concatenate(blocks), w1_other))
 
         image = None
         for iteration in range(ITERS):
@@ -202,8 +202,13 @@
                 forward = normalized_forward(arrived, slope_1, width_row)
             spread = to_all(forward, "z", n_z)
             spread = jnp.moveaxis(spread, 0, 1).reshape(rank, n_z * width_row)
-            partial_out = dot_t(spread, w2)
-            arrived = to_all(partial_out.astype(BF16), "y", n_y)
+            partial_out = dot_t(spread, w2).astype(BF16)
+            if iteration == 0:
+                arrived = to_all(jnp.concatenate([partial_out, slope_rows]), "y", n_y)
+                slope_2 = total(arrived[:, rank:]).sum(axis=0, keepdims=True)
+                arrived = arrived[:, :rank]
+            else:
+                arrived = to_all(partial_out, "y", n_y)
             forward = (slope_2 * total(arrived)).astype(BF16)
             weighted = (slope_2 * forward.astype(F32)).astype(BF16)
             partial_in = dot_n(weighted, w2).astype(BF16)

time: 210 us -> 211 us (level)
  transfers between devices with their start and end apart: 11 -> 14, of which waited for: 4 -> 3; matrix products, arithmetic and copies ran while one was open for 2% -> 3% of each run, Pallas kernels for 1% -> 1%
where the time goes in v6:
time: 211 us; the launch traced here: 210 us
  blocking collectives  134 us (64%)
  starting transfers between devices  45.8 us (22%)
  waiting for transfers between devices  11.6 us (5%)
  local copies, waits for them, and re-layouts  6.1 us (3%)
  Pallas kernels  5.57 us (3%)
  matrix products  3.78 us (2%)
  other arithmetic  2.85 us (1%)
    all_to_all x13, blocking collectives, exchange(): return lax.all_to_all(tiles, axis, split_axis=0, concat_axis=0, tiled=True)  134 us
    ppermute x1, starting transfers between devices, on_device(): there = lax.ppermute(image[:, width_in:], 'core', flip)  18.9 us
    all_to_all x2, starting transfers between devices, exchange(): return lax.all_to_all(tiles, axis, split_axis=0, concat_axis=0, tiled=True)  11.5 us
    ppermute x4, starting transfers between devices, on_device(): here = lax.ppermute(piece, ('y', 'x'), turns[turn])  11.4 us
    all_to_all x2, waiting for transfers between devices, exchange(): return lax.all_to_all(tiles, axis, split_axis=0, concat_axis=0, tiled=True)  10.7 us
  transfers between devices with their start and end apart: 14, of which 3 were waited for; matrix products, arithmetic and copies ran while one was open for 3% of the time, Pallas kernels for 1%

profile of v6, /device:TPU:1, one launch (start us, length us, event | category | flops | bytes accessed | tf_op | source)
XLA Modules:
  0.0 209.7 jit_solution(7524586516426634580)
XLA Ops:
  0.0 1.3 slice_bitcast_fusion
  1.3 0.0 copy-start.3
  1.3 0.7 dynamic-slice_bitcast_fusion.3
  2.1 0.7 collective-permute-start.1
  2.7 4.6 %collective-permute-start.3 = (bf16[64,1024]{1,0:T(8,128)(2,1)S(1)}, bf16[64,1024]{1,0:T(8,128)(2,1)S(1)}, u32[]{:S(2)}, u32[]{:S(2)}) collective-permute-start(bf16[64,1024]{1,0:T(8,128)(2,1)S(1)} %get-tuple-element.14), channel_id=1, source_target_pairs={{0,2},{2,66},{4,130},{6,194},{64,4},{66,68},{68,132},{70,196},{128... | collective-permute-start | bytes 393224 | tf_op jit(solution)/shard_map/ppermute | solution.py:185
  7.3 4.2 %collective-permute-start.5 = (bf16[64,1024]{1,0:T(8,128)(2,1)}, bf16[64,1024]{1,0:T(8,128)(2,1)S(1)}, u32[]{:S(2)}, u32[]{:S(2)}) collective-permute-start(bf16[64,1024]{1,0:T(8,128)(2,1)} %get-tuple-element.13), channel_id=1, source_target_pairs={{0,4},{2,68},{4,132},{6,196},{64,6},{66,70},{68,134},{70,198},{128... | collective-permute-start | bytes 393224 | tf_op jit(solution)/shard_map/ppermute | solution.py:185
  11.6 1.8 collective-permute-start.7
  13.4 0.3 fusion.1
  13.8 1.7 collective-permute-start
  15.5 0.1 iota.9
  15.6 0.7 iota.10
  16.3 0.1 fusion.16
  16.3 0.6 broadcast_in_dim.44
  17.0 0.0 collective-permute-start.9
  17.0 0.7 broadcast_in_dim.40
  17.7 3.3 %all-to-all-start = ((bf16[4,64,256]{2,1,0:T(8,128)(2,1)}), bf16[4,64,256]{2,1,0:T(8,128)(2,1)S(1)}, u32[]{:S(2)}, u32[]{:S(2)}) async-start(bf16[4,64,256]{2,1,0:T(8,128)(2,1)} %broadcast_in_dim.40), calls=%async_computation | async-start | bytes 262144 | tf_op jit(solution)/shard_map/all_to_all | solution.py:29
  21.0 1.2 fusion.15
  22.2 0.5 collective-permute-start.2
  22.7 0.1 collective-permute-start.4
  22.8 0.4 collective-permute-start.6
  23.2 0.1 collective-permute-start.8
  23.3 2.5 %all-to-all-done = bf16[4,64,256]{2,1,0:T(8,128)(2,1)S(1)} async-done(((bf16[4,64,256]{2,1,0:T(8,128)(2,1)}), bf16[4,64,256]{2,1,0:T(8,128)(2,1)S(1)}, u32[]{:S(2)}, u32[]{:S(2)}) %all-to-all-start) | async-done | bytes 131104 | tf_op jit(solution)/shard_map/all_to_all | solution.py:29
  25.9 0.7 broadcast_in_dim.41
  26.6 8.2 %all-to-all-start.1 = ((bf16[8,64,256]{2,1,0:T(8,128)(2,1)}), bf16[8,64,256]{2,1,0:T(8,128)(2,1)}, u32[]{:S(2)}, u32[]{:S(2)}) async-start(bf16[8,64,256]{2,1,0:T(8,128)(2,1)} %broadcast_in_dim.41), calls=%async_computation.1 | async-start | bytes 524288 | tf_op jit(solution)/shard_map/all_to_all | solution.py:29
  34.9 0.9 broadcast_select_fusion.3
  35.8 0.1 maximum_maximum_fusion
  35.9 8.2 %all-to-all-done.1 = bf16[8,64,256]{2,1,0:T(8,128)(2,1)} async-done(((bf16[8,64,256]{2,1,0:T(8,128)(2,1)}), bf16[8,64,256]{2,1,0:T(8,128)(2,1)}, u32[]{:S(2)}, u32[]{:S(2)}) %all-to-all-start.1) | async-done | bytes 262176 | tf_op jit(solution)/shard_map/all_to_all | solution.py:29
  44.1 1.0 copy.14
  45.1 0.4 convolution_convert_fusion.7
  45.6 7.8 %all_to_all.75 = bf16[4,72,256]{2,1,0:T(8,128)(2,1)S(1)} all-to-all(bf16[4,72,256]{2,1,0:T(8,128)(2,1)S(1)} %broadcast_in_dim.47), channel_id=1, replica_groups=mesh['y'=4,'z'=8,'x'=4,'core'=2] {'y'}, dimensions={0} | all-to-all | bytes 294912 | tf_op jit(solution)/shard_map/all_to_all | solution.py:29
  53.5 0.3 convolution_convert_fusion.1
  53.8 12.5 %all_to_all.76 = bf16[8,64,256]{2,1,0:T(8,128)(2,1)S(1)} all-to-all(bf16[8,64,256]{2,1,0:T(8,128)(2,1)S(1)} %bitcast.87), channel_id=1, replica_groups=mesh['y'=4,'z'=8,'x'=4,'core'=2] {'z'}, dimensions={0} | all-to-all | bytes 524288 | tf_op jit(solution)/shard_map/all_to_all | solution.py:29
  66.3 7.2 %all_to_all.77 = bf16[4,64,256]{2,1,0:T(8,128)(2,1)S(1)} all-to-all(bf16[4,64,256]{2,1,0:T(8,128)(2,1)S(1)} %broadcast_in_dim.48), channel_id=1, replica_groups=mesh['y'=4,'z'=8,'x'=4,'core'=2] {'x'}, dimensions={0} | all-to-all | bytes 262144 | tf_op jit(solution)/shard_map/all_to_all | solution.py:29
  73.6 0.2 convolution_convert_fusion.5
  73.8 0.2 convolution_convert_fusion.4
  74.0 12.6 %all_to_all.78 = bf16[32,8,512]{2,1,0:T(8,128)(2,1)S(1)} all-to-all(bf16[32,8,512]{2,1,0:T(8,128)(2,1)S(1)} %bitcast.85), channel_id=1, replica_groups=mesh['y'=4,'z'=8,'x'=4,'core'=2] {'y','z'}, dimensions={0} | all-to-all | bytes 524288 | tf_op jit(solution)/shard_map/all_to_all | solution.py:29
  86.7 0.1 reduce_sum.117
  86.8 13.8 %all_to_all.79 = bf16[32,8,512]{2,1,0:T(8,128)(2,1)S(1)} all-to-all(bf16[32,8,512]{2,1,0:T(8,128)(2,1)S(1)} %broadcast_in_dim.49), channel_id=1, replica_groups=mesh['y'=4,'z'=8,'x'=4,'core'=2] {'y','z'}, dimensions={0} | all-to-all | bytes 524288 | tf_op jit(solution)/shard_map/all_to_all | solution.py:29
  100.6 0.3 fusion.8
  100.9 0.2 fusion.6
  101.1 0.3 fusion
  101.3 0.2 reduce-precision_convert_fusion.1
  101.5 0.1 pad_maximum_fusion.2
  101.6 7.7 %all_to_all.80.arrived_ref = bf16[4,64,384]{2,1,0:T(8,128)(2,1)S(1)} all-to-all(bf16[4,64,384]{2,1,0:T(8,128)(2,1)S(1)} %broadcast_in_dim.50), channel_id=1, replica_groups=mesh['y'=4,'z'=8,'x'=4,'core'=2] {'x'}, dimensions={0} | all-to-all | bytes 393216 | tf_op jit(solution)/shard_map/all_to_all | solution.py:29
  109.3 2.2 %normalized_forward.1 = bf16[64,256]{1,0:T(8,128)(2,1)S(1)} custom-call(bf16[4,64,384]{2,1,0:T(8,128)(2,1)S(1)} %all_to_all.80.arrived_ref, f32[1,256]{1,0:T(1,128)S(1)} %get-tuple-element.27.slope_ref), custom_call_target="tpu_custom_call" | custom-call | tf_op jit(solution)/shard_map/normalized_forward/pallas_call | solution.py:112
  111.6 12.4 %all_to_all.81 = bf16[8,64,256]{2,1,0:T(8,128)(2,1)S(1)} all-to-all(bf16[8,64,256]{2,1,0:T(8,128)(2,1)S(1)} %broadcast_in_dim.51), channel_id=1, replica_groups=mesh['y'=4,'z'=8,'x'=4,'core'=2] {'z'}, dimensions={0} | all-to-all | bytes 524288 | tf_op jit(solution)/shard_map/all_to_all | solution.py:29
  123.9 0.4 convolution_convert_fusion.6
  124.4 7.3 %all_to_all.82 = bf16[4,64,256]{2,1,0:T(8,128)(2,1)S(1)} all-to-all(bf16[4,64,256]{2,1,0:T(8,128)(2,1)S(1)} %broadcast_in_dim.52), channel_id=1, replica_groups=mesh['y'=4,'z'=8,'x'=4,'core'=2] {'y'}, dimensions={0} | all-to-all | bytes 262144 | tf_op jit(solution)/shard_map/all_to_all | solution.py:29
  131.8 0.3 convolution_convert_fusion
  132.1 11.7 %all_to_all.83 = bf16[8,64,256]{2,1,0:T(8,128)(2,1)S(1)} all-to-all(bf16[8,64,256]{2,1,0:T(8,128)(2,1)S(1)} %bitcast.89), channel_id=1, replica_groups=mesh['y'=4,'z'=8,'x'=4,'core'=2] {'z'}, dimensions={0} | all-to-all | bytes 524288 | tf_op jit(solution)/shard_map/all_to_all | solution.py:29
  143.9 7.2 %all_to_all.84 = bf16[4,64,256]{2,1,0:T(8,128)(2,1)S(1)} all-to-all(bf16[4,64,256]{2,1,0:T(8,128)(2,1)S(1)} %broadcast_in_dim.53), channel_id=1, replica_groups=mesh['y'=4,'z'=8,'x'=4,'core'=2] {'x'}, dimensions={0} | all-to-all | bytes 262144 | tf_op jit(solution)/shard_map/all_to_all | solution.py:29
  151.1 0.2 convolution_convert_fusion.3
  151.3 0.2 convolution_convert_fusion.2
  151.6 12.6 %all_to_all.85 = bf16[32,8,512]{2,1,0:T(8,128)(2,1)S(1)} all-to-all(bf16[32,8,512]{2,1,0:T(8,128)(2,1)S(1)} %bitcast.86), channel_id=1, replica_groups=mesh['y'=4,'z'=8,'x'=4,'core'=2] {'y','z'}, dimensions={0} | all-to-all | bytes 524288 | tf_op jit(solution)/shard_map/all_to_all | solution.py:29
  164.2 0.1 reduce_sum.121
  164.3 13.9 %all_to_all.86 = bf16[32,8,512]{2,1,0:T(8,128)(2,1)S(1)} all-to-all(bf16[32,8,512]{2,1,0:T(8,128)(2,1)S(1)} %broadcast_in_dim.54), channel_id=1, replica_groups=mesh['y'=4,'z'=8,'x'=4,'core'=2] {'y','z'}, dimensions={0} | all-to-all | bytes 524288 | tf_op jit(solution)/shard_map/all_to_all | solution.py:29
  178.2 0.2 reduce-precision_convert_fusion
  178.4 18.9 %collective-permute-start.11 = (bf16[64,1024]{1,0:T(8,128)(2,1)S(1)}, bf16[64,1024]{1,0:T(8,128)(2,1)S(1)}, u32[]{:S(2)}, u32[]{:S(2)}) collective-permute-start(bf16[64,1024]{1,0:T(8,128)(2,1)S(1)} %slice.67), channel_id=1, source_target_pairs={{0,1},{1,0},{2,3},{3,2},{4,5},{5,4},{6,7},{7,6},{8,9},{9,8},{10,11... | collective-permute-start | bytes 393224 | tf_op jit(solution)/shard_map/ppermute | solution.py:228
  197.3 0.1 pad_maximum_fusion.3
  197.4 6.9 %all_to_all.87.arrived_ref = bf16[4,64,128]{2,1,0:T(8,128)(2,1)S(1)} all-to-all(bf16[4,64,128]{2,1,0:T(8,128)(2,1)S(1)} %broadcast_in_dim.102), channel_id=1, replica_groups=mesh['y'=4,'z'=8,'x'=4,'core'=2] {'x'}, dimensions={0} | all-to-all | bytes 131072 | tf_op jit(solution)/shard_map/all_to_all | solution.py:29
  204.2 2.0 inverse_of.1.inverse_ref
  206.3 1.2 collective-permute-start.10
  207.5 0.9 collective-permute-done.10.inverse_there_ref
  208.4 1.4 normalized_panels.1
  (53 shorter events, 0.7 us)
Async XLA Ops:
  0.0 13.4 %copy-start = (bf16[2,64,1024]{2,1,0:T(8,128)(2,1)S(1)}, bf16[2,64,1024]{2,1,0:T(8,128)(2,1)}, u32[]{:S(2)}) copy-start(bf16[2,64,1024]{2,1,0:T(8,128)(2,1)} %param.5) | copy-start | bytes 786436
  1.3 12.1 %copy-start.1 = (bf16[2,256,1024]{2,1,0:T(8,128)(2,1)S(1)}, bf16[2,256,1024]{2,1,0:T(8,128)(2,1)}, u32[]{:S(2)}) copy-start(bf16[2,256,1024]{2,1,0:T(8,128)(2,1)} %param.3) | copy-start | bytes 3145732
  1.3 14.2 %copy-start.3 = (f32[2,2,256]{2,1,0:T(2,128)S(1)}, f32[2,2,256]{2,1,0:T(2,128)}, u32[]{:S(2)}) copy-start(f32[2,2,256]{2,1,0:T(2,128)} %param.4) | copy-start | bytes 12292
  2.1 20.2 %collective-permute-start.1 = (bf16[64,1024]{1,0:T(8,128)(2,1)S(1)}, bf16[64,1024]{1,0:T(8,128)(2,1)S(1)}, u32[]{:S(2)}, u32[]{:S(2)}) collective-permute-start(bf16[64,1024]{1,0:T(8,128)(2,1)S(1)} %get-tuple-element.11), channel_id=1, source_target_pairs={{0,0},{2,64},{4,128},{6,192},{64,2},{66,66},{68,130},{70,194},{128... | collective-permute-start | bytes 393224 | tf_op jit(solution)/shard_map/ppermute | solution.py:185
  2.7 20.0 %collective-permute-start.3 = (bf16[64,1024]{1,0:T(8,128)(2,1)S(1)}, bf16[64,1024]{1,0:T(8,128)(2,1)S(1)}, u32[]{:S(2)}, u32[]{:S(2)}) collective-permute-start(bf16[64,1024]{1,0:T(8,128)(2,1)S(1)} %get-tuple-element.14), channel_id=1, source_target_pairs={{0,2},{2,66},{4,130},{6,194},{64,4},{66,68},{68,132},{70,196},{128... | collective-permute-start | bytes 393224 | tf_op jit(solution)/shard_map/ppermute | solution.py:185
  7.3 15.5 %collective-permute-start.5 = (bf16[64,1024]{1,0:T(8,128)(2,1)}, bf16[64,1024]{1,0:T(8,128)(2,1)S(1)}, u32[]{:S(2)}, u32[]{:S(2)}) collective-permute-start(bf16[64,1024]{1,0:T(8,128)(2,1)} %get-tuple-element.13), channel_id=1, source_target_pairs={{0,4},{2,68},{4,132},{6,196},{64,6},{66,70},{68,134},{70,198},{128... | collective-permute-start | bytes 393224 | tf_op jit(solution)/shard_map/ppermute | solution.py:185
  11.6 11.7 %collective-permute-start.7 = (bf16[64,1024]{1,0:T(8,128)(2,1)S(1)}, bf16[64,1024]{1,0:T(8,128)(2,1)S(1)}, u32[]{:S(2)}, u32[]{:S(2)}) collective-permute-start(bf16[64,1024]{1,0:T(8,128)(2,1)S(1)} %get-tuple-element.12), channel_id=1, source_target_pairs={{0,6},{2,70},{4,134},{6,198},{64,0},{66,64},{68,128},{70,192},{128... | collective-permute-start | bytes 393224 | tf_op jit(solution)/shard_map/ppermute | solution.py:185
  13.8 3.2 %collective-permute-start = (f32[64,256]{1,0:T(8,128)S(1)}, f32[64,256]{1,0:T(8,128)S(1)}, u32[]{:S(2)}, u32[]{:S(2)}) collective-permute-start(f32[64,256]{1,0:T(8,128)S(1)} %select_bitcast_fusion), channel_id=1, source_target_pairs={{0,1},{1,0},{2,3},{3,2},{4,5},{5,4},{6,7},{7,6},{8,9},{9,8},{10,11... | collective-permute-start | bytes 196616 | tf_op jit(solution)/shard_map/ppermute | solution.py:168
  17.0 18.9 %collective-permute-start.9 = (bf16[256,1024]{1,0:T(8,128)(2,1)S(1)}, bf16[256,1024]{1,0:T(8,128)(2,1)S(1)}, u32[]{:S(2)}, u32[]{:S(2)}) collective-permute-start(bf16[256,1024]{1,0:T(8,128)(2,1)S(1)} %get-tuple-element.9), channel_id=1, source_target_pairs={{0,1},{1,0},{2,3},{3,2},{4,5},{5,4},{6,7},{7,6},{8,9},{9,8},{10,11... | collective-permute-start | bytes 1572872 | tf_op jit(solution)/shard_map/ppermute | solution.py:188
  17.7 8.1 %all-to-all-start = ((bf16[4,64,256]{2,1,0:T(8,128)(2,1)}), bf16[4,64,256]{2,1,0:T(8,128)(2,1)S(1)}, u32[]{:S(2)}, u32[]{:S(2)}) async-start(bf16[4,64,256]{2,1,0:T(8,128)(2,1)} %broadcast_in_dim.40), calls=%async_computation | async-start | bytes 262144 | tf_op jit(solution)/shard_map/all_to_all | solution.py:29
  22.2 12.5 %collective-permute-start.2 = (bf16[64,1024]{1,0:T(8,128)(2,1)S(1)}, bf16[64,1024]{1,0:T(8,128)(2,1)S(1)}, u32[]{:S(2)}, u32[]{:S(2)}) collective-permute-start(bf16[64,1024]{1,0:T(8,128)(2,1)S(1)} %collective-permute-done.1), channel_id=1, source_target_pairs={{0,1},{1,0},{2,3},{3,2},{4,5},{5,4},{6,7},{7,6},{8,9},{9,8},{10,11... | collective-permute-start | bytes 393224 | tf_op jit(solution)/shard_map/ppermute | solution.py:186
  22.7 12.1 %collective-permute-start.4 = (bf16[64,1024]{1,0:T(8,128)(2,1)S(1)}, bf16[64,1024]{1,0:T(8,128)(2,1)S(1)}, u32[]{:S(2)}, u32[]{:S(2)}) collective-permute-start(bf16[64,1024]{1,0:T(8,128)(2,1)S(1)} %collective-permute-done.3), channel_id=1, source_target_pairs={{0,1},{1,0},{2,3},{3,2},{4,5},{5,4},{6,7},{7,6},{8,9},{9,8},{10,11... | collective-permute-start | bytes 393224 | tf_op jit(solution)/shard_map/ppermute | solution.py:186
  22.8 12.0 %collective-permute-start.6 = (bf16[64,1024]{1,0:T(8,128)(2,1)S(1)}, bf16[64,1024]{1,0:T(8,128)(2,1)}, u32[]{:S(2)}, u32[]{:S(2)}) collective-permute-start(bf16[64,1024]{1,0:T(8,128)(2,1)S(1)} %collective-permute-done.5), channel_id=1, source_target_pairs={{0,1},{1,0},{2,3},{3,2},{4,5},{5,4},{6,7},{7,6},{8,9},{9,8},{10,11... | collective-permute-start | bytes 393224 | tf_op jit(solution)/shard_map/ppermute | solution.py:186
  23.2 12.5 %collective-permute-start.8 = (bf16[64,1024]{1,0:T(8,128)(2,1)S(1)}, bf16[64,1024]{1,0:T(8,128)(2,1)S(1)}, u32[]{:S(2)}, u32[]{:S(2)}) collective-permute-start(bf16[64,1024]{1,0:T(8,128)(2,1)S(1)} %collective-permute-done.7), channel_id=1, source_target_pairs={{0,1},{1,0},{2,3},{3,2},{4,5},{5,4},{6,7},{7,6},{8,9},{9,8},{10,11... | collective-permute-start | bytes 393224 | tf_op jit(solution)/shard_map/ppermute | solution.py:186
  26.6 17.6 %all-to-all-start.1 = ((bf16[8,64,256]{2,1,0:T(8,128)(2,1)}), bf16[8,64,256]{2,1,0:T(8,128)(2,1)}, u32[]{:S(2)}, u32[]{:S(2)}) async-start(bf16[8,64,256]{2,1,0:T(8,128)(2,1)} %broadcast_in_dim.41), calls=%async_computation.1 | async-start | bytes 524288 | tf_op jit(solution)/shard_map/all_to_all | solution.py:29
  35.9 9.7 %copy-start.2 = (bf16[1,256]{1,0:T(2,128)(2,1)S(1)}, bf16[1,256]{1,0:T(2,128)(2,1)}, u32[]{:S(2)}) copy-start(bf16[1,256]{1,0:T(2,128)(2,1)} %get-tuple-element.32) | copy-start | bytes 1540
  178.4 30.0 %collective-permute-start.11 = (bf16[64,1024]{1,0:T(8,128)(2,1)S(1)}, bf16[64,1024]{1,0:T(8,128)(2,1)S(1)}, u32[]{:S(2)}, u32[]{:S(2)}) collective-permute-start(bf16[64,1024]{1,0:T(8,128)(2,1)S(1)} %slice.67), channel_id=1, source_target_pairs={{0,1},{1,0},{2,3},{3,2},{4,5},{5,4},{6,7},{7,6},{8,9},{9,8},{10,11... | collective-permute-start | bytes 393224 | tf_op jit(solution)/shard_map/ppermute | solution.py:228
  206.3 2.1 collective-permute-start.10

commit v7 on v6

--- a/solution.py
+++ b/solution.py
@@ -149,9 +149,15 @@
 
 
 def make(n_x, n_y, n_z):
+    share = n_x // 2
     turns = [
-        [(i * n_x + j, j * n_x + (i + turn) % n_x) for i in range(n_y) for j in range(n_x)]
-        for turn in range(n_x)
+        [
+            ((i * n_x + j) * 2 + c, (j * n_x + (i + share * c + e) % n_x) * 2 + c)
+            for i in range(n_y)
+            for j in range(n_x)
+            for c in range(2)
+        ]
+        for e in range(share)
     ]
     flip = [(0, 1), (1, 0)]
 
@@ -165,7 +171,8 @@
         partial_out = jnp.einsum("bki,oi->bko", panel, w1_own, preferred_element_type=F32)
         mine = jnp.where(first, partial_out[0], partial_out[1])
         theirs = jnp.where(first, partial_out[1], partial_out[0])
-        summed_out = mine + lax.ppermute(theirs, "core", flip)
+        traded = lax.ppermute(theirs, "core", flip)
+        summed_out = mine + traded
 
         slopes = 1.0 - jnp.tanh(jnp.where(first, preact[0], preact[1])) ** 2
         slope_1 = slopes[0:1]
@@ -178,13 +185,20 @@
         slope_spread = jnp.where(at_turn, slope_piece[:, None], 0.0).reshape(1, width_row)
         slope_rows = jnp.concatenate([*three_parts(slope_spread), jnp.zeros((8 - 3, width_row), BF16)])
 
-        blocks = []
-        for turn in range(n_x):
+        def piece(turn):
             start = lax.rem(y_at + turn, n_x) * cut
-            piece = lax.dynamic_slice(w2_own, (start, 0), (cut, width_in), allow_negative_indices=False)
-            here = lax.ppermute(piece, ("y", "x"), turns[turn])
-            there = lax.ppermute(here, "core", flip)
-            blocks.append(jnp.concatenate([jnp.where(first, here, there), jnp.where(first, there, here)], axis=1))
+            return lax.dynamic_slice(w2_own, (start, 0), (cut, width_in), allow_negative_indices=False)
+
+        kept = jnp.concatenate([piece(core * share + e) for e in range(share)])
+        got = lax.ppermute(jnp.concatenate([piece((1 - core) * share + e) for e in range(share)]), "core", flip)
+        rows = jnp.concatenate([jnp.where(first, kept, got), jnp.where(first, got, kept)], axis=1)
+        rows = [rows[e * cut : (e + 1) * cut] for e in range(share)]
+        here = []
+        for e in range(share):
+            here.append(lax.ppermute(rows[e], ("y", "x", "core"), turns[e]))
+        there = [lax.ppermute(block, "core", flip) for block in here]
+        blocks = [jnp.where(first, h, t) for h, t in zip(here, there)]
+        blocks += [jnp.where(first, t, h) for h, t in zip(here, there)]
         w1_other = lax.ppermute(w1_own, "core", flip)
         w2, w1_other = lax.optimization_barrier((jnp.concatenate(blocks), w1_other))
 

time: 211 us -> 215 us (1.019)
  blocking collectives: 134 us -> 144 us
  starting transfers between devices: 45.8 us -> 40.2 us
  local copies, waits for them, and re-layouts: 6.1 us -> 3.34 us
    all_to_all x13, blocking collectives: 134 us -> 144 us  [exchange(): return lax.all_to_all(tiles, axis, split_axis=0, concat_axis=0, tiled=True)]
    ppermute x9 -> x6, waiting for transfers between devices: 0.02 us -> 7.4 us  [the longest x2 5.79 us: on_device(): here.append(lax.ppermute(rows[e], ('y', 'x', 'core'), turns[e]))]
    all_to_all x2, waiting for transfers between devices: 10.7 us -> 4.8 us  [exchange(): return lax.all_to_all(tiles, axis, split_axis=0, concat_axis=0, tiled=True)]
    ppermute x1, starting transfers between devices: 18.9 us -> 14.7 us  [on_device(): there = lax.ppermute(image[:, width_in:], 'core', flip)]
    ppermute x9 -> x6, starting transfers between devices: 14.2 us -> 12.8 us  [the longest x2 8.44 us: on_device(): here.append(lax.ppermute(rows[e], ('y', 'x', 'core'), turns[e]))]
  transfers between devices with their start and end apart: 14 -> 11, of which waited for: 3 -> 5; matrix products, arithmetic and copies ran while one was open for 3% -> 2% of each run, Pallas kernels for 1% -> 1%
where the time goes in v7:
time: 215 us; the launch traced here: 214 us
  blocking collectives  144 us (67%)
  starting transfers between devices  40.2 us (19%)
  waiting for transfers between devices  13.1 us (6%)
  Pallas kernels  5.57 us (3%)
  matrix products  3.78 us (2%)
  other arithmetic  3.52 us (2%)
  local copies, waits for them, and re-layouts  3.34 us (2%)
    all_to_all x13, blocking collectives, exchange(): return lax.all_to_all(tiles, axis, split_axis=0, concat_axis=0, tiled=True)  144 us
    ppermute x1, starting transfers between devices, on_device(): there = lax.ppermute(image[:, width_in:], 'core', flip)  14.7 us
    all_to_all x2, starting transfers between devices, exchange(): return lax.all_to_all(tiles, axis, split_axis=0, concat_axis=0, tiled=True)  10.5 us
    ppermute x2, starting transfers between devices, on_device(): here.append(lax.ppermute(rows[e], ('y', 'x', 'core'), turns[e]))  8.44 us
    ppermute x2, waiting for transfers between devices, on_device(): here.append(lax.ppermute(rows[e], ('y', 'x', 'core'), turns[e]))  5.79 us
    all_to_all x2, waiting for transfers between devices, exchange(): return lax.all_to_all(tiles, axis, split_axis=0, concat_axis=0, tiled=True)  4.8 us
  transfers between devices with their start and end apart: 11, of which 5 were waited for; matrix products, arithmetic and copies ran while one was open for 2% of the time, Pallas kernels for 1%

profile of v7, /device:TPU:1, one launch (start us, length us, event | category | flops | bytes accessed | tf_op | source)
XLA Modules:
  0.0 214.1 jit_solution(10280465667473363837)
XLA Ops:
  0.0 1.3 slice_bitcast_fusion
  1.3 0.0 copy-start.1
  1.4 0.0 copy-start.2
  1.4 3.3 %collective-permute-start.1 = (bf16[128,1024]{1,0:T(8,128)(2,1)S(1)}, bf16[128,1024]{1,0:T(8,128)(2,1)S(1)}, u32[]{:S(2)}, u32[]{:S(2)}) collective-permute-start(bf16[128,1024]{1,0:T(8,128)(2,1)S(1)} %pad_maximum_fusion.3), channel_id=1, source_target_pairs={{0,1},{1,0},{2,3},{3,2},{4,5},{5,4},{6,7},{7,6},{8,9},{9,8},{10,11... | collective-permute-start | bytes 786440 | tf_op jit(solution)/shard_map/ppermute | solution.py:193
  4.7 0.3 fusion.1
  5.1 1.1 collective-permute-start
  6.2 0.9 collective-permute-done
  7.1 0.7 broadcast_in_dim.40
  7.8 3.3 %all-to-all-start = ((bf16[4,64,256]{2,1,0:T(8,128)(2,1)}), bf16[4,64,256]{2,1,0:T(8,128)(2,1)S(1)}, u32[]{:S(2)}, u32[]{:S(2)}) async-start(bf16[4,64,256]{2,1,0:T(8,128)(2,1)} %broadcast_in_dim.40), calls=%async_computation | async-start | bytes 262144 | tf_op jit(solution)/shard_map/all_to_all | solution.py:29
  11.1 4.8 %all-to-all-done = bf16[4,64,256]{2,1,0:T(8,128)(2,1)S(1)} async-done(((bf16[4,64,256]{2,1,0:T(8,128)(2,1)}), bf16[4,64,256]{2,1,0:T(8,128)(2,1)S(1)}, u32[]{:S(2)}, u32[]{:S(2)}) %all-to-all-start) | async-done | bytes 131104 | tf_op jit(solution)/shard_map/all_to_all | solution.py:29
  15.9 0.0 collective-permute-done.1
  15.9 0.1 broadcast_select_fusion.1
  16.0 0.7 fusion.4
  16.8 2.7 %collective-permute-start.2 = (bf16[64,2048]{1,0:T(8,128)(2,1)}, bf16[64,2048]{1,0:T(8,128)(2,1)S(1)}, u32[]{:S(2)}, u32[]{:S(2)}) collective-permute-start(bf16[64,2048]{1,0:T(8,128)(2,1)} %get-tuple-element.15), channel_id=1, source_target_pairs={{0,0},{1,5},{2,64},{3,69},{4,128},{5,133},{6,192},{7,197},{64,2},{... | collective-permute-start | bytes 786440 | tf_op jit(solution)/shard_map/ppermute | solution.py:198
  19.5 0.7 broadcast_in_dim.41
  20.2 7.2 %all-to-all-start.1 = ((bf16[8,64,256]{2,1,0:T(8,128)(2,1)}), bf16[8,64,256]{2,1,0:T(8,128)(2,1)S(1)}, u32[]{:S(2)}, u32[]{:S(2)}) async-start(bf16[8,64,256]{2,1,0:T(8,128)(2,1)} %broadcast_in_dim.41), calls=%async_computation.1 | async-start | bytes 524288 | tf_op jit(solution)/shard_map/all_to_all | solution.py:29
  27.4 0.9 collective-permute-start.6
  28.4 5.7 %collective-permute-start.4 = (bf16[64,2048]{1,0:T(8,128)(2,1)S(1)}, bf16[64,2048]{1,0:T(8,128)(2,1)}, u32[]{:S(2)}, u32[]{:S(2)}) collective-permute-start(bf16[64,2048]{1,0:T(8,128)(2,1)S(1)} %get-tuple-element.16), channel_id=1, source_target_pairs={{0,2},{1,7},{2,66},{3,71},{4,130},{5,135},{6,194},{7,199},{64,4},{... | collective-permute-start | bytes 786440 | tf_op jit(solution)/shard_map/ppermute | solution.py:198
  34.1 0.0 collective-permute-done.2
  34.1 0.1 fusion.17
  34.2 0.1 iota.9
  34.2 0.1 iota.10
  34.3 0.1 broadcast_in_dim.44
  34.4 5.8 %collective-permute-done.4 = bf16[64,2048]{1,0:T(8,128)(2,1)} collective-permute-done((bf16[64,2048]{1,0:T(8,128)(2,1)S(1)}, bf16[64,2048]{1,0:T(8,128)(2,1)}, u32[]{:S(2)}, u32[]{:S(2)}) %collective-permute-start.4) | collective-permute-done | bytes 262176 | tf_op jit(solution)/shard_map/ppermute | solution.py:198
  40.2 1.0 broadcast_select_fusion.5
  41.2 0.7 collective-permute-done.5
  42.0 1.0 broadcast_select_fusion.4
  43.0 0.1 pad_maximum_fusion
  43.1 0.4 convolution_convert_fusion.7
  43.6 9.1 %all_to_all.75 = bf16[4,72,256]{2,1,0:T(8,128)(2,1)S(1)} all-to-all(bf16[4,72,256]{2,1,0:T(8,128)(2,1)S(1)} %broadcast_in_dim.47), channel_id=1, replica_groups=mesh['y'=4,'z'=8,'x'=4,'core'=2] {'y'}, dimensions={0} | all-to-all | bytes 294912 | tf_op jit(solution)/shard_map/all_to_all | solution.py:29
  52.7 0.3 convolution_convert_fusion.1
  53.0 16.0 %all_to_all.76 = bf16[8,64,256]{2,1,0:T(8,128)(2,1)S(1)} all-to-all(bf16[8,64,256]{2,1,0:T(8,128)(2,1)S(1)} %bitcast.88), channel_id=1, replica_groups=mesh['y'=4,'z'=8,'x'=4,'core'=2] {'z'}, dimensions={0} | all-to-all | bytes 524288 | tf_op jit(solution)/shard_map/all_to_all | solution.py:29
  69.1 10.6 %all_to_all.77 = bf16[4,64,256]{2,1,0:T(8,128)(2,1)S(1)} all-to-all(bf16[4,64,256]{2,1,0:T(8,128)(2,1)S(1)} %broadcast_in_dim.48), channel_id=1, replica_groups=mesh['y'=4,'z'=8,'x'=4,'core'=2] {'x'}, dimensions={0} | all-to-all | bytes 262144 | tf_op jit(solution)/shard_map/all_to_all | solution.py:29
  79.7 0.2 convolution_convert_fusion.5
  79.9 0.2 convolution_convert_fusion.4
  80.2 14.2 %all_to_all.78 = bf16[32,8,512]{2,1,0:T(8,128)(2,1)S(1)} all-to-all(bf16[32,8,512]{2,1,0:T(8,128)(2,1)S(1)} %bitcast.86), channel_id=1, replica_groups=mesh['y'=4,'z'=8,'x'=4,'core'=2] {'y','z'}, dimensions={0} | all-to-all | bytes 524288 | tf_op jit(solution)/shard_map/all_to_all | solution.py:29
  94.3 0.1 reduce_sum.117
  94.4 13.8 %all_to_all.79 = bf16[32,8,512]{2,1,0:T(8,128)(2,1)S(1)} all-to-all(bf16[32,8,512]{2,1,0:T(8,128)(2,1)S(1)} %broadcast_in_dim.49), channel_id=1, replica_groups=mesh['y'=4,'z'=8,'x'=4,'core'=2] {'y','z'}, dimensions={0} | all-to-all | bytes 524288 | tf_op jit(solution)/shard_map/all_to_all | solution.py:29
  108.3 0.3 fusion.9
  108.5 0.2 fusion.7
  108.7 0.3 fusion
  109.0 0.2 reduce-precision_convert_fusion.1
  109.2 0.1 pad_maximum_fusion.6
  109.3 7.5 %all_to_all.80.arrived_ref = bf16[4,64,384]{2,1,0:T(8,128)(2,1)S(1)} all-to-all(bf16[4,64,384]{2,1,0:T(8,128)(2,1)S(1)} %broadcast_in_dim.50), channel_id=1, replica_groups=mesh['y'=4,'z'=8,'x'=4,'core'=2] {'x'}, dimensions={0} | all-to-all | bytes 393216 | tf_op jit(solution)/shard_map/all_to_all | solution.py:29
  116.8 2.2 %normalized_forward.1 = bf16[64,256]{1,0:T(8,128)(2,1)S(1)} custom-call(bf16[4,64,384]{2,1,0:T(8,128)(2,1)S(1)} %all_to_all.80.arrived_ref, f32[1,256]{1,0:T(1,128)S(1)} %get-tuple-element.27.slope_ref), custom_call_target="tpu_custom_call" | custom-call | tf_op jit(solution)/shard_map/normalized_forward/pallas_call | solution.py:112
  119.1 12.4 %all_to_all.81 = bf16[8,64,256]{2,1,0:T(8,128)(2,1)S(1)} all-to-all(bf16[8,64,256]{2,1,0:T(8,128)(2,1)S(1)} %broadcast_in_dim.51), channel_id=1, replica_groups=mesh['y'=4,'z'=8,'x'=4,'core'=2] {'z'}, dimensions={0} | all-to-all | bytes 524288 | tf_op jit(solution)/shard_map/all_to_all | solution.py:29
  131.5 0.4 convolution_convert_fusion.6
  132.0 7.3 %all_to_all.82 = bf16[4,64,256]{2,1,0:T(8,128)(2,1)S(1)} all-to-all(bf16[4,64,256]{2,1,0:T(8,128)(2,1)S(1)} %broadcast_in_dim.52), channel_id=1, replica_groups=mesh['y'=4,'z'=8,'x'=4,'core'=2] {'y'}, dimensions={0} | all-to-all | bytes 262144 | tf_op jit(solution)/shard_map/all_to_all | solution.py:29
  139.3 0.3 convolution_convert_fusion
  139.6 11.7 %all_to_all.83 = bf16[8,64,256]{2,1,0:T(8,128)(2,1)S(1)} all-to-all(bf16[8,64,256]{2,1,0:T(8,128)(2,1)S(1)} %bitcast.90), channel_id=1, replica_groups=mesh['y'=4,'z'=8,'x'=4,'core'=2] {'z'}, dimensions={0} | all-to-all | bytes 524288 | tf_op jit(solution)/shard_map/all_to_all | solution.py:29
  151.4 7.2 %all_to_all.84 = bf16[4,64,256]{2,1,0:T(8,128)(2,1)S(1)} all-to-all(bf16[4,64,256]{2,1,0:T(8,128)(2,1)S(1)} %broadcast_in_dim.53), channel_id=1, replica_groups=mesh['y'=4,'z'=8,'x'=4,'core'=2] {'x'}, dimensions={0} | all-to-all | bytes 262144 | tf_op jit(solution)/shard_map/all_to_all | solution.py:29
  158.7 0.2 convolution_convert_fusion.3
  158.9 0.2 convolution_convert_fusion.2
  159.1 12.6 %all_to_all.85 = bf16[32,8,512]{2,1,0:T(8,128)(2,1)S(1)} all-to-all(bf16[32,8,512]{2,1,0:T(8,128)(2,1)S(1)} %bitcast.87), channel_id=1, replica_groups=mesh['y'=4,'z'=8,'x'=4,'core'=2] {'y','z'}, dimensions={0} | all-to-all | bytes 524288 | tf_op jit(solution)/shard_map/all_to_all | solution.py:29
  171.8 0.1 reduce_sum.121
  171.8 14.9 %all_to_all.86 = bf16[32,8,512]{2,1,0:T(8,128)(2,1)S(1)} all-to-all(bf16[32,8,512]{2,1,0:T(8,128)(2,1)S(1)} %broadcast_in_dim.54), channel_id=1, replica_groups=mesh['y'=4,'z'=8,'x'=4,'core'=2] {'y','z'}, dimensions={0} | all-to-all | bytes 524288 | tf_op jit(solution)/shard_map/all_to_all | solution.py:29
  186.7 0.2 reduce-precision_convert_fusion
  187.0 14.7 %collective-permute-start.8 = (bf16[64,1024]{1,0:T(8,128)(2,1)S(1)}, bf16[64,1024]{1,0:T(8,128)(2,1)S(1)}, u32[]{:S(2)}, u32[]{:S(2)}) collective-permute-start(bf16[64,1024]{1,0:T(8,128)(2,1)S(1)} %slice.77), channel_id=1, source_target_pairs={{0,1},{1,0},{2,3},{3,2},{4,5},{5,4},{6,7},{7,6},{8,9},{9,8},{10,11... | collective-permute-start | bytes 393224 | tf_op jit(solution)/shard_map/ppermute | solution.py:242
  201.7 0.1 pad_maximum_fusion.7
  201.7 6.9 %all_to_all.87.arrived_ref = bf16[4,64,128]{2,1,0:T(8,128)(2,1)S(1)} all-to-all(bf16[4,64,128]{2,1,0:T(8,128)(2,1)S(1)} %broadcast_in_dim.102), channel_id=1, replica_groups=mesh['y'=4,'z'=8,'x'=4,'core'=2] {'x'}, dimensions={0} | all-to-all | bytes 131072 | tf_op jit(solution)/shard_map/all_to_all | solution.py:29
  208.6 2.0 inverse_of.1.inverse_ref
  210.6 1.2 collective-permute-start.7
  211.9 0.9 collective-permute-done.7.inverse_there_ref
  212.7 1.4 normalized_panels.1
  (46 shorter events, 0.7 us)
Async XLA Ops:
  0.0 4.7 %copy-start = (bf16[2,64,1024]{2,1,0:T(8,128)(2,1)S(1)}, bf16[2,64,1024]{2,1,0:T(8,128)(2,1)}, u32[]{:S(2)}) copy-start(bf16[2,64,1024]{2,1,0:T(8,128)(2,1)} %param.5) | copy-start | bytes 786436
  1.3 3.4 %copy-start.1 = (bf16[2,256,1024]{2,1,0:T(8,128)(2,1)S(1)}, bf16[2,256,1024]{2,1,0:T(8,128)(2,1)}, u32[]{:S(2)}) copy-start(bf16[2,256,1024]{2,1,0:T(8,128)(2,1)} %param.3) | copy-start | bytes 3145732
  1.4 4.8 %copy-start.2 = (f32[2,2,256]{2,1,0:T(2,128)S(1)}, f32[2,2,256]{2,1,0:T(2,128)}, u32[]{:S(2)}) copy-start(f32[2,2,256]{2,1,0:T(2,128)} %param.4) | copy-start | bytes 12292
  1.4 14.5 %collective-permute-start.1 = (bf16[128,1024]{1,0:T(8,128)(2,1)S(1)}, bf16[128,1024]{1,0:T(8,128)(2,1)S(1)}, u32[]{:S(2)}, u32[]{:S(2)}) collective-permute-start(bf16[128,1024]{1,0:T(8,128)(2,1)S(1)} %pad_maximum_fusion.3), channel_id=1, source_target_pairs={{0,1},{1,0},{2,3},{3,2},{4,5},{5,4},{6,7},{7,6},{8,9},{9,8},{10,11... | collective-permute-start | bytes 786440 | tf_op jit(solution)/shard_map/ppermute | solution.py:193
  5.1 2.0 collective-permute-start
  7.8 8.1 %all-to-all-start = ((bf16[4,64,256]{2,1,0:T(8,128)(2,1)}), bf16[4,64,256]{2,1,0:T(8,128)(2,1)S(1)}, u32[]{:S(2)}, u32[]{:S(2)}) async-start(bf16[4,64,256]{2,1,0:T(8,128)(2,1)} %broadcast_in_dim.40), calls=%async_computation | async-start | bytes 262144 | tf_op jit(solution)/shard_map/all_to_all | solution.py:29
  16.8 17.3 %collective-permute-start.2 = (bf16[64,2048]{1,0:T(8,128)(2,1)}, bf16[64,2048]{1,0:T(8,128)(2,1)S(1)}, u32[]{:S(2)}, u32[]{:S(2)}) collective-permute-start(bf16[64,2048]{1,0:T(8,128)(2,1)} %get-tuple-element.15), channel_id=1, source_target_pairs={{0,0},{1,5},{2,64},{3,69},{4,128},{5,133},{6,192},{7,197},{64,2},{... | collective-permute-start | bytes 786440 | tf_op jit(solution)/shard_map/ppermute | solution.py:198
  20.2 20.0 %all-to-all-start.1 = ((bf16[8,64,256]{2,1,0:T(8,128)(2,1)}), bf16[8,64,256]{2,1,0:T(8,128)(2,1)S(1)}, u32[]{:S(2)}, u32[]{:S(2)}) async-start(bf16[8,64,256]{2,1,0:T(8,128)(2,1)} %broadcast_in_dim.41), calls=%async_computation.1 | async-start | bytes 524288 | tf_op jit(solution)/shard_map/all_to_all | solution.py:29
  27.4 15.6 %collective-permute-start.6 = (bf16[256,1024]{1,0:T(8,128)(2,1)S(1)}, bf16[256,1024]{1,0:T(8,128)(2,1)S(1)}, u32[]{:S(2)}, u32[]{:S(2)}) collective-permute-start(bf16[256,1024]{1,0:T(8,128)(2,1)S(1)} %get-tuple-element.9), channel_id=1, source_target_pairs={{0,1},{1,0},{2,3},{3,2},{4,5},{5,4},{6,7},{7,6},{8,9},{9,8},{10,11... | collective-permute-start | bytes 1572872 | tf_op jit(solution)/shard_map/ppermute | solution.py:202
  28.4 11.8 %collective-permute-start.4 = (bf16[64,2048]{1,0:T(8,128)(2,1)S(1)}, bf16[64,2048]{1,0:T(8,128)(2,1)}, u32[]{:S(2)}, u32[]{:S(2)}) collective-permute-start(bf16[64,2048]{1,0:T(8,128)(2,1)S(1)} %get-tuple-element.16), channel_id=1, source_target_pairs={{0,2},{1,7},{2,66},{3,71},{4,130},{5,135},{6,194},{7,199},{64,4},{... | collective-permute-start | bytes 786440 | tf_op jit(solution)/shard_map/ppermute | solution.py:198
  34.1 6.2 %collective-permute-start.3 = (bf16[64,2048]{1,0:T(8,128)(2,1)S(1)}, bf16[64,2048]{1,0:T(8,128)(2,1)}, u32[]{:S(2)}, u32[]{:S(2)}) collective-permute-start(bf16[64,2048]{1,0:T(8,128)(2,1)S(1)} %collective-permute-done.2), channel_id=1, source_target_pairs={{0,1},{1,0},{2,3},{3,2},{4,5},{5,4},{6,7},{7,6},{8,9},{9,8},{10,11... | collective-permute-start | bytes 786440 | tf_op jit(solution)/shard_map/ppermute | solution.py:199
  40.2 1.7 collective-permute-start.5
  187.0 25.8 %collective-permute-start.8 = (bf16[64,1024]{1,0:T(8,128)(2,1)S(1)}, bf16[64,1024]{1,0:T(8,128)(2,1)S(1)}, u32[]{:S(2)}, u32[]{:S(2)}) collective-permute-start(bf16[64,1024]{1,0:T(8,128)(2,1)S(1)} %slice.77), channel_id=1, source_target_pairs={{0,1},{1,0},{2,3},{3,2},{4,5},{5,4},{6,7},{7,6},{8,9},{9,8},{10,11... | collective-permute-start | bytes 393224 | tf_op jit(solution)/shard_map/ppermute | solution.py:242
  210.6 2.1 collective-permute-start.7

commit v8 on v7

--- a/solution.py
+++ b/solution.py
@@ -37,36 +37,48 @@
     return jnp.sum(tiles.astype(F32), axis=0)
 
 
-def inverse_factor(gram):
-    n = gram.shape[0]
+def inverse_factors(grams):
+    n = grams[0].shape[0]
     count = n // 8
     rows = lax.broadcasted_iota(jnp.int32, (n, n), 0)
     cols = lax.broadcasted_iota(jnp.int32, (n, n), 1)
-    both = jnp.concatenate([(rows == cols).astype(F32), gram * (1.0 / WIDTH)], axis=1)
-    blocks = [both[8 * i : 8 * i + 8] for i in range(count)]
+    eye = (rows == cols).astype(F32)
     row_of = lax.broadcasted_iota(jnp.int32, (8, 2 * n), 0)
-    done = []
-    for k in range(count):
-        live = range(k, count)
-        columns = [
-            {i: jnp.broadcast_to(blocks[i][:, n + 8 * k + t : n + 8 * k + t + 1], (8, 2 * n)) for i in live}
+    many = []
+    for gram in grams:
+        both = jnp.concatenate([eye, gram * (1.0 / WIDTH)], axis=1)
+        many.append([both[8 * i : 8 * i + 8] for i in range(count)])
+
+    def columns_of(blocks, k):
+        return [
+            {i: jnp.broadcast_to(blocks[i][:, n + 8 * k + t : n + 8 * k + t + 1], (8, 2 * n)) for i in range(k, count)}
             for t in range(8)
         ]
-        scale = jnp.zeros((8, 2 * n), F32)
+
+    def step(blocks, columns, scale, k, t):
+        live = range(k, count)
+        inverse = 1.0 / columns[t][k][t : t + 1, :]
+        factors = {i: columns[t][i] * inverse for i in live}
+        factors[k] = jnp.where(row_of > t, factors[k], 0.0)
+        for u in range(t + 1, 8):
+            entry = columns[u][k][t : t + 1, :]
+            for i in live:
+                columns[u][i] = columns[u][i] - factors[i] * entry
+        pivot_row = blocks[k][t : t + 1, :]
+        for i in live:
+            blocks[i] = blocks[i] - factors[i] * pivot_row
+        return jnp.where(row_of == t, inverse, scale)
+
+    done = [[] for _ in many]
+    for k in range(count):
+        columns = [columns_of(blocks, k) for blocks in many]
+        scales = [jnp.zeros((8, 2 * n), F32) for _ in many]
         for t in range(8):
-            inverse = 1.0 / columns[t][k][t : t + 1, :]
-            scale = jnp.where(row_of == t, inverse, scale)
-            factors = {i: columns[t][i] * inverse for i in live}
-            factors[k] = jnp.where(row_of > t, factors[k], 0.0)
-            for u in range(t + 1, 8):
-                entry = columns[u][k][t : t + 1, :]
-                for i in live:
-                    columns[u][i] = columns[u][i] - factors[i] * entry
-            pivot_row = blocks[k][t : t + 1, :]
-            for i in live:
-                blocks[i] = blocks[i] - factors[i] * pivot_row
-        done.append(blocks[k] * jnp.sqrt(scale))
-    return jnp.concatenate(done, axis=0)[:, :n]
+            for g, blocks in enumerate(many):
+                scales[g] = step(blocks, columns[g], scales[g], k, t)
+        for g, blocks in enumerate(many):
+            done[g].append(blocks[k] * jnp.sqrt(scales[g]))
+    return [jnp.concatenate(d, axis=0)[:, :n] for d in done]
 
 
 def exact_dot(a, b):
@@ -83,27 +95,11 @@
     return summed[:, :rank] + summed[:, rank:]
 
 
-def inverse_of(arrived, start):
-    rank = arrived.shape[1]
-
-    def kernel(arrived_ref, out_ref):
-        out_ref[...] = inverse_factor(gram_of_parts(arrived_ref, start, rank))
-
-    return pl.pallas_call(
-        kernel,
-        in_specs=[WHOLE],
-        out_specs=WHOLE,
-        out_shape=pltpu.VMEM((rank, rank), F32),
-        cost_estimate=pl.CostEstimate(flops=60_000_000, bytes_accessed=200_000, transcendentals=0),
-        name="inverse_of",
-    )(on_chip(arrived))
-
-
 def normalized_forward(arrived, slope, width):
     count, rank, _ = arrived.shape
 
     def kernel(arrived_ref, slope_ref, out_ref):
-        inverse = inverse_factor(gram_of_parts(arrived_ref, width, rank))
+        (inverse,) = inverse_factors([gram_of_parts(arrived_ref, width, rank)])
         summed = arrived_ref[0, :, :width].astype(F32)
         for i in range(1, count):
             summed = summed + arrived_ref[i, :, :width].astype(F32)
@@ -118,23 +114,30 @@
     )(on_chip(arrived), on_chip(slope))
 
 
-def normalized_panels(core, inverse, inverse_there, image, there):
+def normalized_panels(core, arrived, image, there):
     rank, width = there.shape
 
-    def kernel(core_ref, inverse_ref, inverse_there_ref, image_ref, there_ref, out_ref):
+    def kernel(core_ref, arrived_ref, image_ref, there_ref, out_ref):
         here_at = core_ref[0]
-        here = exact_dot(inverse_ref[...], image_ref[:, :width].astype(F32))
+        inverses = []
+        for b in (here_at, 1 - here_at):
+            gram = arrived_ref[pl.ds(b, 1)][0].astype(F32)
+            for i in range(2, arrived_ref.shape[0], 2):
+                gram = gram + arrived_ref[pl.ds(i + b, 1)][0].astype(F32)
+            inverses.append(gram[:, :rank] + gram[:, rank:])
+        inverses = inverse_factors(inverses)
+        here = exact_dot(inverses[0], image_ref[:, :width].astype(F32))
         out_ref[pl.ds(here_at, 1)] = here[None]
-        away = exact_dot(inverse_there_ref[...], there_ref[...].astype(F32))
+        away = exact_dot(inverses[1], there_ref[...].astype(F32))
         out_ref[pl.ds(1 - here_at, 1)] = away[None]
 
     return pl.pallas_call(
         kernel,
-        in_specs=[pl.BlockSpec(memory_space=pltpu.SMEM)] + [WHOLE] * 4,
+        in_specs=[pl.BlockSpec(memory_space=pltpu.SMEM)] + [WHOLE] * 3,
         out_specs=WHOLE,
         out_shape=jax.ShapeDtypeStruct((2, rank, width), F32),
         name="normalized_panels",
-    )(core, on_chip(inverse), on_chip(inverse_there), on_chip(image), on_chip(there))
+    )(core, on_chip(arrived), on_chip(image), on_chip(there))
 
 
 def three_parts(x):
@@ -199,8 +202,9 @@
         there = [lax.ppermute(block, "core", flip) for block in here]
         blocks = [jnp.where(first, h, t) for h, t in zip(here, there)]
         blocks += [jnp.where(first, t, h) for h, t in zip(here, there)]
+        w2 = jnp.concatenate(blocks)
         w1_other = lax.ppermute(w1_own, "core", flip)
-        w2, w1_other = lax.optimization_barrier((jnp.concatenate(blocks), w1_other))
+        w1, w2 = lax.optimization_barrier((jnp.concatenate([w1_own, w1_other], axis=1), w2))
 
         image = None
         for iteration in range(ITERS):
@@ -208,10 +212,8 @@
                 arrived = to_all(summed_out.astype(BF16), "x", n_x)
                 forward = (slope_1 * total(arrived)).astype(BF16)
             else:
-                own, other = image[:, :width_in], image[:, width_in:]
-                partial_out = dot_t(own, w1_own) + dot_t(other, w1_other)
-                gram = dot_t(own, own) + dot_t(other, other)
-                message = jnp.concatenate([partial_out.astype(BF16), high_low(gram)], axis=1)
+                partial_out = dot_t(image, w1).astype(BF16)
+                message = jnp.concatenate([partial_out, high_low(dot_t(image, image))], axis=1)
                 arrived = to_all(message, "x", n_x)
                 forward = normalized_forward(arrived, slope_1, width_row)
             spread = to_all(forward, "z", n_z)
@@ -230,20 +232,18 @@
             summed = total(exchange(blocks, "z")).astype(BF16)
             cotangent = total(to_all(summed, "x", n_x)).astype(BF16)
             weighted = (slope_1 * cotangent.astype(F32)).astype(BF16)
-            partial_in = jnp.concatenate([dot_n(weighted, w1_own), dot_n(weighted, w1_other)], axis=1)
+            partial_in = dot_n(weighted, w1).astype(BF16)
             groups = rank // 8
             cuts = n_y * n_z // groups
             length = 2 * width_in // cuts
-            pieces = partial_in.astype(BF16).reshape(groups, 8, cuts, length)
+            pieces = partial_in.reshape(groups, 8, cuts, length)
             pieces = jnp.moveaxis(pieces, 2, 1).reshape(groups * cuts, 8, length)
             piece = total(exchange(pieces, ("y", "z"))).astype(BF16)
             image = to_all(piece, ("y", "z"), groups * cuts).reshape(groups, cuts, 8, length)
             image = jnp.moveaxis(image, 1, 2).reshape(rank, 2 * width_in)
         there = lax.ppermute(image[:, width_in:], "core", flip)
-        gram = dot_t(image, image)
-        inverse = inverse_of(to_all(high_low(gram), "x", n_x), 0)
-        inverse_there = lax.ppermute(inverse, "core", flip)
-        return normalized_panels(core.reshape(1).astype(jnp.int32), inverse, inverse_there, image, there)
+        arrived = to_all(high_low(dot_t(image, image)), ("x", "core"), 2 * n_x)
+        return normalized_panels(core.reshape(1).astype(jnp.int32), arrived, image, there)
 
     return on_device
 

time: 215 us -> 202 us (0.940)
  blocking collectives: 144 us -> 137 us
  starting transfers between devices: 40.2 us -> 37.8 us
    all_to_all x13, blocking collectives: 144 us -> 137 us  [exchange(): return lax.all_to_all(tiles, axis, split_axis=0, concat_axis=0, tiled=True)]
    all_to_all x2, waiting for transfers between devices: 4.8 us -> 10.6 us  [exchange(): return lax.all_to_all(tiles, axis, split_axis=0, concat_axis=0, tiled=True)]
    ppermute x2, waiting for transfers between devices: 5.79 us -> 0.01 us  [on_device(): here.append(lax.ppermute(rows[e], ('y', 'x', 'core'), turns[e]))]
    pallas_call x1, Pallas kernels: 1.35 us -> 3.86 us  [normalized_panels(): pl.pallas_call(kernel, in_specs=[pl.BlockSpec(memory_space=pltpu.SMEM)] +...]
  transfers between devices with their start and end apart: 11 -> 10, of which waited for: 5 -> 2; matrix products, arithmetic and copies ran while one was open for 2% -> 2% of each run, Pallas kernels for 1% -> 0%
where the time goes in v8:
time: 202 us; the launch traced here: 201 us
  blocking collectives  137 us (68%)
  starting transfers between devices  37.8 us (19%)
  waiting for transfers between devices  11.2 us (6%)
  Pallas kernels  6.06 us (3%)
  local copies, waits for them, and re-layouts  3.36 us (2%)
  matrix products  3.28 us (2%)
    all_to_all x13, blocking collectives, exchange(): return lax.all_to_all(tiles, axis, split_axis=0, concat_axis=0, tiled=True)  137 us
    ppermute x1, starting transfers between devices, on_device(): there = lax.ppermute(image[:, width_in:], 'core', flip)  14.6 us
    all_to_all x2, starting transfers between devices, exchange(): return lax.all_to_all(tiles, axis, split_axis=0, concat_axis=0, tiled=True)  11.5 us
    all_to_all x2, waiting for transfers between devices, exchange(): return lax.all_to_all(tiles, axis, split_axis=0, concat_axis=0, tiled=True)  10.6 us
    ppermute x2, starting transfers between devices, on_device(): here.append(lax.ppermute(rows[e], ('y', 'x', 'core'), turns[e]))  6.65 us
  transfers between devices with their start and end apart: 10, of which 2 were waited for; matrix products, arithmetic and copies ran while one was open for 2% of the time, Pallas kernels for 0%

profile of v8, /device:TPU:1, one launch (start us, length us, event | category | flops | bytes accessed | tf_op | source)
XLA Modules:
  0.0 200.9 jit_solution(16049718265747124003)
XLA Ops:
  0.0 0.0 copy-start
  0.0 1.3 fusion.13
  1.3 0.0 copy-start.1
  1.4 0.0 copy-start.2
  1.4 3.3 %collective-permute-start.2 = (bf16[128,1024]{1,0:T(8,128)(2,1)S(1)}, bf16[128,1024]{1,0:T(8,128)(2,1)S(1)}, u32[]{:S(2)}, u32[]{:S(2)}) collective-permute-start(bf16[128,1024]{1,0:T(8,128)(2,1)S(1)} %pad_maximum_fusion.4), channel_id=1, source_target_pairs={{0,1},{1,0},{2,3},{3,2},{4,5},{5,4},{6,7},{7,6},{8,9},{9,8},{10,11... | collective-permute-start | bytes 786440 | tf_op jit(solution)/shard_map/ppermute | solution.py:196
  4.7 0.1 collective-permute-start.1
  4.8 0.0 copy-done
  4.8 0.0 copy-done.1
  4.8 0.3 fusion
  5.2 1.0 collective-permute-start
  6.2 0.1 fusion.12
  6.3 0.1 iota.9
  6.4 0.1 iota.10
  6.5 0.1 broadcast_in_dim.44
  6.5 0.5 collective-permute-done
  7.1 0.7 broadcast_in_dim.40
  7.8 3.3 %all-to-all-start = ((bf16[4,64,256]{2,1,0:T(8,128)(2,1)}), bf16[4,64,256]{2,1,0:T(8,128)(2,1)S(1)}, u32[]{:S(2)}, u32[]{:S(2)}) async-start(bf16[4,64,256]{2,1,0:T(8,128)(2,1)} %broadcast_in_dim.40), calls=%async_computation | async-start | bytes 262144 | tf_op jit(solution)/shard_map/all_to_all | solution.py:29
  11.1 0.0 collective-permute-done.2
  11.1 0.1 broadcast_select_fusion.1
  11.2 4.8 %collective-permute-start.3 = (bf16[64,2048]{1,0:T(8,128)(2,1)S(1)}, bf16[64,2048]{1,0:T(8,128)(2,1)S(1)}, u32[]{:S(2)}, u32[]{:S(2)}) collective-permute-start(bf16[64,2048]{1,0:T(8,128)(2,1)S(1)} %get-tuple-element.15), channel_id=1, source_target_pairs={{0,0},{1,5},{2,64},{3,69},{4,128},{5,133},{6,192},{7,197},{64,2},{... | collective-permute-start | bytes 786440 | tf_op jit(solution)/shard_map/ppermute | solution.py:201
  16.1 0.0 all-to-all-done
  16.1 1.8 collective-permute-start.5
  17.9 0.7 broadcast_in_dim.41
  18.7 8.2 %all-to-all-start.1 = ((bf16[8,64,256]{2,1,0:T(8,128)(2,1)}), bf16[8,64,256]{2,1,0:T(8,128)(2,1)S(1)}, u32[]{:S(2)}, u32[]{:S(2)}) async-start(bf16[8,64,256]{2,1,0:T(8,128)(2,1)} %broadcast_in_dim.41), calls=%async_computation.1 | async-start | bytes 524288 | tf_op jit(solution)/shard_map/all_to_all | solution.py:29
  26.9 0.0 collective-permute-done.3
  26.9 0.1 collective-permute-start.4
  27.0 0.0 collective-permute-done.5
  27.0 0.6 collective-permute-start.6
  27.6 0.0 collective-permute-done.1
  27.6 1.1 pad_maximum_fusion
  28.7 10.6 %all-to-all-done.1 = bf16[8,64,256]{2,1,0:T(8,128)(2,1)S(1)} async-done(((bf16[8,64,256]{2,1,0:T(8,128)(2,1)}), bf16[8,64,256]{2,1,0:T(8,128)(2,1)S(1)}, u32[]{:S(2)}, u32[]{:S(2)}) %all-to-all-start.1) | async-done | bytes 262176 | tf_op jit(solution)/shard_map/all_to_all | solution.py:29
  39.3 0.0 collective-permute-done.4
  39.4 0.0 collective-permute-done.6
  39.4 0.1 pad_maximum_fusion.1
  39.5 0.4 convolution_convert_fusion.6
  40.0 8.5 %all_to_all.75 = bf16[4,72,256]{2,1,0:T(8,128)(2,1)S(1)} all-to-all(bf16[4,72,256]{2,1,0:T(8,128)(2,1)S(1)} %broadcast_in_dim.47), channel_id=1, replica_groups=mesh['y'=4,'z'=8,'x'=4,'core'=2] {'y'}, dimensions={0} | all-to-all | bytes 294912 | tf_op jit(solution)/shard_map/all_to_all | solution.py:29
  48.6 0.3 convolution_convert_fusion.3
  48.9 11.9 %all_to_all.76 = bf16[8,64,256]{2,1,0:T(8,128)(2,1)S(1)} all-to-all(bf16[8,64,256]{2,1,0:T(8,128)(2,1)S(1)} %bitcast.88), channel_id=1, replica_groups=mesh['y'=4,'z'=8,'x'=4,'core'=2] {'z'}, dimensions={0} | all-to-all | bytes 524288 | tf_op jit(solution)/shard_map/all_to_all | solution.py:29
  60.9 7.2 %all_to_all.77 = bf16[4,64,256]{2,1,0:T(8,128)(2,1)S(1)} all-to-all(bf16[4,64,256]{2,1,0:T(8,128)(2,1)S(1)} %broadcast_in_dim.48), channel_id=1, replica_groups=mesh['y'=4,'z'=8,'x'=4,'core'=2] {'x'}, dimensions={0} | all-to-all | bytes 262144 | tf_op jit(solution)/shard_map/all_to_all | solution.py:29
  68.2 0.3 convolution_convert_fusion.2
  68.5 14.1 %all_to_all.78 = bf16[32,8,512]{2,1,0:T(8,128)(2,1)S(1)} all-to-all(bf16[32,8,512]{2,1,0:T(8,128)(2,1)S(1)} %bitcast.95), channel_id=1, replica_groups=mesh['y'=4,'z'=8,'x'=4,'core'=2] {'y','z'}, dimensions={0} | all-to-all | bytes 524288 | tf_op jit(solution)/shard_map/all_to_all | solution.py:29
  82.6 0.1 reduce_sum.117
  82.6 14.1 %all_to_all.79 = bf16[32,8,512]{2,1,0:T(8,128)(2,1)S(1)} all-to-all(bf16[32,8,512]{2,1,0:T(8,128)(2,1)S(1)} %broadcast_in_dim.49), channel_id=1, replica_groups=mesh['y'=4,'z'=8,'x'=4,'core'=2] {'y','z'}, dimensions={0} | all-to-all | bytes 524288 | tf_op jit(solution)/shard_map/all_to_all | solution.py:29
  96.8 0.4 convolution_convert_fusion.5
  97.2 0.2 reduce-precision_convert_fusion.1
  97.5 0.1 pad_maximum_fusion.5
  97.6 7.5 %all_to_all.80.arrived_ref = bf16[4,64,384]{2,1,0:T(8,128)(2,1)S(1)} all-to-all(bf16[4,64,384]{2,1,0:T(8,128)(2,1)S(1)} %broadcast_in_dim.50), channel_id=1, replica_groups=mesh['y'=4,'z'=8,'x'=4,'core'=2] {'x'}, dimensions={0} | all-to-all | bytes 393216 | tf_op jit(solution)/shard_map/all_to_all | solution.py:29
  105.1 2.2 %normalized_forward.1 = bf16[64,256]{1,0:T(8,128)(2,1)S(1)} custom-call(bf16[4,64,384]{2,1,0:T(8,128)(2,1)S(1)} %all_to_all.80.arrived_ref, f32[1,256]{1,0:T(1,128)S(1)} %get-tuple-element.27.slope_ref), custom_call_target="tpu_custom_call" | custom-call | tf_op jit(solution)/shard_map/normalized_forward/pallas_call | solution.py:108
  107.3 12.5 %all_to_all.81 = bf16[8,64,256]{2,1,0:T(8,128)(2,1)S(1)} all-to-all(bf16[8,64,256]{2,1,0:T(8,128)(2,1)S(1)} %broadcast_in_dim.51), channel_id=1, replica_groups=mesh['y'=4,'z'=8,'x'=4,'core'=2] {'z'}, dimensions={0} | all-to-all | bytes 524288 | tf_op jit(solution)/shard_map/all_to_all | solution.py:29
  119.8 0.4 convolution_convert_fusion.4
  120.3 7.2 %all_to_all.82 = bf16[4,64,256]{2,1,0:T(8,128)(2,1)S(1)} all-to-all(bf16[4,64,256]{2,1,0:T(8,128)(2,1)S(1)} %broadcast_in_dim.52), channel_id=1, replica_groups=mesh['y'=4,'z'=8,'x'=4,'core'=2] {'y'}, dimensions={0} | all-to-all | bytes 262144 | tf_op jit(solution)/shard_map/all_to_all | solution.py:29
  127.5 0.3 convolution_convert_fusion.1
  127.9 11.7 %all_to_all.83 = bf16[8,64,256]{2,1,0:T(8,128)(2,1)S(1)} all-to-all(bf16[8,64,256]{2,1,0:T(8,128)(2,1)S(1)} %bitcast.90), channel_id=1, replica_groups=mesh['y'=4,'z'=8,'x'=4,'core'=2] {'z'}, dimensions={0} | all-to-all | bytes 524288 | tf_op jit(solution)/shard_map/all_to_all | solution.py:29
  139.7 7.2 %all_to_all.84 = bf16[4,64,256]{2,1,0:T(8,128)(2,1)S(1)} all-to-all(bf16[4,64,256]{2,1,0:T(8,128)(2,1)S(1)} %broadcast_in_dim.53), channel_id=1, replica_groups=mesh['y'=4,'z'=8,'x'=4,'core'=2] {'x'}, dimensions={0} | all-to-all | bytes 262144 | tf_op jit(solution)/shard_map/all_to_all | solution.py:29
  146.9 0.3 convolution_convert_fusion
  147.2 12.6 %all_to_all.85 = bf16[32,8,512]{2,1,0:T(8,128)(2,1)S(1)} all-to-all(bf16[32,8,512]{2,1,0:T(8,128)(2,1)S(1)} %bitcast.93), channel_id=1, replica_groups=mesh['y'=4,'z'=8,'x'=4,'core'=2] {'y','z'}, dimensions={0} | all-to-all | bytes 524288 | tf_op jit(solution)/shard_map/all_to_all | solution.py:29
  159.9 0.1 reduce_sum.121
  159.9 14.5 %all_to_all.86 = bf16[32,8,512]{2,1,0:T(8,128)(2,1)S(1)} all-to-all(bf16[32,8,512]{2,1,0:T(8,128)(2,1)S(1)} %broadcast_in_dim.54), channel_id=1, replica_groups=mesh['y'=4,'z'=8,'x'=4,'core'=2] {'y','z'}, dimensions={0} | all-to-all | bytes 524288 | tf_op jit(solution)/shard_map/all_to_all | solution.py:29
  174.5 0.2 reduce-precision_convert_fusion
  174.7 14.6 %collective-permute-start.7 = (bf16[64,1024]{1,0:T(8,128)(2,1)S(1)}, bf16[64,1024]{1,0:T(8,128)(2,1)S(1)}, u32[]{:S(2)}, u32[]{:S(2)}) collective-permute-start(bf16[64,1024]{1,0:T(8,128)(2,1)S(1)} %slice.67), channel_id=1, source_target_pairs={{0,1},{1,0},{2,3},{3,2},{4,5},{5,4},{6,7},{7,6},{8,9},{9,8},{10,11... | collective-permute-start | bytes 393224 | tf_op jit(solution)/shard_map/ppermute | solution.py:244
  189.3 0.1 pad_maximum_fusion.6
  189.4 7.6 %all_to_all.87.arrived_ref = bf16[8,64,128]{2,1,0:T(8,128)(2,1)S(1)} all-to-all(bf16[8,64,128]{2,1,0:T(8,128)(2,1)S(1)} %broadcast_in_dim.102), channel_id=1, replica_groups=mesh['y'=4,'z'=8,'x'=4,'core'=2] {'x','core'}, dimensions={0} | all-to-all | bytes 262144 | tf_op jit(solution)/shard_map/all_to_all | solution.py:29
  197.0 0.0 collective-permute-done.7.there_ref
  197.0 3.9 %normalized_panels.1 = f32[2,64,1024]{2,1,0:T(8,128)} custom-call(s32[1]{0:T(128)} %bitcast.core_ref, bf16[8,64,128]{2,1,0:T(8,128)(2,1)S(1)} %all_to_all.87.arrived_ref, bf16[64,2048]{1,0:T(8,128)(2,1)S(1)} %bitcast.84, bf16[64,1024]{1,0:T(8,128)(2,1)S(1)} %collective-permute-done.7.there_ref), custom_call_target="tpu_custom_call" | custom-call | tf_op jit(solution)/shard_map/normalized_panels/pallas_call | solution.py:134
  (38 shorter events, 0.7 us)
Async XLA Ops:
  0.0 4.8 %copy-start = (bf16[2,64,1024]{2,1,0:T(8,128)(2,1)S(1)}, bf16[2,64,1024]{2,1,0:T(8,128)(2,1)}, u32[]{:S(2)}) copy-start(bf16[2,64,1024]{2,1,0:T(8,128)(2,1)} %param.5) | copy-start | bytes 786436
  1.3 3.5 %copy-start.1 = (bf16[2,256,1024]{2,1,0:T(8,128)(2,1)S(1)}, bf16[2,256,1024]{2,1,0:T(8,128)(2,1)}, u32[]{:S(2)}) copy-start(bf16[2,256,1024]{2,1,0:T(8,128)(2,1)} %param.3) | copy-start | bytes 3145732
  1.4 4.8 %copy-start.2 = (f32[2,2,256]{2,1,0:T(2,128)S(1)}, f32[2,2,256]{2,1,0:T(2,128)}, u32[]{:S(2)}) copy-start(f32[2,2,256]{2,1,0:T(2,128)} %param.4) | copy-start | bytes 12292
  1.4 9.7 %collective-permute-start.2 = (bf16[128,1024]{1,0:T(8,128)(2,1)S(1)}, bf16[128,1024]{1,0:T(8,128)(2,1)S(1)}, u32[]{:S(2)}, u32[]{:S(2)}) collective-permute-start(bf16[128,1024]{1,0:T(8,128)(2,1)S(1)} %pad_maximum_fusion.4), channel_id=1, source_target_pairs={{0,1},{1,0},{2,3},{3,2},{4,5},{5,4},{6,7},{7,6},{8,9},{9,8},{10,11... | collective-permute-start | bytes 786440 | tf_op jit(solution)/shard_map/ppermute | solution.py:196
  4.7 22.8 %collective-permute-start.1 = (bf16[256,1024]{1,0:T(8,128)(2,1)S(1)}, bf16[256,1024]{1,0:T(8,128)(2,1)}, u32[]{:S(2)}, u32[]{:S(2)}) collective-permute-start(bf16[256,1024]{1,0:T(8,128)(2,1)S(1)} %get-tuple-element.10), channel_id=1, source_target_pairs={{0,1},{1,0},{2,3},{3,2},{4,5},{5,4},{6,7},{7,6},{8,9},{9,8},{10,11... | collective-permute-start | bytes 1572872 | tf_op jit(solution)/shard_map/ppermute | solution.py:206
  5.2 1.9 collective-permute-start
  7.8 8.3 %all-to-all-start = ((bf16[4,64,256]{2,1,0:T(8,128)(2,1)}), bf16[4,64,256]{2,1,0:T(8,128)(2,1)S(1)}, u32[]{:S(2)}, u32[]{:S(2)}) async-start(bf16[4,64,256]{2,1,0:T(8,128)(2,1)} %broadcast_in_dim.40), calls=%async_computation | async-start | bytes 262144 | tf_op jit(solution)/shard_map/all_to_all | solution.py:29
  11.2 15.6 %collective-permute-start.3 = (bf16[64,2048]{1,0:T(8,128)(2,1)S(1)}, bf16[64,2048]{1,0:T(8,128)(2,1)S(1)}, u32[]{:S(2)}, u32[]{:S(2)}) collective-permute-start(bf16[64,2048]{1,0:T(8,128)(2,1)S(1)} %get-tuple-element.15), channel_id=1, source_target_pairs={{0,0},{1,5},{2,64},{3,69},{4,128},{5,133},{6,192},{7,197},{64,2},{... | collective-permute-start | bytes 786440 | tf_op jit(solution)/shard_map/ppermute | solution.py:201
  16.1 10.9 %collective-permute-start.5 = (bf16[64,2048]{1,0:T(8,128)(2,1)S(1)}, bf16[64,2048]{1,0:T(8,128)(2,1)S(1)}, u32[]{:S(2)}, u32[]{:S(2)}) collective-permute-start(bf16[64,2048]{1,0:T(8,128)(2,1)S(1)} %get-tuple-element.16), channel_id=1, source_target_pairs={{0,2},{1,7},{2,66},{3,71},{4,130},{5,135},{6,194},{7,199},{64,4},{... | collective-permute-start | bytes 786440 | tf_op jit(solution)/shard_map/ppermute | solution.py:201
  18.7 20.6 %all-to-all-start.1 = ((bf16[8,64,256]{2,1,0:T(8,128)(2,1)}), bf16[8,64,256]{2,1,0:T(8,128)(2,1)S(1)}, u32[]{:S(2)}, u32[]{:S(2)}) async-start(bf16[8,64,256]{2,1,0:T(8,128)(2,1)} %broadcast_in_dim.41), calls=%async_computation.1 | async-start | bytes 524288 | tf_op jit(solution)/shard_map/all_to_all | solution.py:29
  26.9 12.4 %collective-permute-start.4 = (bf16[64,2048]{1,0:T(8,128)(2,1)S(1)}, bf16[64,2048]{1,0:T(8,128)(2,1)S(1)}, u32[]{:S(2)}, u32[]{:S(2)}) collective-permute-start(bf16[64,2048]{1,0:T(8,128)(2,1)S(1)} %collective-permute-done.3), channel_id=1, source_target_pairs={{0,1},{1,0},{2,3},{3,2},{4,5},{5,4},{6,7},{7,6},{8,9},{9,8},{10,11... | collective-permute-start | bytes 786440 | tf_op jit(solution)/shard_map/ppermute | solution.py:202
  27.0 12.4 %collective-permute-start.6 = (bf16[64,2048]{1,0:T(8,128)(2,1)S(1)}, bf16[64,2048]{1,0:T(8,128)(2,1)S(1)}, u32[]{:S(2)}, u32[]{:S(2)}) collective-permute-start(bf16[64,2048]{1,0:T(8,128)(2,1)S(1)} %collective-permute-done.5), channel_id=1, source_target_pairs={{0,1},{1,0},{2,3},{3,2},{4,5},{5,4},{6,7},{7,6},{8,9},{9,8},{10,11... | collective-permute-start | bytes 786440 | tf_op jit(solution)/shard_map/ppermute | solution.py:202
  174.7 22.4 %collective-permute-start.7 = (bf16[64,1024]{1,0:T(8,128)(2,1)S(1)}, bf16[64,1024]{1,0:T(8,128)(2,1)S(1)}, u32[]{:S(2)}, u32[]{:S(2)}) collective-permute-start(bf16[64,1024]{1,0:T(8,128)(2,1)S(1)} %slice.67), channel_id=1, source_target_pairs={{0,1},{1,0},{2,3},{3,2},{4,5},{5,4},{6,7},{7,6},{8,9},{9,8},{10,11... | collective-permute-start | bytes 393224 | tf_op jit(solution)/shard_map/ppermute | solution.py:244

commit v9 on v8

--- a/solution.py
+++ b/solution.py
@@ -44,9 +44,13 @@
     cols = lax.broadcasted_iota(jnp.int32, (n, n), 1)
     eye = (rows == cols).astype(F32)
     row_of = lax.broadcasted_iota(jnp.int32, (8, 2 * n), 0)
-    many = []
+    many, across = [], []
     for gram in grams:
-        both = jnp.concatenate([eye, gram * (1.0 / WIDTH)], axis=1)
+        gram = gram * (1.0 / WIDTH)
+        diagonal = gram * eye
+        down = 1.0 / jnp.sqrt(jnp.sum(diagonal, axis=1, keepdims=True))
+        across.append(1.0 / jnp.sqrt(jnp.sum(diagonal, axis=0, keepdims=True)))
+        both = jnp.concatenate([eye, gram * down * across[-1]], axis=1)
         many.append([both[8 * i : 8 * i + 8] for i in range(count)])
 
     def columns_of(blocks, k):
@@ -57,28 +61,36 @@
 
     def step(blocks, columns, scale, k, t):
         live = range(k, count)
-        inverse = 1.0 / columns[t][k][t : t + 1, :]
-        factors = {i: columns[t][i] * inverse for i in live}
-        factors[k] = jnp.where(row_of > t, factors[k], 0.0)
-        for u in range(t + 1, 8):
-            entry = columns[u][k][t : t + 1, :]
+        first, second = columns[t], columns[t + 1]
+        a, b, d = first[k][t : t + 1], second[k][t : t + 1], second[k][t + 1 : t + 2]
+        over_a, over_next = 1.0 / a, a * (1.0 / (a * d - b * b))
+        ratio = b * over_a
+        second = {i: second[i] - first[i] * ratio for i in live}
+        first = dict(first)
+        first[k] = jnp.where(row_of > t, first[k], 0.0)
+        second[k] = jnp.where(row_of > t + 1, second[k], 0.0)
+        for u in range(t + 2, 8):
+            entry = columns[u][k][t : t + 1]
+            entry_next = (columns[u][k][t + 1 : t + 2] - entry * ratio) * over_next
+            entry = entry * over_a
             for i in live:
-                columns[u][i] = columns[u][i] - factors[i] * entry
-        pivot_row = blocks[k][t : t + 1, :]
+                columns[u][i] = columns[u][i] - first[i] * entry - second[i] * entry_next
+        row = blocks[k][t : t + 1] * over_a
+        row_next = (blocks[k][t + 1 : t + 2] - b * row) * over_next
         for i in live:
-            blocks[i] = blocks[i] - factors[i] * pivot_row
-        return jnp.where(row_of == t, inverse, scale)
+            blocks[i] = blocks[i] - first[i] * row - second[i] * row_next
+        return jnp.where(row_of == t, over_a, jnp.where(row_of == t + 1, over_next, scale))
 
     done = [[] for _ in many]
     for k in range(count):
         columns = [columns_of(blocks, k) for blocks in many]
         scales = [jnp.zeros((8, 2 * n), F32) for _ in many]
-        for t in range(8):
+        for t in range(0, 8, 2):
             for g, blocks in enumerate(many):
                 scales[g] = step(blocks, columns[g], scales[g], k, t)
         for g, blocks in enumerate(many):
             done[g].append(blocks[k] * jnp.sqrt(scales[g]))
-    return [jnp.concatenate(d, axis=0)[:, :n] for d in done]
+    return [jnp.concatenate(d, axis=0)[:, :n] * s for d, s in zip(done, across)]
 
 
 def exact_dot(a, b):
@@ -93,6 +105,36 @@
     for part in parts[1:]:
         summed = summed + part
     return summed[:, :rank] + summed[:, rank:]
+
+
+def first_partial(panel, weights):
+    inputs, rank, width = panel.shape
+    rows = weights.shape[1]
+
+    def kernel(panel_ref, weights_ref, mine_ref, theirs_ref, panel_here, block_here, sems):
+        panel_copy = pltpu.make_async_copy(panel_ref, panel_here, sems.at[0])
+        block_copy = pltpu.make_async_copy(weights_ref.at[0], block_here, sems.at[1])
+        panel_copy.start()
+        block_copy.start()
+        panel_copy.wait()
+        block_copy.wait()
+        core = lax.axis_index("core")
+        block = block_here[...]
+        mine_ref[...] = dot_t(panel_here[pl.ds(core, 1)][0], block)
+        theirs_ref[...] = dot_t(panel_here[pl.ds(1 - core, 1)][0], block)
+
+    return pl.pallas_call(
+        kernel,
+        in_specs=[pl.BlockSpec(memory_space=pltpu.HBM)] * 2,
+        out_specs=[WHOLE] * 2,
+        out_shape=[pltpu.VMEM((rank, rows), F32)] * 2,
+        scratch_shapes=[
+            pltpu.VMEM((inputs, rank, width), BF16),
+            pltpu.VMEM((rows, width), BF16),
+            pltpu.SemaphoreType.DMA((2,)),
+        ],
+        name="first_partial",
+    )(panel, weights)
 
 
 def normalized_forward(arrived, slope, width):
@@ -171,9 +213,7 @@
         width_row = weights.shape[1]
         w1_own, w2_own = weights[0], weights[1]
 
-        partial_out = jnp.einsum("bki,oi->bko", panel, w1_own, preferred_element_type=F32)
-        mine = jnp.where(first, partial_out[0], partial_out[1])
-        theirs = jnp.where(first, partial_out[1], partial_out[0])
+        mine, theirs = first_partial(panel, weights)
         traded = lax.ppermute(theirs, "core", flip)
         summed_out = mine + traded
 

time: 202 us -> 202 us (level)
  transfers between devices with their start and end apart: 10 -> 10, of which waited for: 2 -> 2; matrix products, arithmetic and copies ran while one was open for 2% -> 1% of each run, Pallas kernels for 0% -> 1%
where the time goes in v9:
time: 202 us; the launch traced here: 201 us
  blocking collectives  137 us (68%)
  starting transfers between devices  37.1 us (18%)
  waiting for transfers between devices  12.2 us (6%)
  Pallas kernels  6.69 us (3%)
  local copies, waits for them, and re-layouts  3.3 us (2%)
  matrix products  2.96 us (1%)
    all_to_all x13, blocking collectives, exchange(): return lax.all_to_all(tiles, axis, split_axis=0, concat_axis=0, tiled=True)  137 us
    ppermute x1, starting transfers between devices, on_device(): there = lax.ppermute(image[:, width_in:], 'core', flip)  14.4 us
    all_to_all x2, waiting for transfers between devices, exchange(): return lax.all_to_all(tiles, axis, split_axis=0, concat_axis=0, tiled=True)  11.6 us
    all_to_all x2, starting transfers between devices, exchange(): return lax.all_to_all(tiles, axis, split_axis=0, concat_axis=0, tiled=True)  11.5 us
    ppermute x2, starting transfers between devices, on_device(): here.append(lax.ppermute(rows[e], ('y', 'x', 'core'), turns[e]))  6.65 us
  transfers between devices with their start and end apart: 10, of which 2 were waited for; matrix products, arithmetic and copies ran while one was open for 1% of the time, Pallas kernels for 1%

profile of v9, /device:TPU:1, one launch (start us, length us, event | category | flops | bytes accessed | tf_op | source)
XLA Modules:
  0.0 201.3 jit_solution(9299832351877960615)
XLA Ops:
  0.0 1.3 fusion.9
  1.3 0.0 copy-start
  1.4 3.3 %collective-permute-start.2 = (bf16[128,1024]{1,0:T(8,128)(2,1)S(1)}, bf16[128,1024]{1,0:T(8,128)(2,1)S(1)}, u32[]{:S(2)}, u32[]{:S(2)}) collective-permute-start(bf16[128,1024]{1,0:T(8,128)(2,1)S(1)} %pad_maximum_fusion.4), channel_id=1, source_target_pairs={{0,1},{1,0},{2,3},{3,2},{4,5},{5,4},{6,7},{7,6},{8,9},{9,8},{10,11... | collective-permute-start | bytes 786440 | tf_op jit(solution)/shard_map/ppermute | solution.py:236
  4.7 0.1 collective-permute-start.1
  4.8 1.6 first_partial.1
  6.3 0.5 collective-permute-start
  6.8 0.0 copy-done
  6.9 0.1 fusion.8
  7.0 0.1 iota.9
  7.0 0.1 iota.10
  7.1 0.1 broadcast_in_dim.44
  7.2 0.5 collective-permute-done
  7.8 0.7 broadcast_in_dim.40
  8.4 3.3 %all-to-all-start = ((bf16[4,64,256]{2,1,0:T(8,128)(2,1)}), bf16[4,64,256]{2,1,0:T(8,128)(2,1)S(1)}, u32[]{:S(2)}, u32[]{:S(2)}) async-start(bf16[4,64,256]{2,1,0:T(8,128)(2,1)} %broadcast_in_dim.40), calls=%async_computation | async-start | bytes 262144 | tf_op jit(solution)/shard_map/all_to_all | solution.py:29
  11.8 0.0 collective-permute-done.2
  11.8 0.1 broadcast_select_fusion.1
  11.9 4.8 %collective-permute-start.3 = (bf16[64,2048]{1,0:T(8,128)(2,1)S(1)}, bf16[64,2048]{1,0:T(8,128)(2,1)S(1)}, u32[]{:S(2)}, u32[]{:S(2)}) collective-permute-start(bf16[64,2048]{1,0:T(8,128)(2,1)S(1)} %get-tuple-element.19), channel_id=1, source_target_pairs={{0,0},{1,5},{2,64},{3,69},{4,128},{5,133},{6,192},{7,197},{64,2},{... | collective-permute-start | bytes 786440 | tf_op jit(solution)/shard_map/ppermute | solution.py:241
  16.8 0.0 all-to-all-done
  16.8 1.8 collective-permute-start.5
  18.6 0.7 broadcast_in_dim.41
  19.4 8.2 %all-to-all-start.1 = ((bf16[8,64,256]{2,1,0:T(8,128)(2,1)}), bf16[8,64,256]{2,1,0:T(8,128)(2,1)S(1)}, u32[]{:S(2)}, u32[]{:S(2)}) async-start(bf16[8,64,256]{2,1,0:T(8,128)(2,1)} %broadcast_in_dim.41), calls=%async_computation.1 | async-start | bytes 524288 | tf_op jit(solution)/shard_map/all_to_all | solution.py:29
  27.5 0.0 collective-permute-done.3
  27.6 0.1 collective-permute-start.4
  27.7 0.0 collective-permute-done.5
  27.7 0.6 collective-permute-start.6
  28.2 0.0 collective-permute-done.1
  28.3 0.1 pad_maximum_fusion
  28.3 11.6 %all-to-all-done.1 = bf16[8,64,256]{2,1,0:T(8,128)(2,1)S(1)} async-done(((bf16[8,64,256]{2,1,0:T(8,128)(2,1)}), bf16[8,64,256]{2,1,0:T(8,128)(2,1)S(1)}, u32[]{:S(2)}, u32[]{:S(2)}) %all-to-all-start.1) | async-done | bytes 262176 | tf_op jit(solution)/shard_map/all_to_all | solution.py:29
  40.0 0.0 collective-permute-done.4
  40.1 0.0 collective-permute-done.6
  40.1 1.0 broadcast_select_fusion.4
  41.1 0.1 pad_maximum_fusion.1
  41.1 0.4 convolution_convert_fusion.6
  41.6 8.5 %all_to_all.75 = bf16[4,72,256]{2,1,0:T(8,128)(2,1)S(1)} all-to-all(bf16[4,72,256]{2,1,0:T(8,128)(2,1)S(1)} %broadcast_in_dim.47), channel_id=1, replica_groups=mesh['y'=4,'z'=8,'x'=4,'core'=2] {'y'}, dimensions={0} | all-to-all | bytes 294912 | tf_op jit(solution)/shard_map/all_to_all | solution.py:29
  50.2 0.3 convolution_convert_fusion.3
  50.5 11.9 %all_to_all.76 = bf16[8,64,256]{2,1,0:T(8,128)(2,1)S(1)} all-to-all(bf16[8,64,256]{2,1,0:T(8,128)(2,1)S(1)} %bitcast.78), channel_id=1, replica_groups=mesh['y'=4,'z'=8,'x'=4,'core'=2] {'z'}, dimensions={0} | all-to-all | bytes 524288 | tf_op jit(solution)/shard_map/all_to_all | solution.py:29
  62.5 7.2 %all_to_all.77 = bf16[4,64,256]{2,1,0:T(8,128)(2,1)S(1)} all-to-all(bf16[4,64,256]{2,1,0:T(8,128)(2,1)S(1)} %broadcast_in_dim.48), channel_id=1, replica_groups=mesh['y'=4,'z'=8,'x'=4,'core'=2] {'x'}, dimensions={0} | all-to-all | bytes 262144 | tf_op jit(solution)/shard_map/all_to_all | solution.py:29
  69.7 0.3 convolution_convert_fusion.2
  70.1 14.1 %all_to_all.78 = bf16[32,8,512]{2,1,0:T(8,128)(2,1)S(1)} all-to-all(bf16[32,8,512]{2,1,0:T(8,128)(2,1)S(1)} %bitcast.85), channel_id=1, replica_groups=mesh['y'=4,'z'=8,'x'=4,'core'=2] {'y','z'}, dimensions={0} | all-to-all | bytes 524288 | tf_op jit(solution)/shard_map/all_to_all | solution.py:29
  84.2 0.1 reduce_sum.117
  84.2 14.1 %all_to_all.79 = bf16[32,8,512]{2,1,0:T(8,128)(2,1)S(1)} all-to-all(bf16[32,8,512]{2,1,0:T(8,128)(2,1)S(1)} %broadcast_in_dim.49), channel_id=1, replica_groups=mesh['y'=4,'z'=8,'x'=4,'core'=2] {'y','z'}, dimensions={0} | all-to-all | bytes 524288 | tf_op jit(solution)/shard_map/all_to_all | solution.py:29
  98.4 0.4 convolution_convert_fusion.5
  98.8 0.2 reduce-precision_convert_fusion.1
  99.0 0.1 pad_maximum_fusion.5
  99.1 7.5 %all_to_all.80.arrived_ref = bf16[4,64,384]{2,1,0:T(8,128)(2,1)S(1)} all-to-all(bf16[4,64,384]{2,1,0:T(8,128)(2,1)S(1)} %broadcast_in_dim.50), channel_id=1, replica_groups=mesh['y'=4,'z'=8,'x'=4,'core'=2] {'x'}, dimensions={0} | all-to-all | bytes 393216 | tf_op jit(solution)/shard_map/all_to_all | solution.py:29
  106.7 1.7 normalized_forward.1
  108.5 12.5 %all_to_all.81 = bf16[8,64,256]{2,1,0:T(8,128)(2,1)S(1)} all-to-all(bf16[8,64,256]{2,1,0:T(8,128)(2,1)S(1)} %broadcast_in_dim.51), channel_id=1, replica_groups=mesh['y'=4,'z'=8,'x'=4,'core'=2] {'z'}, dimensions={0} | all-to-all | bytes 524288 | tf_op jit(solution)/shard_map/all_to_all | solution.py:29
  121.0 0.4 convolution_convert_fusion.4
  121.4 7.2 %all_to_all.82 = bf16[4,64,256]{2,1,0:T(8,128)(2,1)S(1)} all-to-all(bf16[4,64,256]{2,1,0:T(8,128)(2,1)S(1)} %broadcast_in_dim.52), channel_id=1, replica_groups=mesh['y'=4,'z'=8,'x'=4,'core'=2] {'y'}, dimensions={0} | all-to-all | bytes 262144 | tf_op jit(solution)/shard_map/all_to_all | solution.py:29
  128.7 0.3 convolution_convert_fusion.1
  129.0 11.7 %all_to_all.83 = bf16[8,64,256]{2,1,0:T(8,128)(2,1)S(1)} all-to-all(bf16[8,64,256]{2,1,0:T(8,128)(2,1)S(1)} %bitcast.80), channel_id=1, replica_groups=mesh['y'=4,'z'=8,'x'=4,'core'=2] {'z'}, dimensions={0} | all-to-all | bytes 524288 | tf_op jit(solution)/shard_map/all_to_all | solution.py:29
  140.8 7.2 %all_to_all.84 = bf16[4,64,256]{2,1,0:T(8,128)(2,1)S(1)} all-to-all(bf16[4,64,256]{2,1,0:T(8,128)(2,1)S(1)} %broadcast_in_dim.53), channel_id=1, replica_groups=mesh['y'=4,'z'=8,'x'=4,'core'=2] {'x'}, dimensions={0} | all-to-all | bytes 262144 | tf_op jit(solution)/shard_map/all_to_all | solution.py:29
  148.0 0.3 convolution_convert_fusion
  148.3 12.6 %all_to_all.85 = bf16[32,8,512]{2,1,0:T(8,128)(2,1)S(1)} all-to-all(bf16[32,8,512]{2,1,0:T(8,128)(2,1)S(1)} %bitcast.83), channel_id=1, replica_groups=mesh['y'=4,'z'=8,'x'=4,'core'=2] {'y','z'}, dimensions={0} | all-to-all | bytes 524288 | tf_op jit(solution)/shard_map/all_to_all | solution.py:29
  161.0 0.1 reduce_sum.121
  161.0 14.5 %all_to_all.86 = bf16[32,8,512]{2,1,0:T(8,128)(2,1)S(1)} all-to-all(bf16[32,8,512]{2,1,0:T(8,128)(2,1)S(1)} %broadcast_in_dim.54), channel_id=1, replica_groups=mesh['y'=4,'z'=8,'x'=4,'core'=2] {'y','z'}, dimensions={0} | all-to-all | bytes 524288 | tf_op jit(solution)/shard_map/all_to_all | solution.py:29
  175.6 0.2 reduce-precision_convert_fusion
  175.8 14.4 %collective-permute-start.7 = (bf16[64,1024]{1,0:T(8,128)(2,1)S(1)}, bf16[64,1024]{1,0:T(8,128)(2,1)S(1)}, u32[]{:S(2)}, u32[]{:S(2)}) collective-permute-start(bf16[64,1024]{1,0:T(8,128)(2,1)S(1)} %slice.55), channel_id=1, source_target_pairs={{0,1},{1,0},{2,3},{3,2},{4,5},{5,4},{6,7},{7,6},{8,9},{9,8},{10,11... | collective-permute-start | bytes 393224 | tf_op jit(solution)/shard_map/ppermute | solution.py:284
  190.2 0.1 pad_maximum_fusion.6
  190.3 7.6 %all_to_all.87.arrived_ref = bf16[8,64,128]{2,1,0:T(8,128)(2,1)S(1)} all-to-all(bf16[8,64,128]{2,1,0:T(8,128)(2,1)S(1)} %broadcast_in_dim.102), channel_id=1, replica_groups=mesh['y'=4,'z'=8,'x'=4,'core'=2] {'x','core'}, dimensions={0} | all-to-all | bytes 262144 | tf_op jit(solution)/shard_map/all_to_all | solution.py:29
  197.9 0.0 collective-permute-done.7.there_ref
  197.9 3.4 %normalized_panels.1 = f32[2,64,1024]{2,1,0:T(8,128)} custom-call(s32[1]{0:T(128)} %bitcast.core_ref, bf16[8,64,128]{2,1,0:T(8,128)(2,1)S(1)} %all_to_all.87.arrived_ref, bf16[64,2048]{1,0:T(8,128)(2,1)S(1)} %bitcast.74, bf16[64,1024]{1,0:T(8,128)(2,1)S(1)} %collective-permute-done.7.there_ref), custom_call_target="tpu_custom_call" | custom-call | tf_op jit(solution)/shard_map/normalized_panels/pallas_call | solution.py:176
  (35 shorter events, 0.7 us)
Async XLA Ops:
  1.3 5.5 %copy-start = (f32[2,2,256]{2,1,0:T(2,128)S(1)}, f32[2,2,256]{2,1,0:T(2,128)}, u32[]{:S(2)}) copy-start(f32[2,2,256]{2,1,0:T(2,128)} %param.4) | copy-start | bytes 12292
  1.4 10.4 %collective-permute-start.2 = (bf16[128,1024]{1,0:T(8,128)(2,1)S(1)}, bf16[128,1024]{1,0:T(8,128)(2,1)S(1)}, u32[]{:S(2)}, u32[]{:S(2)}) collective-permute-start(bf16[128,1024]{1,0:T(8,128)(2,1)S(1)} %pad_maximum_fusion.4), channel_id=1, source_target_pairs={{0,1},{1,0},{2,3},{3,2},{4,5},{5,4},{6,7},{7,6},{8,9},{9,8},{10,11... | collective-permute-start | bytes 786440 | tf_op jit(solution)/shard_map/ppermute | solution.py:236
  4.7 23.6 %collective-permute-start.1 = (bf16[256,1024]{1,0:T(8,128)(2,1)S(1)}, bf16[256,1024]{1,0:T(8,128)(2,1)S(1)}, u32[]{:S(2)}, u32[]{:S(2)}) collective-permute-start(bf16[256,1024]{1,0:T(8,128)(2,1)S(1)} %get-tuple-element.14), channel_id=1, source_target_pairs={{0,1},{1,0},{2,3},{3,2},{4,5},{5,4},{6,7},{7,6},{8,9},{9,8},{10,11... | collective-permute-start | bytes 1572872 | tf_op jit(solution)/shard_map/ppermute | solution.py:246
  6.3 1.4 collective-permute-start
  8.4 8.4 %all-to-all-start = ((bf16[4,64,256]{2,1,0:T(8,128)(2,1)}), bf16[4,64,256]{2,1,0:T(8,128)(2,1)S(1)}, u32[]{:S(2)}, u32[]{:S(2)}) async-start(bf16[4,64,256]{2,1,0:T(8,128)(2,1)} %broadcast_in_dim.40), calls=%async_computation | async-start | bytes 262144 | tf_op jit(solution)/shard_map/all_to_all | solution.py:29
  11.9 15.6 %collective-permute-start.3 = (bf16[64,2048]{1,0:T(8,128)(2,1)S(1)}, bf16[64,2048]{1,0:T(8,128)(2,1)S(1)}, u32[]{:S(2)}, u32[]{:S(2)}) collective-permute-start(bf16[64,2048]{1,0:T(8,128)(2,1)S(1)} %get-tuple-element.19), channel_id=1, source_target_pairs={{0,0},{1,5},{2,64},{3,69},{4,128},{5,133},{6,192},{7,197},{64,2},{... | collective-permute-start | bytes 786440 | tf_op jit(solution)/shard_map/ppermute | solution.py:241
  16.8 10.9 %collective-permute-start.5 = (bf16[64,2048]{1,0:T(8,128)(2,1)S(1)}, bf16[64,2048]{1,0:T(8,128)(2,1)S(1)}, u32[]{:S(2)}, u32[]{:S(2)}) collective-permute-start(bf16[64,2048]{1,0:T(8,128)(2,1)S(1)} %get-tuple-element.20), channel_id=1, source_target_pairs={{0,2},{1,7},{2,66},{3,71},{4,130},{5,135},{6,194},{7,199},{64,4},{... | collective-permute-start | bytes 786440 | tf_op jit(solution)/shard_map/ppermute | solution.py:241
  19.4 20.6 %all-to-all-start.1 = ((bf16[8,64,256]{2,1,0:T(8,128)(2,1)}), bf16[8,64,256]{2,1,0:T(8,128)(2,1)S(1)}, u32[]{:S(2)}, u32[]{:S(2)}) async-start(bf16[8,64,256]{2,1,0:T(8,128)(2,1)} %broadcast_in_dim.41), calls=%async_computation.1 | async-start | bytes 524288 | tf_op jit(solution)/shard_map/all_to_all | solution.py:29
  27.6 12.5 %collective-permute-start.4 = (bf16[64,2048]{1,0:T(8,128)(2,1)S(1)}, bf16[64,2048]{1,0:T(8,128)(2,1)S(1)}, u32[]{:S(2)}, u32[]{:S(2)}) collective-permute-start(bf16[64,2048]{1,0:T(8,128)(2,1)S(1)} %collective-permute-done.3), channel_id=1, source_target_pairs={{0,1},{1,0},{2,3},{3,2},{4,5},{5,4},{6,7},{7,6},{8,9},{9,8},{10,11... | collective-permute-start | bytes 786440 | tf_op jit(solution)/shard_map/ppermute | solution.py:242
  27.7 12.4 %collective-permute-start.6 = (bf16[64,2048]{1,0:T(8,128)(2,1)S(1)}, bf16[64,2048]{1,0:T(8,128)(2,1)}, u32[]{:S(2)}, u32[]{:S(2)}) collective-permute-start(bf16[64,2048]{1,0:T(8,128)(2,1)S(1)} %collective-permute-done.5), channel_id=1, source_target_pairs={{0,1},{1,0},{2,3},{3,2},{4,5},{5,4},{6,7},{7,6},{8,9},{9,8},{10,11... | collective-permute-start | bytes 786440 | tf_op jit(solution)/shard_map/ppermute | solution.py:242
  175.8 22.1 %collective-permute-start.7 = (bf16[64,1024]{1,0:T(8,128)(2,1)S(1)}, bf16[64,1024]{1,0:T(8,128)(2,1)S(1)}, u32[]{:S(2)}, u32[]{:S(2)}) collective-permute-start(bf16[64,1024]{1,0:T(8,128)(2,1)S(1)} %slice.55), channel_id=1, source_target_pairs={{0,1},{1,0},{2,3},{3,2},{4,5},{5,4},{6,7},{7,6},{8,9},{9,8},{10,11... | collective-permute-start | bytes 393224 | tf_op jit(solution)/shard_map/ppermute | solution.py:284

commit v10 on v9

--- a/solution.py
+++ b/solution.py
@@ -156,11 +156,19 @@
     )(on_chip(arrived), on_chip(slope))
 
 
-def normalized_panels(core, arrived, image, there):
+def normalized_panels(arrived, image, there):
     rank, width = there.shape
 
-    def kernel(core_ref, arrived_ref, image_ref, there_ref, out_ref):
-        here_at = core_ref[0]
+    def times(inverse, panel):
+        high = inverse.astype(BF16)
+        rest = inverse - high.astype(F32)
+        middle = rest.astype(BF16)
+        low = (rest - middle.astype(F32)).astype(BF16)
+        products = dot_n(jnp.concatenate([high, middle, low]), panel)
+        return products[:rank] + (products[rank : 2 * rank] + products[2 * rank :])
+
+    def kernel(arrived_ref, image_ref, there_ref, out_ref, result, sems):
+        here_at = lax.axis_index("core")
         inverses = []
         for b in (here_at, 1 - here_at):
             gram = arrived_ref[pl.ds(b, 1)][0].astype(F32)
@@ -168,18 +176,23 @@
                 gram = gram + arrived_ref[pl.ds(i + b, 1)][0].astype(F32)
             inverses.append(gram[:, :rank] + gram[:, rank:])
         inverses = inverse_factors(inverses)
-        here = exact_dot(inverses[0], image_ref[:, :width].astype(F32))
-        out_ref[pl.ds(here_at, 1)] = here[None]
-        away = exact_dot(inverses[1], there_ref[...].astype(F32))
-        out_ref[pl.ds(1 - here_at, 1)] = away[None]
+        result[0] = times(inverses[0], image_ref[:, :width])
+        first = pltpu.make_async_copy(result.at[0], out_ref.at[here_at], sems.at[0])
+        first.start()
+        result[1] = times(inverses[1], there_ref[...])
+        second = pltpu.make_async_copy(result.at[1], out_ref.at[1 - here_at], sems.at[1])
+        second.start()
+        first.wait()
+        second.wait()
 
     return pl.pallas_call(
         kernel,
-        in_specs=[pl.BlockSpec(memory_space=pltpu.SMEM)] + [WHOLE] * 3,
-        out_specs=WHOLE,
+        in_specs=[WHOLE] * 3,
+        out_specs=pl.BlockSpec(memory_space=pltpu.HBM),
         out_shape=jax.ShapeDtypeStruct((2, rank, width), F32),
+        scratch_shapes=[pltpu.VMEM((2, rank, width), F32), pltpu.SemaphoreType.DMA((2,))],
         name="normalized_panels",
-    )(core, on_chip(arrived), on_chip(image), on_chip(there))
+    )(on_chip(arrived), on_chip(image), on_chip(there))
 
 
 def three_parts(x):
@@ -205,6 +218,7 @@
         for e in range(share)
     ]
     flip = [(0, 1), (1, 0)]
+    near, far = [(i, i ^ 1) for i in range(n_x)], [(i, n_x - 1 - i) for i in range(n_x)]
 
     def on_device(weights, preact, panel):
         core = lax.axis_index("core")
@@ -270,7 +284,10 @@
             partial_in = dot_n(weighted, w2).astype(BF16)
             blocks = jnp.moveaxis(partial_in.reshape(rank, n_z, width_row), 1, 0)
             summed = total(exchange(blocks, "z")).astype(BF16)
-            cotangent = total(to_all(summed, "x", n_x)).astype(BF16)
+            for step in (near, far):
+                there = lax.ppermute(summed, "x", step)
+                summed = (summed.astype(F32) + there.astype(F32)).astype(BF16)
+            cotangent = summed
             weighted = (slope_1 * cotangent.astype(F32)).astype(BF16)
             partial_in = dot_n(weighted, w1).astype(BF16)
             groups = rank // 8
@@ -283,7 +300,7 @@
             image = jnp.moveaxis(image, 1, 2).reshape(rank, 2 * width_in)
         there = lax.ppermute(image[:, width_in:], "core", flip)
         arrived = to_all(high_low(dot_t(image, image)), ("x", "core"), 2 * n_x)
-        return normalized_panels(core.reshape(1).astype(jnp.int32), arrived, image, there)
+        return normalized_panels(arrived, image, there)
 
     return on_device
 

time: 202 us -> 205 us (1.015)
  blocking collectives: 137 us -> 124 us
  waiting for transfers between devices: 12.2 us -> 24.6 us
  starting transfers between devices: 37.1 us -> 41.1 us
    all_to_all x13 -> x11, blocking collectives: 137 us -> 124 us  [exchange(): return lax.all_to_all(tiles, axis, split_axis=0, concat_axis=0, tiled=True)]
    ppermute x0 -> x4, waiting for transfers between devices: none -> 12.4 us  [on_device(): there = lax.ppermute(summed, 'x', step)]
    ppermute x1, starting transfers between devices: 14.4 us -> 16.6 us  [on_device(): there = lax.ppermute(image[:, width_in:], 'core', flip)]
  transfers between devices with their start and end apart: 10 -> 14, of which waited for: 2 -> 6; matrix products, arithmetic and copies ran while one was open for 1% -> 1% of each run, Pallas kernels for 1% -> 1%
where the time goes in v10:
time: 205 us; the launch traced here: 204 us
  blocking collectives  124 us (60%)
  starting transfers between devices  41.1 us (20%)
  waiting for transfers between devices  24.6 us (12%)
  Pallas kernels  6.09 us (3%)
  local copies, waits for them, and re-layouts  3.28 us (2%)
  matrix products  2.97 us (1%)
    all_to_all x11, blocking collectives, exchange(): return lax.all_to_all(tiles, axis, split_axis=0, concat_axis=0, tiled=True)  124 us
    ppermute x1, starting transfers between devices, on_device(): there = lax.ppermute(image[:, width_in:], 'core', flip)  16.6 us
    ppermute x4, waiting for transfers between devices, on_device(): there = lax.ppermute(summed, 'x', step)  12.4 us
    all_to_all x2, waiting for transfers between devices, exchange(): return lax.all_to_all(tiles, axis, split_axis=0, concat_axis=0, tiled=True)  11.6 us
    all_to_all x2, starting transfers between devices, exchange(): return lax.all_to_all(tiles, axis, split_axis=0, concat_axis=0, tiled=True)  11.5 us
    ppermute x2, starting transfers between devices, on_device(): here.append(lax.ppermute(rows[e], ('y', 'x', 'core'), turns[e]))  6.65 us
  transfers between devices with their start and end apart: 14, of which 6 were waited for; matrix products, arithmetic and copies ran while one was open for 1% of the time, Pallas kernels for 1%

profile of v10, /device:TPU:1, one launch (start us, length us, event | category | flops | bytes accessed | tf_op | source)
XLA Modules:
  0.0 204.1 jit_solution(8694770753524592294)
XLA Ops:
  0.0 1.3 fusion.9
  1.3 0.0 copy-start
  1.4 3.3 %collective-permute-start.2 = (bf16[128,1024]{1,0:T(8,128)(2,1)S(1)}, bf16[128,1024]{1,0:T(8,128)(2,1)S(1)}, u32[]{:S(2)}, u32[]{:S(2)}) collective-permute-start(bf16[128,1024]{1,0:T(8,128)(2,1)S(1)} %pad_maximum_fusion.4), channel_id=1, source_target_pairs={{0,1},{1,0},{2,3},{3,2},{4,5},{5,4},{6,7},{7,6},{8,9},{9,8},{10,11... | collective-permute-start | bytes 786440 | tf_op jit(solution)/shard_map/ppermute | solution.py:250
  4.7 0.1 collective-permute-start.1
  4.8 1.6 first_partial.1
  6.3 0.5 collective-permute-start
  6.9 0.1 fusion.8
  7.0 0.1 iota.9
  7.0 0.1 iota.10
  7.1 0.1 broadcast_in_dim.40
  7.2 0.5 collective-permute-done
  7.8 0.7 broadcast_in_dim.36
  8.4 3.3 %all-to-all-start = ((bf16[4,64,256]{2,1,0:T(8,128)(2,1)}), bf16[4,64,256]{2,1,0:T(8,128)(2,1)S(1)}, u32[]{:S(2)}, u32[]{:S(2)}) async-start(bf16[4,64,256]{2,1,0:T(8,128)(2,1)} %broadcast_in_dim.36), calls=%async_computation | async-start | bytes 262144 | tf_op jit(solution)/shard_map/all_to_all | solution.py:29
  11.8 0.0 collective-permute-done.2
  11.8 0.1 broadcast_select_fusion.1
  11.9 4.8 %collective-permute-start.3 = (bf16[64,2048]{1,0:T(8,128)(2,1)S(1)}, bf16[64,2048]{1,0:T(8,128)(2,1)S(1)}, u32[]{:S(2)}, u32[]{:S(2)}) collective-permute-start(bf16[64,2048]{1,0:T(8,128)(2,1)S(1)} %get-tuple-element.19), channel_id=1, source_target_pairs={{0,0},{1,5},{2,64},{3,69},{4,128},{5,133},{6,192},{7,197},{64,2},{... | collective-permute-start | bytes 786440 | tf_op jit(solution)/shard_map/ppermute | solution.py:255
  16.8 1.8 collective-permute-start.5
  18.6 0.7 broadcast_in_dim.37
  19.4 8.2 %all-to-all-start.1 = ((bf16[8,64,256]{2,1,0:T(8,128)(2,1)}), bf16[8,64,256]{2,1,0:T(8,128)(2,1)S(1)}, u32[]{:S(2)}, u32[]{:S(2)}) async-start(bf16[8,64,256]{2,1,0:T(8,128)(2,1)} %broadcast_in_dim.37), calls=%async_computation.1 | async-start | bytes 524288 | tf_op jit(solution)/shard_map/all_to_all | solution.py:29
  27.5 0.0 collective-permute-done.3
  27.6 0.1 collective-permute-start.4
  27.7 0.6 collective-permute-start.6
  28.2 0.0 collective-permute-done.1
  28.3 0.1 pad_maximum_fusion
  28.3 11.6 %all-to-all-done.1 = bf16[8,64,256]{2,1,0:T(8,128)(2,1)S(1)} async-done(((bf16[8,64,256]{2,1,0:T(8,128)(2,1)}), bf16[8,64,256]{2,1,0:T(8,128)(2,1)S(1)}, u32[]{:S(2)}, u32[]{:S(2)}) %all-to-all-start.1) | async-done | bytes 262176 | tf_op jit(solution)/shard_map/all_to_all | solution.py:29
  40.0 0.0 collective-permute-done.4
  40.1 1.0 broadcast_select_fusion.4
  41.1 0.1 pad_maximum_fusion.1
  41.1 0.4 convolution_convert_fusion.6
  41.6 8.5 %all_to_all.65 = bf16[4,72,256]{2,1,0:T(8,128)(2,1)S(1)} all-to-all(bf16[4,72,256]{2,1,0:T(8,128)(2,1)S(1)} %broadcast_in_dim.43), channel_id=1, replica_groups=mesh['y'=4,'z'=8,'x'=4,'core'=2] {'y'}, dimensions={0} | all-to-all | bytes 294912 | tf_op jit(solution)/shard_map/all_to_all | solution.py:29
  50.2 0.3 convolution_convert_fusion.3
  50.5 11.9 %all_to_all.66 = bf16[8,64,256]{2,1,0:T(8,128)(2,1)S(1)} all-to-all(bf16[8,64,256]{2,1,0:T(8,128)(2,1)S(1)} %bitcast.77), channel_id=1, replica_groups=mesh['y'=4,'z'=8,'x'=4,'core'=2] {'z'}, dimensions={0} | all-to-all | bytes 524288 | tf_op jit(solution)/shard_map/all_to_all | solution.py:29
  62.5 0.1 collective-permute-start.7
  62.6 2.8 %collective-permute-done.7 = bf16[64,256]{1,0:T(8,128)(2,1)S(1)} collective-permute-done((bf16[64,256]{1,0:T(8,128)(2,1)S(1)}, bf16[64,256]{1,0:T(8,128)(2,1)S(1)}, u32[]{:S(2)}, u32[]{:S(2)}) %collective-permute-start.7) | collective-permute-done | bytes 32800 | tf_op jit(solution)/shard_map/ppermute | solution.py:288
  65.4 0.1 collective-permute-start.8
  65.5 4.0 %collective-permute-done.8 = bf16[64,256]{1,0:T(8,128)(2,1)S(1)} collective-permute-done((bf16[64,256]{1,0:T(8,128)(2,1)S(1)}, bf16[64,256]{1,0:T(8,128)(2,1)S(1)}, u32[]{:S(2)}, u32[]{:S(2)}) %collective-permute-start.8) | collective-permute-done | bytes 32800 | tf_op jit(solution)/shard_map/ppermute | solution.py:288
  69.4 0.3 convolution_convert_fusion.2
  69.7 14.1 %all_to_all.67 = bf16[32,8,512]{2,1,0:T(8,128)(2,1)S(1)} all-to-all(bf16[32,8,512]{2,1,0:T(8,128)(2,1)S(1)} %bitcast.83), channel_id=1, replica_groups=mesh['y'=4,'z'=8,'x'=4,'core'=2] {'y','z'}, dimensions={0} | all-to-all | bytes 524288 | tf_op jit(solution)/shard_map/all_to_all | solution.py:29
  83.8 0.1 reduce_sum.92
  83.9 14.1 %all_to_all.68 = bf16[32,8,512]{2,1,0:T(8,128)(2,1)S(1)} all-to-all(bf16[32,8,512]{2,1,0:T(8,128)(2,1)S(1)} %broadcast_in_dim.44), channel_id=1, replica_groups=mesh['y'=4,'z'=8,'x'=4,'core'=2] {'y','z'}, dimensions={0} | all-to-all | bytes 524288 | tf_op jit(solution)/shard_map/all_to_all | solution.py:29
  98.0 0.4 convolution_convert_fusion.5
  98.5 0.2 reduce-precision_convert_fusion.1
  98.7 0.1 pad_maximum_fusion.5
  98.8 7.5 %all_to_all.69.arrived_ref = bf16[4,64,384]{2,1,0:T(8,128)(2,1)S(1)} all-to-all(bf16[4,64,384]{2,1,0:T(8,128)(2,1)S(1)} %broadcast_in_dim.45), channel_id=1, replica_groups=mesh['y'=4,'z'=8,'x'=4,'core'=2] {'x'}, dimensions={0} | all-to-all | bytes 393216 | tf_op jit(solution)/shard_map/all_to_all | solution.py:29
  106.3 1.7 normalized_forward.1
  108.1 12.4 %all_to_all.70 = bf16[8,64,256]{2,1,0:T(8,128)(2,1)S(1)} all-to-all(bf16[8,64,256]{2,1,0:T(8,128)(2,1)S(1)} %broadcast_in_dim.46), channel_id=1, replica_groups=mesh['y'=4,'z'=8,'x'=4,'core'=2] {'z'}, dimensions={0} | all-to-all | bytes 524288 | tf_op jit(solution)/shard_map/all_to_all | solution.py:29
  120.5 0.4 convolution_convert_fusion.4
  120.9 7.5 %all_to_all.71 = bf16[4,64,256]{2,1,0:T(8,128)(2,1)S(1)} all-to-all(bf16[4,64,256]{2,1,0:T(8,128)(2,1)S(1)} %broadcast_in_dim.86), channel_id=1, replica_groups=mesh['y'=4,'z'=8,'x'=4,'core'=2] {'y'}, dimensions={0} | all-to-all | bytes 262144 | tf_op jit(solution)/shard_map/all_to_all | solution.py:29
  128.5 0.3 convolution_convert_fusion.1
  128.8 11.7 %all_to_all.72 = bf16[8,64,256]{2,1,0:T(8,128)(2,1)S(1)} all-to-all(bf16[8,64,256]{2,1,0:T(8,128)(2,1)S(1)} %bitcast.79), channel_id=1, replica_groups=mesh['y'=4,'z'=8,'x'=4,'core'=2] {'z'}, dimensions={0} | all-to-all | bytes 524288 | tf_op jit(solution)/shard_map/all_to_all | solution.py:29
  140.6 0.4 collective-permute-start.9
  141.0 2.5 %collective-permute-done.9 = bf16[64,256]{1,0:T(8,128)(2,1)S(1)} collective-permute-done((bf16[64,256]{1,0:T(8,128)(2,1)S(1)}, bf16[64,256]{1,0:T(8,128)(2,1)S(1)}, u32[]{:S(2)}, u32[]{:S(2)}) %collective-permute-start.9) | collective-permute-done | bytes 32800 | tf_op jit(solution)/shard_map/ppermute | solution.py:288
  143.5 1.2 collective-permute-start.10
  144.6 3.2 %collective-permute-done.10 = bf16[64,256]{1,0:T(8,128)(2,1)S(1)} collective-permute-done((bf16[64,256]{1,0:T(8,128)(2,1)S(1)}, bf16[64,256]{1,0:T(8,128)(2,1)S(1)}, u32[]{:S(2)}, u32[]{:S(2)}) %collective-permute-start.10) | collective-permute-done | bytes 32800 | tf_op jit(solution)/shard_map/ppermute | solution.py:288
  147.8 0.3 convolution_convert_fusion
  148.1 12.6 %all_to_all.73 = bf16[32,8,512]{2,1,0:T(8,128)(2,1)S(1)} all-to-all(bf16[32,8,512]{2,1,0:T(8,128)(2,1)S(1)} %bitcast.81), channel_id=1, replica_groups=mesh['y'=4,'z'=8,'x'=4,'core'=2] {'y','z'}, dimensions={0} | all-to-all | bytes 524288 | tf_op jit(solution)/shard_map/all_to_all | solution.py:29
  160.8 0.1 reduce_sum.95
  160.8 15.7 %all_to_all.74 = bf16[32,8,512]{2,1,0:T(8,128)(2,1)S(1)} all-to-all(bf16[32,8,512]{2,1,0:T(8,128)(2,1)S(1)} %broadcast_in_dim.87), channel_id=1, replica_groups=mesh['y'=4,'z'=8,'x'=4,'core'=2] {'y','z'}, dimensions={0} | all-to-all | bytes 524288 | tf_op jit(solution)/shard_map/all_to_all | solution.py:29
  176.6 0.2 reduce-precision_convert_fusion
  176.8 16.6 %collective-permute-start.11 = (bf16[64,1024]{1,0:T(8,128)(2,1)S(1)}, bf16[64,1024]{1,0:T(8,128)(2,1)S(1)}, u32[]{:S(2)}, u32[]{:S(2)}) collective-permute-start(bf16[64,1024]{1,0:T(8,128)(2,1)S(1)} %slice.55), channel_id=1, source_target_pairs={{0,1},{1,0},{2,3},{3,2},{4,5},{5,4},{6,7},{7,6},{8,9},{9,8},{10,11... | collective-permute-start | bytes 393224 | tf_op jit(solution)/shard_map/ppermute | solution.py:301
  193.4 0.1 pad_maximum_fusion.6
  193.5 7.6 %all_to_all.75.arrived_ref = bf16[8,64,128]{2,1,0:T(8,128)(2,1)S(1)} all-to-all(bf16[8,64,128]{2,1,0:T(8,128)(2,1)S(1)} %broadcast_in_dim.88), channel_id=1, replica_groups=mesh['y'=4,'z'=8,'x'=4,'core'=2] {'x','core'}, dimensions={0} | all-to-all | bytes 262144 | tf_op jit(solution)/shard_map/all_to_all | solution.py:29
  201.2 0.0 collective-permute-done.11.there_ref
  201.2 2.8 %normalized_panels.1 = f32[2,64,1024]{2,1,0:T(8,128)} custom-call(bf16[8,64,128]{2,1,0:T(8,128)(2,1)S(1)} %all_to_all.75.arrived_ref, bf16[64,2048]{1,0:T(8,128)(2,1)S(1)} %bitcast.73, bf16[64,1024]{1,0:T(8,128)(2,1)S(1)} %collective-permute-done.11.there_ref), custom_call_target="tpu_custom_call" | custom-call | tf_op jit(solution)/shard_map/normalized_panels/pallas_call | solution.py:188
  (37 shorter events, 0.6 us)
Async XLA Ops:
  1.3 5.5 %copy-start = (f32[2,2,256]{2,1,0:T(2,128)S(1)}, f32[2,2,256]{2,1,0:T(2,128)}, u32[]{:S(2)}) copy-start(f32[2,2,256]{2,1,0:T(2,128)} %param.4) | copy-start | bytes 12292
  1.4 10.4 %collective-permute-start.2 = (bf16[128,1024]{1,0:T(8,128)(2,1)S(1)}, bf16[128,1024]{1,0:T(8,128)(2,1)S(1)}, u32[]{:S(2)}, u32[]{:S(2)}) collective-permute-start(bf16[128,1024]{1,0:T(8,128)(2,1)S(1)} %pad_maximum_fusion.4), channel_id=1, source_target_pairs={{0,1},{1,0},{2,3},{3,2},{4,5},{5,4},{6,7},{7,6},{8,9},{9,8},{10,11... | collective-permute-start | bytes 786440 | tf_op jit(solution)/shard_map/ppermute | solution.py:250
  4.7 23.6 %collective-permute-start.1 = (bf16[256,1024]{1,0:T(8,128)(2,1)S(1)}, bf16[256,1024]{1,0:T(8,128)(2,1)S(1)}, u32[]{:S(2)}, u32[]{:S(2)}) collective-permute-start(bf16[256,1024]{1,0:T(8,128)(2,1)S(1)} %get-tuple-element.14), channel_id=1, source_target_pairs={{0,1},{1,0},{2,3},{3,2},{4,5},{5,4},{6,7},{7,6},{8,9},{9,8},{10,11... | collective-permute-start | bytes 1572872 | tf_op jit(solution)/shard_map/ppermute | solution.py:260
  6.3 1.4 collective-permute-start
  8.4 8.4 %all-to-all-start = ((bf16[4,64,256]{2,1,0:T(8,128)(2,1)}), bf16[4,64,256]{2,1,0:T(8,128)(2,1)S(1)}, u32[]{:S(2)}, u32[]{:S(2)}) async-start(bf16[4,64,256]{2,1,0:T(8,128)(2,1)} %broadcast_in_dim.36), calls=%async_computation | async-start | bytes 262144 | tf_op jit(solution)/shard_map/all_to_all | solution.py:29
  11.9 15.6 %collective-permute-start.3 = (bf16[64,2048]{1,0:T(8,128)(2,1)S(1)}, bf16[64,2048]{1,0:T(8,128)(2,1)S(1)}, u32[]{:S(2)}, u32[]{:S(2)}) collective-permute-start(bf16[64,2048]{1,0:T(8,128)(2,1)S(1)} %get-tuple-element.19), channel_id=1, source_target_pairs={{0,0},{1,5},{2,64},{3,69},{4,128},{5,133},{6,192},{7,197},{64,2},{... | collective-permute-start | bytes 786440 | tf_op jit(solution)/shard_map/ppermute | solution.py:255
  16.8 10.9 %collective-permute-start.5 = (bf16[64,2048]{1,0:T(8,128)(2,1)S(1)}, bf16[64,2048]{1,0:T(8,128)(2,1)S(1)}, u32[]{:S(2)}, u32[]{:S(2)}) collective-permute-start(bf16[64,2048]{1,0:T(8,128)(2,1)S(1)} %get-tuple-element.20), channel_id=1, source_target_pairs={{0,2},{1,7},{2,66},{3,71},{4,130},{5,135},{6,194},{7,199},{64,4},{... | collective-permute-start | bytes 786440 | tf_op jit(solution)/shard_map/ppermute | solution.py:255
  19.4 20.6 %all-to-all-start.1 = ((bf16[8,64,256]{2,1,0:T(8,128)(2,1)}), bf16[8,64,256]{2,1,0:T(8,128)(2,1)S(1)}, u32[]{:S(2)}, u32[]{:S(2)}) async-start(bf16[8,64,256]{2,1,0:T(8,128)(2,1)} %broadcast_in_dim.37), calls=%async_computation.1 | async-start | bytes 524288 | tf_op jit(solution)/shard_map/all_to_all | solution.py:29
  27.6 12.5 %collective-permute-start.4 = (bf16[64,2048]{1,0:T(8,128)(2,1)S(1)}, bf16[64,2048]{1,0:T(8,128)(2,1)S(1)}, u32[]{:S(2)}, u32[]{:S(2)}) collective-permute-start(bf16[64,2048]{1,0:T(8,128)(2,1)S(1)} %collective-permute-done.3), channel_id=1, source_target_pairs={{0,1},{1,0},{2,3},{3,2},{4,5},{5,4},{6,7},{7,6},{8,9},{9,8},{10,11... | collective-permute-start | bytes 786440 | tf_op jit(solution)/shard_map/ppermute | solution.py:256
  27.7 12.4 %collective-permute-start.6 = (bf16[64,2048]{1,0:T(8,128)(2,1)S(1)}, bf16[64,2048]{1,0:T(8,128)(2,1)}, u32[]{:S(2)}, u32[]{:S(2)}) collective-permute-start(bf16[64,2048]{1,0:T(8,128)(2,1)S(1)} %collective-permute-done.5), channel_id=1, source_target_pairs={{0,1},{1,0},{2,3},{3,2},{4,5},{5,4},{6,7},{7,6},{8,9},{9,8},{10,11... | collective-permute-start | bytes 786440 | tf_op jit(solution)/shard_map/ppermute | solution.py:256
  62.5 2.9 %collective-permute-start.7 = (bf16[64,256]{1,0:T(8,128)(2,1)S(1)}, bf16[64,256]{1,0:T(8,128)(2,1)S(1)}, u32[]{:S(2)}, u32[]{:S(2)}) collective-permute-start(bf16[64,256]{1,0:T(8,128)(2,1)S(1)} %reduce_sum.91), channel_id=1, source_target_pairs={{0,2},{2,0},{4,6},{6,4},{1,3},{3,1},{5,7},{7,5},{8,10},{10,8},{12,... | collective-permute-start | bytes 98312 | tf_op jit(solution)/shard_map/ppermute | solution.py:288
  65.4 4.1 %collective-permute-start.8 = (bf16[64,256]{1,0:T(8,128)(2,1)S(1)}, bf16[64,256]{1,0:T(8,128)(2,1)S(1)}, u32[]{:S(2)}, u32[]{:S(2)}) collective-permute-start(bf16[64,256]{1,0:T(8,128)(2,1)S(1)} %add_convert_fusion.3), channel_id=1, source_target_pairs={{0,6},{2,4},{4,2},{6,0},{1,7},{3,5},{5,3},{7,1},{8,14},{10,12},{12... | collective-permute-start | bytes 98312 | tf_op jit(solution)/shard_map/ppermute | solution.py:288
  140.6 2.9 %collective-permute-start.9 = (bf16[64,256]{1,0:T(8,128)(2,1)S(1)}, bf16[64,256]{1,0:T(8,128)(2,1)S(1)}, u32[]{:S(2)}, u32[]{:S(2)}) collective-permute-start(bf16[64,256]{1,0:T(8,128)(2,1)S(1)} %reduce_sum.94), channel_id=1, source_target_pairs={{0,2},{2,0},{4,6},{6,4},{1,3},{3,1},{5,7},{7,5},{8,10},{10,8},{12,... | collective-permute-start | bytes 98312 | tf_op jit(solution)/shard_map/ppermute | solution.py:288
  143.5 4.4 %collective-permute-start.10 = (bf16[64,256]{1,0:T(8,128)(2,1)S(1)}, bf16[64,256]{1,0:T(8,128)(2,1)S(1)}, u32[]{:S(2)}, u32[]{:S(2)}) collective-permute-start(bf16[64,256]{1,0:T(8,128)(2,1)S(1)} %add_convert_fusion.1), channel_id=1, source_target_pairs={{0,6},{2,4},{4,2},{6,0},{1,7},{3,5},{5,3},{7,1},{8,14},{10,12},{12... | collective-permute-start | bytes 98312 | tf_op jit(solution)/shard_map/ppermute | solution.py:288
  176.8 24.4 %collective-permute-start.11 = (bf16[64,1024]{1,0:T(8,128)(2,1)S(1)}, bf16[64,1024]{1,0:T(8,128)(2,1)S(1)}, u32[]{:S(2)}, u32[]{:S(2)}) collective-permute-start(bf16[64,1024]{1,0:T(8,128)(2,1)S(1)} %slice.55), channel_id=1, source_target_pairs={{0,1},{1,0},{2,3},{3,2},{4,5},{5,4},{6,7},{7,6},{8,9},{9,8},{10,11... | collective-permute-start | bytes 393224 | tf_op jit(solution)/shard_map/ppermute | solution.py:301

commit v11 on v10

--- a/solution.py
+++ b/solution.py
@@ -100,7 +100,7 @@
 
 
 def gram_of_parts(parts_ref, start, rank):
-    parts = [parts_ref[i, :, start : start + 2 * rank].astype(F32) for i in range(parts_ref.shape[0])]
+    parts = [parts_ref[i, :rank, start : start + 2 * rank].astype(F32) for i in range(parts_ref.shape[0])]
     summed = parts[0]
     for part in parts[1:]:
         summed = summed + part
@@ -138,13 +138,13 @@
 
 
 def normalized_forward(arrived, slope, width):
-    count, rank, _ = arrived.shape
+    count, rank = arrived.shape[0], arrived.shape[1] - 8
 
     def kernel(arrived_ref, slope_ref, out_ref):
         (inverse,) = inverse_factors([gram_of_parts(arrived_ref, width, rank)])
-        summed = arrived_ref[0, :, :width].astype(F32)
+        summed = arrived_ref[0, :rank, :width].astype(F32)
         for i in range(1, count):
-            summed = summed + arrived_ref[i, :, :width].astype(F32)
+            summed = summed + arrived_ref[i, :rank, :width].astype(F32)
         out_ref[...] = (slope_ref[...] * exact_dot(inverse, summed)).astype(BF16)
 
     return pl.pallas_call(
@@ -218,7 +218,6 @@
         for e in range(share)
     ]
     flip = [(0, 1), (1, 0)]
-    near, far = [(i, i ^ 1) for i in range(n_x)], [(i, n_x - 1 - i) for i in range(n_x)]
 
     def on_device(weights, preact, panel):
         core = lax.axis_index("core")
@@ -266,8 +265,10 @@
                 arrived = to_all(summed_out.astype(BF16), "x", n_x)
                 forward = (slope_1 * total(arrived)).astype(BF16)
             else:
+                paced = lax.ppermute(image[:8, : width_row + 2 * rank], "core", flip)
                 partial_out = dot_t(image, w1).astype(BF16)
                 message = jnp.concatenate([partial_out, high_low(dot_t(image, image))], axis=1)
+                message = jnp.concatenate([message, paced])
                 arrived = to_all(message, "x", n_x)
                 forward = normalized_forward(arrived, slope_1, width_row)
             spread = to_all(forward, "z", n_z)
@@ -284,10 +285,7 @@
             partial_in = dot_n(weighted, w2).astype(BF16)
             blocks = jnp.moveaxis(partial_in.reshape(rank, n_z, width_row), 1, 0)
             summed = total(exchange(blocks, "z")).astype(BF16)
-            for step in (near, far):
-                there = lax.ppermute(summed, "x", step)
-                summed = (summed.astype(F32) + there.astype(F32)).astype(BF16)
-            cotangent = summed
+            cotangent = total(to_all(summed, "x", n_x)).astype(BF16)
             weighted = (slope_1 * cotangent.astype(F32)).astype(BF16)
             partial_in = dot_n(weighted, w1).astype(BF16)
             groups = rank // 8

time: 205 us -> 203 us (level)
  blocking collectives: 124 us -> 138 us
  waiting for transfers between devices: 24.6 us -> 12.8 us
  starting transfers between devices: 41.1 us -> 36.7 us
    all_to_all x11 -> x13, blocking collectives: 124 us -> 138 us  [exchange(): return lax.all_to_all(tiles, axis, split_axis=0, concat_axis=0, tiled=True)]
    ppermute x4 -> x1, waiting for transfers between devices: 12.4 us -> 0.6 us  [on_device(): paced = lax.ppermute(image[:8, :width_row + 2 * rank], 'core', flip)]
    ppermute x1, starting transfers between devices: 16.6 us -> 8.54 us  [on_device(): there = lax.ppermute(image[:, width_in:], 'core', flip)]
    ppermute x4 -> x1, starting transfers between devices: 1.71 us -> 5.42 us  [on_device(): paced = lax.ppermute(image[:8, :width_row + 2 * rank], 'core', flip)]
  transfers between devices with their start and end apart: 14 -> 11, of which waited for: 6 -> 3; matrix products, arithmetic and copies ran while one was open for 1% -> 1% of each run, Pallas kernels for 1% -> 1%
where the time goes in v11:
time: 203 us; the launch traced here: 202 us
  blocking collectives  138 us (68%)
  starting transfers between devices  36.7 us (18%)
  waiting for transfers between devices  12.8 us (6%)
  Pallas kernels  6.08 us (3%)
  local copies, waits for them, and re-layouts  3.3 us (2%)
  matrix products  2.97 us (1%)
    all_to_all x13, blocking collectives, exchange(): return lax.all_to_all(tiles, axis, split_axis=0, concat_axis=0, tiled=True)  138 us
    all_to_all x2, waiting for transfers between devices, exchange(): return lax.all_to_all(tiles, axis, split_axis=0, concat_axis=0, tiled=True)  11.6 us
    all_to_all x2, starting transfers between devices, exchange(): return lax.all_to_all(tiles, axis, split_axis=0, concat_axis=0, tiled=True)  11.5 us
    ppermute x1, starting transfers between devices, on_device(): there = lax.ppermute(image[:, width_in:], 'core', flip)  8.54 us
    ppermute x2, starting transfers between devices, on_device(): here.append(lax.ppermute(rows[e], ('y', 'x', 'core'), turns[e]))  6.65 us
    ppermute x1, starting transfers between devices, on_device(): paced = lax.ppermute(image[:8, :width_row + 2 * rank], 'core', flip)  5.42 us
  transfers between devices with their start and end apart: 11, of which 3 were waited for; matrix products, arithmetic and copies ran while one was open for 1% of the time, Pallas kernels for 1%

profile of v11, /device:TPU:1, one launch (start us, length us, event | category | flops | bytes accessed | tf_op | source)
XLA Modules:
  0.0 202.0 jit_solution(6181888186823165302)
XLA Ops:
  0.0 1.3 fusion.9
  1.3 0.0 copy-start
  1.4 3.3 %collective-permute-start.2 = (bf16[128,1024]{1,0:T(8,128)(2,1)S(1)}, bf16[128,1024]{1,0:T(8,128)(2,1)S(1)}, u32[]{:S(2)}, u32[]{:S(2)}) collective-permute-start(bf16[128,1024]{1,0:T(8,128)(2,1)S(1)} %pad_maximum_fusion.4), channel_id=1, source_target_pairs={{0,1},{1,0},{2,3},{3,2},{4,5},{5,4},{6,7},{7,6},{8,9},{9,8},{10,11... | collective-permute-start | bytes 786440 | tf_op jit(solution)/shard_map/ppermute | solution.py:249
  4.7 0.1 collective-permute-start.1
  4.8 1.6 first_partial.1
  6.3 0.5 collective-permute-start
  6.8 0.0 copy-done
  6.9 0.1 fusion.8
  7.0 0.1 iota.9
  7.0 0.1 iota.10
  7.1 0.1 broadcast_in_dim.44
  7.2 0.5 collective-permute-done
  7.8 0.7 broadcast_in_dim.40
  8.4 3.3 %all-to-all-start = ((bf16[4,64,256]{2,1,0:T(8,128)(2,1)}), bf16[4,64,256]{2,1,0:T(8,128)(2,1)S(1)}, u32[]{:S(2)}, u32[]{:S(2)}) async-start(bf16[4,64,256]{2,1,0:T(8,128)(2,1)} %broadcast_in_dim.40), calls=%async_computation | async-start | bytes 262144 | tf_op jit(solution)/shard_map/all_to_all | solution.py:29
  11.8 0.0 collective-permute-done.2
  11.8 0.1 broadcast_select_fusion.1
  11.9 4.8 %collective-permute-start.3 = (bf16[64,2048]{1,0:T(8,128)(2,1)S(1)}, bf16[64,2048]{1,0:T(8,128)(2,1)S(1)}, u32[]{:S(2)}, u32[]{:S(2)}) collective-permute-start(bf16[64,2048]{1,0:T(8,128)(2,1)S(1)} %get-tuple-element.19), channel_id=1, source_target_pairs={{0,0},{1,5},{2,64},{3,69},{4,128},{5,133},{6,192},{7,197},{64,2},{... | collective-permute-start | bytes 786440 | tf_op jit(solution)/shard_map/ppermute | solution.py:254
  16.8 0.0 all-to-all-done
  16.8 1.8 collective-permute-start.5
  18.6 0.7 broadcast_in_dim.41
  19.4 8.2 %all-to-all-start.1 = ((bf16[8,64,256]{2,1,0:T(8,128)(2,1)}), bf16[8,64,256]{2,1,0:T(8,128)(2,1)S(1)}, u32[]{:S(2)}, u32[]{:S(2)}) async-start(bf16[8,64,256]{2,1,0:T(8,128)(2,1)} %broadcast_in_dim.41), calls=%async_computation.1 | async-start | bytes 524288 | tf_op jit(solution)/shard_map/all_to_all | solution.py:29
  27.5 0.0 collective-permute-done.3
  27.6 0.1 collective-permute-start.4
  27.7 0.0 collective-permute-done.5
  27.7 0.6 collective-permute-start.6
  28.2 0.0 collective-permute-done.1
  28.3 0.1 pad_maximum_fusion
  28.3 11.6 %all-to-all-done.1 = bf16[8,64,256]{2,1,0:T(8,128)(2,1)S(1)} async-done(((bf16[8,64,256]{2,1,0:T(8,128)(2,1)}), bf16[8,64,256]{2,1,0:T(8,128)(2,1)S(1)}, u32[]{:S(2)}, u32[]{:S(2)}) %all-to-all-start.1) | async-done | bytes 262176 | tf_op jit(solution)/shard_map/all_to_all | solution.py:29
  40.0 0.0 collective-permute-done.4
  40.1 0.0 collective-permute-done.6
  40.1 1.0 broadcast_select_fusion.4
  41.1 0.1 pad_maximum_fusion.1
  41.2 0.4 convolution_convert_fusion.6
  41.7 8.5 %all_to_all.75 = bf16[4,72,256]{2,1,0:T(8,128)(2,1)S(1)} all-to-all(bf16[4,72,256]{2,1,0:T(8,128)(2,1)S(1)} %broadcast_in_dim.47), channel_id=1, replica_groups=mesh['y'=4,'z'=8,'x'=4,'core'=2] {'y'}, dimensions={0} | all-to-all | bytes 294912 | tf_op jit(solution)/shard_map/all_to_all | solution.py:29
  50.2 0.3 convolution_convert_fusion.3
  50.6 11.9 %all_to_all.76 = bf16[8,64,256]{2,1,0:T(8,128)(2,1)S(1)} all-to-all(bf16[8,64,256]{2,1,0:T(8,128)(2,1)S(1)} %bitcast.78), channel_id=1, replica_groups=mesh['y'=4,'z'=8,'x'=4,'core'=2] {'z'}, dimensions={0} | all-to-all | bytes 524288 | tf_op jit(solution)/shard_map/all_to_all | solution.py:29
  62.6 7.2 %all_to_all.77 = bf16[4,64,256]{2,1,0:T(8,128)(2,1)S(1)} all-to-all(bf16[4,64,256]{2,1,0:T(8,128)(2,1)S(1)} %broadcast_in_dim.48), channel_id=1, replica_groups=mesh['y'=4,'z'=8,'x'=4,'core'=2] {'x'}, dimensions={0} | all-to-all | bytes 262144 | tf_op jit(solution)/shard_map/all_to_all | solution.py:29
  69.8 0.3 convolution_convert_fusion.2
  70.1 14.1 %all_to_all.78 = bf16[32,8,512]{2,1,0:T(8,128)(2,1)S(1)} all-to-all(bf16[32,8,512]{2,1,0:T(8,128)(2,1)S(1)} %bitcast.85), channel_id=1, replica_groups=mesh['y'=4,'z'=8,'x'=4,'core'=2] {'y','z'}, dimensions={0} | all-to-all | bytes 524288 | tf_op jit(solution)/shard_map/all_to_all | solution.py:29
  84.2 0.1 reduce_sum.117
  84.3 14.1 %all_to_all.79 = bf16[32,8,512]{2,1,0:T(8,128)(2,1)S(1)} all-to-all(bf16[32,8,512]{2,1,0:T(8,128)(2,1)S(1)} %broadcast_in_dim.49), channel_id=1, replica_groups=mesh['y'=4,'z'=8,'x'=4,'core'=2] {'y','z'}, dimensions={0} | all-to-all | bytes 524288 | tf_op jit(solution)/shard_map/all_to_all | solution.py:29
  98.4 0.4 convolution_convert_fusion.5
  98.9 5.4 %collective-permute-start.7 = (bf16[8,384]{1,0:T(8,128)(2,1)S(1)}, bf16[8,384]{1,0:T(8,128)(2,1)S(1)}, u32[]{:S(2)}, u32[]{:S(2)}) collective-permute-start(bf16[8,384]{1,0:T(8,128)(2,1)S(1)} %slice.59), channel_id=1, source_target_pairs={{0,1},{1,0},{2,3},{3,2},{4,5},{5,4},{6,7},{7,6},{8,9},{9,8},{10,11... | collective-permute-start | bytes 18440 | tf_op jit(solution)/shard_map/ppermute | solution.py:268
  104.3 0.2 reduce-precision_convert_fusion.1
  104.5 0.6 collective-permute-done.7
  105.1 0.1 pad_maximum_fusion.5
  105.2 8.4 %all_to_all.80.arrived_ref = bf16[4,72,384]{2,1,0:T(8,128)(2,1)S(1)} all-to-all(bf16[4,72,384]{2,1,0:T(8,128)(2,1)S(1)} %broadcast_in_dim.50), channel_id=1, replica_groups=mesh['y'=4,'z'=8,'x'=4,'core'=2] {'x'}, dimensions={0} | all-to-all | bytes 442368 | tf_op jit(solution)/shard_map/all_to_all | solution.py:29
  113.6 1.7 normalized_forward.1
  115.4 13.1 %all_to_all.81 = bf16[8,64,256]{2,1,0:T(8,128)(2,1)S(1)} all-to-all(bf16[8,64,256]{2,1,0:T(8,128)(2,1)S(1)} %broadcast_in_dim.51), channel_id=1, replica_groups=mesh['y'=4,'z'=8,'x'=4,'core'=2] {'z'}, dimensions={0} | all-to-all | bytes 524288 | tf_op jit(solution)/shard_map/all_to_all | solution.py:29
  128.5 0.4 convolution_convert_fusion.4
  129.0 7.2 %all_to_all.82 = bf16[4,64,256]{2,1,0:T(8,128)(2,1)S(1)} all-to-all(bf16[4,64,256]{2,1,0:T(8,128)(2,1)S(1)} %broadcast_in_dim.52), channel_id=1, replica_groups=mesh['y'=4,'z'=8,'x'=4,'core'=2] {'y'}, dimensions={0} | all-to-all | bytes 262144 | tf_op jit(solution)/shard_map/all_to_all | solution.py:29
  136.2 0.3 convolution_convert_fusion.1
  136.6 12.0 %all_to_all.83 = bf16[8,64,256]{2,1,0:T(8,128)(2,1)S(1)} all-to-all(bf16[8,64,256]{2,1,0:T(8,128)(2,1)S(1)} %bitcast.80), channel_id=1, replica_groups=mesh['y'=4,'z'=8,'x'=4,'core'=2] {'z'}, dimensions={0} | all-to-all | bytes 524288 | tf_op jit(solution)/shard_map/all_to_all | solution.py:29
  148.6 7.2 %all_to_all.84 = bf16[4,64,256]{2,1,0:T(8,128)(2,1)S(1)} all-to-all(bf16[4,64,256]{2,1,0:T(8,128)(2,1)S(1)} %broadcast_in_dim.53), channel_id=1, replica_groups=mesh['y'=4,'z'=8,'x'=4,'core'=2] {'x'}, dimensions={0} | all-to-all | bytes 262144 | tf_op jit(solution)/shard_map/all_to_all | solution.py:29
  155.8 0.3 convolution_convert_fusion
  156.1 12.6 %all_to_all.85 = bf16[32,8,512]{2,1,0:T(8,128)(2,1)S(1)} all-to-all(bf16[32,8,512]{2,1,0:T(8,128)(2,1)S(1)} %bitcast.83), channel_id=1, replica_groups=mesh['y'=4,'z'=8,'x'=4,'core'=2] {'y','z'}, dimensions={0} | all-to-all | bytes 524288 | tf_op jit(solution)/shard_map/all_to_all | solution.py:29
  168.8 0.1 reduce_sum.121
  168.8 13.8 %all_to_all.86 = bf16[32,8,512]{2,1,0:T(8,128)(2,1)S(1)} all-to-all(bf16[32,8,512]{2,1,0:T(8,128)(2,1)S(1)} %broadcast_in_dim.54), channel_id=1, replica_groups=mesh['y'=4,'z'=8,'x'=4,'core'=2] {'y','z'}, dimensions={0} | all-to-all | bytes 524288 | tf_op jit(solution)/shard_map/all_to_all | solution.py:29
  182.7 0.2 reduce-precision_convert_fusion
  182.9 8.5 %collective-permute-start.8 = (bf16[64,1024]{1,0:T(8,128)(2,1)S(1)}, bf16[64,1024]{1,0:T(8,128)(2,1)S(1)}, u32[]{:S(2)}, u32[]{:S(2)}) collective-permute-start(bf16[64,1024]{1,0:T(8,128)(2,1)S(1)} %slice.60), channel_id=1, source_target_pairs={{0,1},{1,0},{2,3},{3,2},{4,5},{5,4},{6,7},{7,6},{8,9},{9,8},{10,11... | collective-permute-start | bytes 393224 | tf_op jit(solution)/shard_map/ppermute | solution.py:299
  191.4 0.1 pad_maximum_fusion.6
  191.5 7.6 %all_to_all.87.arrived_ref = bf16[8,64,128]{2,1,0:T(8,128)(2,1)S(1)} all-to-all(bf16[8,64,128]{2,1,0:T(8,128)(2,1)S(1)} %broadcast_in_dim.102), channel_id=1, replica_groups=mesh['y'=4,'z'=8,'x'=4,'core'=2] {'x','core'}, dimensions={0} | all-to-all | bytes 262144 | tf_op jit(solution)/shard_map/all_to_all | solution.py:29
  199.2 0.0 collective-permute-done.8.there_ref
  199.2 2.8 %normalized_panels.1 = f32[2,64,1024]{2,1,0:T(8,128)} custom-call(bf16[8,64,128]{2,1,0:T(8,128)(2,1)S(1)} %all_to_all.87.arrived_ref, bf16[64,2048]{1,0:T(8,128)(2,1)S(1)} %bitcast.73, bf16[64,1024]{1,0:T(8,128)(2,1)S(1)} %collective-permute-done.8.there_ref), custom_call_target="tpu_custom_call" | custom-call | tf_op jit(solution)/shard_map/normalized_panels/pallas_call | solution.py:188
  (36 shorter events, 0.7 us)
Async XLA Ops:
  1.3 5.5 %copy-start = (f32[2,2,256]{2,1,0:T(2,128)S(1)}, f32[2,2,256]{2,1,0:T(2,128)}, u32[]{:S(2)}) copy-start(f32[2,2,256]{2,1,0:T(2,128)} %param.4) | copy-start | bytes 12292
  1.4 10.4 %collective-permute-start.2 = (bf16[128,1024]{1,0:T(8,128)(2,1)S(1)}, bf16[128,1024]{1,0:T(8,128)(2,1)S(1)}, u32[]{:S(2)}, u32[]{:S(2)}) collective-permute-start(bf16[128,1024]{1,0:T(8,128)(2,1)S(1)} %pad_maximum_fusion.4), channel_id=1, source_target_pairs={{0,1},{1,0},{2,3},{3,2},{4,5},{5,4},{6,7},{7,6},{8,9},{9,8},{10,11... | collective-permute-start | bytes 786440 | tf_op jit(solution)/shard_map/ppermute | solution.py:249
  4.7 23.6 %collective-permute-start.1 = (bf16[256,1024]{1,0:T(8,128)(2,1)S(1)}, bf16[256,1024]{1,0:T(8,128)(2,1)S(1)}, u32[]{:S(2)}, u32[]{:S(2)}) collective-permute-start(bf16[256,1024]{1,0:T(8,128)(2,1)S(1)} %get-tuple-element.14), channel_id=1, source_target_pairs={{0,1},{1,0},{2,3},{3,2},{4,5},{5,4},{6,7},{7,6},{8,9},{9,8},{10,11... | collective-permute-start | bytes 1572872 | tf_op jit(solution)/shard_map/ppermute | solution.py:259
  6.3 1.4 collective-permute-start
  8.4 8.4 %all-to-all-start = ((bf16[4,64,256]{2,1,0:T(8,128)(2,1)}), bf16[4,64,256]{2,1,0:T(8,128)(2,1)S(1)}, u32[]{:S(2)}, u32[]{:S(2)}) async-start(bf16[4,64,256]{2,1,0:T(8,128)(2,1)} %broadcast_in_dim.40), calls=%async_computation | async-start | bytes 262144 | tf_op jit(solution)/shard_map/all_to_all | solution.py:29
  11.9 15.6 %collective-permute-start.3 = (bf16[64,2048]{1,0:T(8,128)(2,1)S(1)}, bf16[64,2048]{1,0:T(8,128)(2,1)S(1)}, u32[]{:S(2)}, u32[]{:S(2)}) collective-permute-start(bf16[64,2048]{1,0:T(8,128)(2,1)S(1)} %get-tuple-element.19), channel_id=1, source_target_pairs={{0,0},{1,5},{2,64},{3,69},{4,128},{5,133},{6,192},{7,197},{64,2},{... | collective-permute-start | bytes 786440 | tf_op jit(solution)/shard_map/ppermute | solution.py:254
  16.8 10.9 %collective-permute-start.5 = (bf16[64,2048]{1,0:T(8,128)(2,1)S(1)}, bf16[64,2048]{1,0:T(8,128)(2,1)S(1)}, u32[]{:S(2)}, u32[]{:S(2)}) collective-permute-start(bf16[64,2048]{1,0:T(8,128)(2,1)S(1)} %get-tuple-element.20), channel_id=1, source_target_pairs={{0,2},{1,7},{2,66},{3,71},{4,130},{5,135},{6,194},{7,199},{64,4},{... | collective-permute-start | bytes 786440 | tf_op jit(solution)/shard_map/ppermute | solution.py:254
  19.4 20.6 %all-to-all-start.1 = ((bf16[8,64,256]{2,1,0:T(8,128)(2,1)}), bf16[8,64,256]{2,1,0:T(8,128)(2,1)S(1)}, u32[]{:S(2)}, u32[]{:S(2)}) async-start(bf16[8,64,256]{2,1,0:T(8,128)(2,1)} %broadcast_in_dim.41), calls=%async_computation.1 | async-start | bytes 524288 | tf_op jit(solution)/shard_map/all_to_all | solution.py:29
  27.6 12.5 %collective-permute-start.4 = (bf16[64,2048]{1,0:T(8,128)(2,1)S(1)}, bf16[64,2048]{1,0:T(8,128)(2,1)S(1)}, u32[]{:S(2)}, u32[]{:S(2)}) collective-permute-start(bf16[64,2048]{1,0:T(8,128)(2,1)S(1)} %collective-permute-done.3), channel_id=1, source_target_pairs={{0,1},{1,0},{2,3},{3,2},{4,5},{5,4},{6,7},{7,6},{8,9},{9,8},{10,11... | collective-permute-start | bytes 786440 | tf_op jit(solution)/shard_map/ppermute | solution.py:255
  27.7 12.4 %collective-permute-start.6 = (bf16[64,2048]{1,0:T(8,128)(2,1)S(1)}, bf16[64,2048]{1,0:T(8,128)(2,1)}, u32[]{:S(2)}, u32[]{:S(2)}) collective-permute-start(bf16[64,2048]{1,0:T(8,128)(2,1)S(1)} %collective-permute-done.5), channel_id=1, source_target_pairs={{0,1},{1,0},{2,3},{3,2},{4,5},{5,4},{6,7},{7,6},{8,9},{9,8},{10,11... | collective-permute-start | bytes 786440 | tf_op jit(solution)/shard_map/ppermute | solution.py:255
  98.9 6.2 %collective-permute-start.7 = (bf16[8,384]{1,0:T(8,128)(2,1)S(1)}, bf16[8,384]{1,0:T(8,128)(2,1)S(1)}, u32[]{:S(2)}, u32[]{:S(2)}) collective-permute-start(bf16[8,384]{1,0:T(8,128)(2,1)S(1)} %slice.59), channel_id=1, source_target_pairs={{0,1},{1,0},{2,3},{3,2},{4,5},{5,4},{6,7},{7,6},{8,9},{9,8},{10,11... | collective-permute-start | bytes 18440 | tf_op jit(solution)/shard_map/ppermute | solution.py:268
  182.9 16.3 %collective-permute-start.8 = (bf16[64,1024]{1,0:T(8,128)(2,1)S(1)}, bf16[64,1024]{1,0:T(8,128)(2,1)S(1)}, u32[]{:S(2)}, u32[]{:S(2)}) collective-permute-start(bf16[64,1024]{1,0:T(8,128)(2,1)S(1)} %slice.60), channel_id=1, source_target_pairs={{0,1},{1,0},{2,3},{3,2},{4,5},{5,4},{6,7},{7,6},{8,9},{9,8},{10,11... | collective-permute-start | bytes 393224 | tf_op jit(solution)/shard_map/ppermute | solution.py:299

commit v12 on v10

--- a/solution.py
+++ b/solution.py
@@ -218,7 +218,6 @@
         for e in range(share)
     ]
     flip = [(0, 1), (1, 0)]
-    near, far = [(i, i ^ 1) for i in range(n_x)], [(i, n_x - 1 - i) for i in range(n_x)]
 
     def on_device(weights, preact, panel):
         core = lax.axis_index("core")
@@ -284,10 +283,9 @@
             partial_in = dot_n(weighted, w2).astype(BF16)
             blocks = jnp.moveaxis(partial_in.reshape(rank, n_z, width_row), 1, 0)
             summed = total(exchange(blocks, "z")).astype(BF16)
-            for step in (near, far):
-                there = lax.ppermute(summed, "x", step)
-                summed = (summed.astype(F32) + there.astype(F32)).astype(BF16)
-            cotangent = summed
+            if iteration == ITERS - 1:
+                summed = jnp.concatenate([summed, lax.ppermute(summed[:8], "core", flip)])
+            cotangent = total(to_all(summed, "x", n_x)[:, :rank]).astype(BF16)
             weighted = (slope_1 * cotangent.astype(F32)).astype(BF16)
             partial_in = dot_n(weighted, w1).astype(BF16)
             groups = rank // 8

time: 205 us -> 203 us (level)
  blocking collectives: 124 us -> 138 us
  waiting for transfers between devices: 24.6 us -> 13 us
  starting transfers between devices: 41.1 us -> 36.5 us
    all_to_all x11 -> x13, blocking collectives: 124 us -> 138 us  [exchange(): return lax.all_to_all(tiles, axis, split_axis=0, concat_axis=0, tiled=True)]
    ppermute x1, starting transfers between devices: 16.6 us -> 3.72 us  [on_device(): there = lax.ppermute(image[:, width_in:], 'core', flip)]
    ppermute x4 -> x1, waiting for transfers between devices: 12.4 us -> 0.82 us  [on_device(): summed = jnp.concatenate([summed, lax.ppermute(summed[:8], 'core', flip)])]
    ppermute x4 -> x1, starting transfers between devices: 1.71 us -> 10.1 us  [on_device(): summed = jnp.concatenate([summed, lax.ppermute(summed[:8], 'core', flip)])]
  transfers between devices with their start and end apart: 14 -> 11, of which waited for: 6 -> 3; matrix products, arithmetic and copies ran while one was open for 1% -> 1% of each run, Pallas kernels for 1% -> 1%
where the time goes in v12:
time: 203 us; the launch traced here: 202 us
  blocking collectives  138 us (68%)
  starting transfers between devices  36.5 us (18%)
  waiting for transfers between devices  13 us (6%)
  Pallas kernels  6.09 us (3%)
  local copies, waits for them, and re-layouts  3.31 us (2%)
  matrix products  2.96 us (1%)
    all_to_all x13, blocking collectives, exchange(): return lax.all_to_all(tiles, axis, split_axis=0, concat_axis=0, tiled=True)  138 us
    all_to_all x2, waiting for transfers between devices, exchange(): return lax.all_to_all(tiles, axis, split_axis=0, concat_axis=0, tiled=True)  11.6 us
    all_to_all x2, starting transfers between devices, exchange(): return lax.all_to_all(tiles, axis, split_axis=0, concat_axis=0, tiled=True)  11.5 us
    ppermute x1, starting transfers between devices, on_device(): summed = jnp.concatenate([summed, lax.ppermute(summed[:8], 'core', flip)])  10.1 us
    ppermute x2, starting transfers between devices, on_device(): here.append(lax.ppermute(rows[e], ('y', 'x', 'core'), turns[e]))  6.65 us
  transfers between devices with their start and end apart: 11, of which 3 were waited for; matrix products, arithmetic and copies ran while one was open for 1% of the time, Pallas kernels for 1%

profile of v12, /device:TPU:1, one launch (start us, length us, event | category | flops | bytes accessed | tf_op | source)
XLA Modules:
  0.0 202.4 jit_solution(178012066078127639)
XLA Ops:
  0.0 1.3 fusion.9
  1.3 0.0 copy-start
  1.4 3.3 %collective-permute-start.2 = (bf16[128,1024]{1,0:T(8,128)(2,1)S(1)}, bf16[128,1024]{1,0:T(8,128)(2,1)S(1)}, u32[]{:S(2)}, u32[]{:S(2)}) collective-permute-start(bf16[128,1024]{1,0:T(8,128)(2,1)S(1)} %pad_maximum_fusion.4), channel_id=1, source_target_pairs={{0,1},{1,0},{2,3},{3,2},{4,5},{5,4},{6,7},{7,6},{8,9},{9,8},{10,11... | collective-permute-start | bytes 786440 | tf_op jit(solution)/shard_map/ppermute | solution.py:249
  4.7 0.1 collective-permute-start.1
  4.8 1.6 first_partial.1
  6.3 0.5 collective-permute-start
  6.8 0.0 copy-done
  6.9 0.1 fusion.8
  7.0 0.1 iota.9
  7.0 0.1 iota.10
  7.1 0.1 broadcast_in_dim.44
  7.2 0.5 collective-permute-done
  7.8 0.7 broadcast_in_dim.40
  8.4 3.3 %all-to-all-start = ((bf16[4,64,256]{2,1,0:T(8,128)(2,1)}), bf16[4,64,256]{2,1,0:T(8,128)(2,1)S(1)}, u32[]{:S(2)}, u32[]{:S(2)}) async-start(bf16[4,64,256]{2,1,0:T(8,128)(2,1)} %broadcast_in_dim.40), calls=%async_computation | async-start | bytes 262144 | tf_op jit(solution)/shard_map/all_to_all | solution.py:29
  11.8 0.0 collective-permute-done.2
  11.8 0.1 broadcast_select_fusion.1
  11.9 4.8 %collective-permute-start.3 = (bf16[64,2048]{1,0:T(8,128)(2,1)S(1)}, bf16[64,2048]{1,0:T(8,128)(2,1)S(1)}, u32[]{:S(2)}, u32[]{:S(2)}) collective-permute-start(bf16[64,2048]{1,0:T(8,128)(2,1)S(1)} %get-tuple-element.19), channel_id=1, source_target_pairs={{0,0},{1,5},{2,64},{3,69},{4,128},{5,133},{6,192},{7,197},{64,2},{... | collective-permute-start | bytes 786440 | tf_op jit(solution)/shard_map/ppermute | solution.py:254
  16.8 0.0 all-to-all-done
  16.8 1.8 collective-permute-start.5
  18.6 0.7 broadcast_in_dim.41
  19.4 8.2 %all-to-all-start.1 = ((bf16[8,64,256]{2,1,0:T(8,128)(2,1)}), bf16[8,64,256]{2,1,0:T(8,128)(2,1)S(1)}, u32[]{:S(2)}, u32[]{:S(2)}) async-start(bf16[8,64,256]{2,1,0:T(8,128)(2,1)} %broadcast_in_dim.41), calls=%async_computation.1 | async-start | bytes 524288 | tf_op jit(solution)/shard_map/all_to_all | solution.py:29
  27.5 0.0 collective-permute-done.3
  27.6 0.1 collective-permute-start.4
  27.7 0.0 collective-permute-done.5
  27.7 0.6 collective-permute-start.6
  28.2 0.0 collective-permute-done.1
  28.3 0.1 pad_maximum_fusion
  28.3 11.6 %all-to-all-done.1 = bf16[8,64,256]{2,1,0:T(8,128)(2,1)S(1)} async-done(((bf16[8,64,256]{2,1,0:T(8,128)(2,1)}), bf16[8,64,256]{2,1,0:T(8,128)(2,1)S(1)}, u32[]{:S(2)}, u32[]{:S(2)}) %all-to-all-start.1) | async-done | bytes 262176 | tf_op jit(solution)/shard_map/all_to_all | solution.py:29
  40.0 0.0 collective-permute-done.4
  40.1 0.0 collective-permute-done.6
  40.1 1.0 broadcast_select_fusion.4
  41.1 0.1 pad_maximum_fusion.1
  41.1 0.4 convolution_convert_fusion.6
  41.6 8.5 %all_to_all.75 = bf16[4,72,256]{2,1,0:T(8,128)(2,1)S(1)} all-to-all(bf16[4,72,256]{2,1,0:T(8,128)(2,1)S(1)} %broadcast_in_dim.47), channel_id=1, replica_groups=mesh['y'=4,'z'=8,'x'=4,'core'=2] {'y'}, dimensions={0} | all-to-all | bytes 294912 | tf_op jit(solution)/shard_map/all_to_all | solution.py:29
  50.2 0.3 convolution_convert_fusion.3
  50.5 11.9 %all_to_all.76 = bf16[8,64,256]{2,1,0:T(8,128)(2,1)S(1)} all-to-all(bf16[8,64,256]{2,1,0:T(8,128)(2,1)S(1)} %bitcast.77), channel_id=1, replica_groups=mesh['y'=4,'z'=8,'x'=4,'core'=2] {'z'}, dimensions={0} | all-to-all | bytes 524288 | tf_op jit(solution)/shard_map/all_to_all | solution.py:29
  62.5 7.2 %all_to_all.77 = bf16[4,64,256]{2,1,0:T(8,128)(2,1)S(1)} all-to-all(bf16[4,64,256]{2,1,0:T(8,128)(2,1)S(1)} %broadcast_in_dim.48), channel_id=1, replica_groups=mesh['y'=4,'z'=8,'x'=4,'core'=2] {'x'}, dimensions={0} | all-to-all | bytes 262144 | tf_op jit(solution)/shard_map/all_to_all | solution.py:29
  69.7 0.3 convolution_convert_fusion.2
  70.1 14.1 %all_to_all.78 = bf16[32,8,512]{2,1,0:T(8,128)(2,1)S(1)} all-to-all(bf16[32,8,512]{2,1,0:T(8,128)(2,1)S(1)} %bitcast.84), channel_id=1, replica_groups=mesh['y'=4,'z'=8,'x'=4,'core'=2] {'y','z'}, dimensions={0} | all-to-all | bytes 524288 | tf_op jit(solution)/shard_map/all_to_all | solution.py:29
  84.2 0.1 reduce_sum.117
  84.2 14.1 %all_to_all.79 = bf16[32,8,512]{2,1,0:T(8,128)(2,1)S(1)} all-to-all(bf16[32,8,512]{2,1,0:T(8,128)(2,1)S(1)} %broadcast_in_dim.49), channel_id=1, replica_groups=mesh['y'=4,'z'=8,'x'=4,'core'=2] {'y','z'}, dimensions={0} | all-to-all | bytes 524288 | tf_op jit(solution)/shard_map/all_to_all | solution.py:29
  98.4 0.4 convolution_convert_fusion.5
  98.8 0.2 reduce-precision_convert_fusion.1
  99.0 0.1 pad_maximum_fusion.5
  99.1 7.5 %all_to_all.80.arrived_ref = bf16[4,64,384]{2,1,0:T(8,128)(2,1)S(1)} all-to-all(bf16[4,64,384]{2,1,0:T(8,128)(2,1)S(1)} %broadcast_in_dim.50), channel_id=1, replica_groups=mesh['y'=4,'z'=8,'x'=4,'core'=2] {'x'}, dimensions={0} | all-to-all | bytes 393216 | tf_op jit(solution)/shard_map/all_to_all | solution.py:29
  106.7 1.7 normalized_forward.1
  108.5 12.5 %all_to_all.81 = bf16[8,64,256]{2,1,0:T(8,128)(2,1)S(1)} all-to-all(bf16[8,64,256]{2,1,0:T(8,128)(2,1)S(1)} %broadcast_in_dim.51), channel_id=1, replica_groups=mesh['y'=4,'z'=8,'x'=4,'core'=2] {'z'}, dimensions={0} | all-to-all | bytes 524288 | tf_op jit(solution)/shard_map/all_to_all | solution.py:29
  121.0 0.4 convolution_convert_fusion.4
  121.4 7.2 %all_to_all.82 = bf16[4,64,256]{2,1,0:T(8,128)(2,1)S(1)} all-to-all(bf16[4,64,256]{2,1,0:T(8,128)(2,1)S(1)} %broadcast_in_dim.52), channel_id=1, replica_groups=mesh['y'=4,'z'=8,'x'=4,'core'=2] {'y'}, dimensions={0} | all-to-all | bytes 262144 | tf_op jit(solution)/shard_map/all_to_all | solution.py:29
  128.7 0.3 convolution_convert_fusion.1
  129.0 11.7 %all_to_all.83 = bf16[8,64,256]{2,1,0:T(8,128)(2,1)S(1)} all-to-all(bf16[8,64,256]{2,1,0:T(8,128)(2,1)S(1)} %bitcast.79), channel_id=1, replica_groups=mesh['y'=4,'z'=8,'x'=4,'core'=2] {'z'}, dimensions={0} | all-to-all | bytes 524288 | tf_op jit(solution)/shard_map/all_to_all | solution.py:29
  140.8 10.1 %collective-permute-start.7 = (bf16[8,256]{1,0:T(8,128)(2,1)S(1)}, bf16[8,256]{1,0:T(8,128)(2,1)S(1)}, u32[]{:S(2)}, u32[]{:S(2)}) collective-permute-start(bf16[8,256]{1,0:T(8,128)(2,1)S(1)} %slice.63), channel_id=1, source_target_pairs={{0,1},{1,0},{2,3},{3,2},{4,5},{5,4},{6,7},{7,6},{8,9},{9,8},{10,11... | collective-permute-start | bytes 12296 | tf_op jit(solution)/shard_map/ppermute | solution.py:287
  150.9 0.8 collective-permute-done.7
  151.7 7.3 %all_to_all.84 = bf16[4,72,256]{2,1,0:T(8,128)(2,1)S(1)} all-to-all(bf16[4,72,256]{2,1,0:T(8,128)(2,1)S(1)} %broadcast_in_dim.53), channel_id=1, replica_groups=mesh['y'=4,'z'=8,'x'=4,'core'=2] {'x'}, dimensions={0} | all-to-all | bytes 294912 | tf_op jit(solution)/shard_map/all_to_all | solution.py:29
  159.0 0.3 convolution_convert_fusion
  159.3 12.6 %all_to_all.85 = bf16[32,8,512]{2,1,0:T(8,128)(2,1)S(1)} all-to-all(bf16[32,8,512]{2,1,0:T(8,128)(2,1)S(1)} %bitcast.82), channel_id=1, replica_groups=mesh['y'=4,'z'=8,'x'=4,'core'=2] {'y','z'}, dimensions={0} | all-to-all | bytes 524288 | tf_op jit(solution)/shard_map/all_to_all | solution.py:29
  172.0 0.1 reduce_sum.121
  172.0 15.7 %all_to_all.86 = bf16[32,8,512]{2,1,0:T(8,128)(2,1)S(1)} all-to-all(bf16[32,8,512]{2,1,0:T(8,128)(2,1)S(1)} %broadcast_in_dim.54), channel_id=1, replica_groups=mesh['y'=4,'z'=8,'x'=4,'core'=2] {'y','z'}, dimensions={0} | all-to-all | bytes 524288 | tf_op jit(solution)/shard_map/all_to_all | solution.py:29
  187.7 0.2 reduce-precision_convert_fusion
  188.0 3.7 %collective-permute-start.8 = (bf16[64,1024]{1,0:T(8,128)(2,1)S(1)}, bf16[64,1024]{1,0:T(8,128)(2,1)S(1)}, u32[]{:S(2)}, u32[]{:S(2)}) collective-permute-start(bf16[64,1024]{1,0:T(8,128)(2,1)S(1)} %slice.65), channel_id=1, source_target_pairs={{0,1},{1,0},{2,3},{3,2},{4,5},{5,4},{6,7},{7,6},{8,9},{9,8},{10,11... | collective-permute-start | bytes 393224 | tf_op jit(solution)/shard_map/ppermute | solution.py:299
  191.7 0.1 pad_maximum_fusion.7
  191.8 7.9 %all_to_all.87.arrived_ref = bf16[8,64,128]{2,1,0:T(8,128)(2,1)S(1)} all-to-all(bf16[8,64,128]{2,1,0:T(8,128)(2,1)S(1)} %broadcast_in_dim.102), channel_id=1, replica_groups=mesh['y'=4,'z'=8,'x'=4,'core'=2] {'x','core'}, dimensions={0} | all-to-all | bytes 262144 | tf_op jit(solution)/shard_map/all_to_all | solution.py:29
  199.6 0.0 collective-permute-done.8.there_ref
  199.7 2.8 %normalized_panels.1 = f32[2,64,1024]{2,1,0:T(8,128)} custom-call(bf16[8,64,128]{2,1,0:T(8,128)(2,1)S(1)} %all_to_all.87.arrived_ref, bf16[64,2048]{1,0:T(8,128)(2,1)S(1)} %bitcast.73, bf16[64,1024]{1,0:T(8,128)(2,1)S(1)} %collective-permute-done.8.there_ref), custom_call_target="tpu_custom_call" | custom-call | tf_op jit(solution)/shard_map/normalized_panels/pallas_call | solution.py:188
  (37 shorter events, 0.7 us)
Async XLA Ops:
  1.3 5.5 %copy-start = (f32[2,2,256]{2,1,0:T(2,128)S(1)}, f32[2,2,256]{2,1,0:T(2,128)}, u32[]{:S(2)}) copy-start(f32[2,2,256]{2,1,0:T(2,128)} %param.4) | copy-start | bytes 12292
  1.4 10.4 %collective-permute-start.2 = (bf16[128,1024]{1,0:T(8,128)(2,1)S(1)}, bf16[128,1024]{1,0:T(8,128)(2,1)S(1)}, u32[]{:S(2)}, u32[]{:S(2)}) collective-permute-start(bf16[128,1024]{1,0:T(8,128)(2,1)S(1)} %pad_maximum_fusion.4), channel_id=1, source_target_pairs={{0,1},{1,0},{2,3},{3,2},{4,5},{5,4},{6,7},{7,6},{8,9},{9,8},{10,11... | collective-permute-start | bytes 786440 | tf_op jit(solution)/shard_map/ppermute | solution.py:249
  4.7 23.6 %collective-permute-start.1 = (bf16[256,1024]{1,0:T(8,128)(2,1)S(1)}, bf16[256,1024]{1,0:T(8,128)(2,1)S(1)}, u32[]{:S(2)}, u32[]{:S(2)}) collective-permute-start(bf16[256,1024]{1,0:T(8,128)(2,1)S(1)} %get-tuple-element.14), channel_id=1, source_target_pairs={{0,1},{1,0},{2,3},{3,2},{4,5},{5,4},{6,7},{7,6},{8,9},{9,8},{10,11... | collective-permute-start | bytes 1572872 | tf_op jit(solution)/shard_map/ppermute | solution.py:259
  6.3 1.4 collective-permute-start
  8.4 8.4 %all-to-all-start = ((bf16[4,64,256]{2,1,0:T(8,128)(2,1)}), bf16[4,64,256]{2,1,0:T(8,128)(2,1)S(1)}, u32[]{:S(2)}, u32[]{:S(2)}) async-start(bf16[4,64,256]{2,1,0:T(8,128)(2,1)} %broadcast_in_dim.40), calls=%async_computation | async-start | bytes 262144 | tf_op jit(solution)/shard_map/all_to_all | solution.py:29
  11.9 15.6 %collective-permute-start.3 = (bf16[64,2048]{1,0:T(8,128)(2,1)S(1)}, bf16[64,2048]{1,0:T(8,128)(2,1)S(1)}, u32[]{:S(2)}, u32[]{:S(2)}) collective-permute-start(bf16[64,2048]{1,0:T(8,128)(2,1)S(1)} %get-tuple-element.19), channel_id=1, source_target_pairs={{0,0},{1,5},{2,64},{3,69},{4,128},{5,133},{6,192},{7,197},{64,2},{... | collective-permute-start | bytes 786440 | tf_op jit(solution)/shard_map/ppermute | solution.py:254
  16.8 10.9 %collective-permute-start.5 = (bf16[64,2048]{1,0:T(8,128)(2,1)S(1)}, bf16[64,2048]{1,0:T(8,128)(2,1)S(1)}, u32[]{:S(2)}, u32[]{:S(2)}) collective-permute-start(bf16[64,2048]{1,0:T(8,128)(2,1)S(1)} %get-tuple-element.20), channel_id=1, source_target_pairs={{0,2},{1,7},{2,66},{3,71},{4,130},{5,135},{6,194},{7,199},{64,4},{... | collective-permute-start | bytes 786440 | tf_op jit(solution)/shard_map/ppermute | solution.py:254
  19.4 20.6 %all-to-all-start.1 = ((bf16[8,64,256]{2,1,0:T(8,128)(2,1)}), bf16[8,64,256]{2,1,0:T(8,128)(2,1)S(1)}, u32[]{:S(2)}, u32[]{:S(2)}) async-start(bf16[8,64,256]{2,1,0:T(8,128)(2,1)} %broadcast_in_dim.41), calls=%async_computation.1 | async-start | bytes 524288 | tf_op jit(solution)/shard_map/all_to_all | solution.py:29
  27.6 12.5 %collective-permute-start.4 = (bf16[64,2048]{1,0:T(8,128)(2,1)S(1)}, bf16[64,2048]{1,0:T(8,128)(2,1)S(1)}, u32[]{:S(2)}, u32[]{:S(2)}) collective-permute-start(bf16[64,2048]{1,0:T(8,128)(2,1)S(1)} %collective-permute-done.3), channel_id=1, source_target_pairs={{0,1},{1,0},{2,3},{3,2},{4,5},{5,4},{6,7},{7,6},{8,9},{9,8},{10,11... | collective-permute-start | bytes 786440 | tf_op jit(solution)/shard_map/ppermute | solution.py:255
  27.7 12.4 %collective-permute-start.6 = (bf16[64,2048]{1,0:T(8,128)(2,1)S(1)}, bf16[64,2048]{1,0:T(8,128)(2,1)}, u32[]{:S(2)}, u32[]{:S(2)}) collective-permute-start(bf16[64,2048]{1,0:T(8,128)(2,1)S(1)} %collective-permute-done.5), channel_id=1, source_target_pairs={{0,1},{1,0},{2,3},{3,2},{4,5},{5,4},{6,7},{7,6},{8,9},{9,8},{10,11... | collective-permute-start | bytes 786440 | tf_op jit(solution)/shard_map/ppermute | solution.py:255
  140.8 10.9 %collective-permute-start.7 = (bf16[8,256]{1,0:T(8,128)(2,1)S(1)}, bf16[8,256]{1,0:T(8,128)(2,1)S(1)}, u32[]{:S(2)}, u32[]{:S(2)}) collective-permute-start(bf16[8,256]{1,0:T(8,128)(2,1)S(1)} %slice.63), channel_id=1, source_target_pairs={{0,1},{1,0},{2,3},{3,2},{4,5},{5,4},{6,7},{7,6},{8,9},{9,8},{10,11... | collective-permute-start | bytes 12296 | tf_op jit(solution)/shard_map/ppermute | solution.py:287
  188.0 11.7 %collective-permute-start.8 = (bf16[64,1024]{1,0:T(8,128)(2,1)S(1)}, bf16[64,1024]{1,0:T(8,128)(2,1)S(1)}, u32[]{:S(2)}, u32[]{:S(2)}) collective-permute-start(bf16[64,1024]{1,0:T(8,128)(2,1)S(1)} %slice.65), channel_id=1, source_target_pairs={{0,1},{1,0},{2,3},{3,2},{4,5},{5,4},{6,7},{7,6},{8,9},{9,8},{10,11... | collective-permute-start | bytes 393224 | tf_op jit(solution)/shard_map/ppermute | solution.py:299

commit v13 on v12

--- a/solution.py
+++ b/solution.py
@@ -113,15 +113,24 @@
 
     def kernel(panel_ref, weights_ref, mine_ref, theirs_ref, panel_here, block_here, sems):
         panel_copy = pltpu.make_async_copy(panel_ref, panel_here, sems.at[0])
-        block_copy = pltpu.make_async_copy(weights_ref.at[0], block_here, sems.at[1])
+        half = rows // 2
+        block_copies = [
+            pltpu.make_async_copy(
+                weights_ref.at[0, pl.ds(i * half, half)], block_here.at[pl.ds(i * half, half)], sems.at[1 + i]
+            )
+            for i in range(2)
+        ]
         panel_copy.start()
-        block_copy.start()
+        for copy in block_copies:
+            copy.start()
         panel_copy.wait()
-        block_copy.wait()
         core = lax.axis_index("core")
-        block = block_here[...]
-        mine_ref[...] = dot_t(panel_here[pl.ds(core, 1)][0], block)
-        theirs_ref[...] = dot_t(panel_here[pl.ds(1 - core, 1)][0], block)
+        for i, copy in enumerate(block_copies):
+            copy.wait()
+            at = slice(i * half, (i + 1) * half)
+            block = block_here[at]
+            mine_ref[:, at] = dot_t(panel_here[pl.ds(core, 1)][0], block)
+            theirs_ref[:, at] = dot_t(panel_here[pl.ds(1 - core, 1)][0], block)
 
     return pl.pallas_call(
         kernel,
@@ -131,7 +140,7 @@
         scratch_shapes=[
             pltpu.VMEM((inputs, rank, width), BF16),
             pltpu.VMEM((rows, width), BF16),
-            pltpu.SemaphoreType.DMA((2,)),
+            pltpu.SemaphoreType.DMA((3,)),
         ],
         name="first_partial",
     )(panel, weights)
@@ -283,9 +292,7 @@
             partial_in = dot_n(weighted, w2).astype(BF16)
             blocks = jnp.moveaxis(partial_in.reshape(rank, n_z, width_row), 1, 0)
             summed = total(exchange(blocks, "z")).astype(BF16)
-            if iteration == ITERS - 1:
-                summed = jnp.concatenate([summed, lax.ppermute(summed[:8], "core", flip)])
-            cotangent = total(to_all(summed, "x", n_x)[:, :rank]).astype(BF16)
+            cotangent = total(to_all(summed, "x", n_x)).astype(BF16)
             weighted = (slope_1 * cotangent.astype(F32)).astype(BF16)
             partial_in = dot_n(weighted, w1).astype(BF16)
             groups = rank // 8

time: 203 us -> 202 us (level)
    ppermute x1, starting transfers between devices: 3.72 us -> 14.4 us  [on_device(): there = lax.ppermute(image[:, width_in:], 'core', flip)]
    ppermute x1 -> x0, starting transfers between devices: 10.1 us -> none  [on_device(): summed = jnp.concatenate([summed, lax.ppermute(summed[:8], 'core', flip)])]
  transfers between devices with their start and end apart: 11 -> 10, of which waited for: 3 -> 2; matrix products, arithmetic and copies ran while one was open for 1% -> 1% of each run, Pallas kernels for 1% -> 1%
where the time goes in v13:
time: 202 us; the launch traced here: 201 us
  blocking collectives  137 us (68%)
  starting transfers between devices  37.1 us (18%)
  waiting for transfers between devices  12.2 us (6%)
  Pallas kernels  6.15 us (3%)
  local copies, waits for them, and re-layouts  3.3 us (2%)
  matrix products  2.97 us (1%)
    all_to_all x13, blocking collectives, exchange(): return lax.all_to_all(tiles, axis, split_axis=0, concat_axis=0, tiled=True)  137 us
    ppermute x1, starting transfers between devices, on_device(): there = lax.ppermute(image[:, width_in:], 'core', flip)  14.4 us
    all_to_all x2, waiting for transfers between devices, exchange(): return lax.all_to_all(tiles, axis, split_axis=0, concat_axis=0, tiled=True)  11.6 us
    all_to_all x2, starting transfers between devices, exchange(): return lax.all_to_all(tiles, axis, split_axis=0, concat_axis=0, tiled=True)  11.5 us
    ppermute x2, starting transfers between devices, on_device(): here.append(lax.ppermute(rows[e], ('y', 'x', 'core'), turns[e]))  6.65 us
  transfers between devices with their start and end apart: 10, of which 2 were waited for; matrix products, arithmetic and copies ran while one was open for 1% of the time, Pallas kernels for 1%

profile of v13, /device:TPU:1, one launch (start us, length us, event | category | flops | bytes accessed | tf_op | source)
XLA Modules:
  0.0 200.7 jit_solution(7766193909473578209)
XLA Ops:
  0.0 1.3 fusion.9
  1.3 0.0 copy-start
  1.4 3.3 %collective-permute-start.2 = (bf16[128,1024]{1,0:T(8,128)(2,1)S(1)}, bf16[128,1024]{1,0:T(8,128)(2,1)S(1)}, u32[]{:S(2)}, u32[]{:S(2)}) collective-permute-start(bf16[128,1024]{1,0:T(8,128)(2,1)S(1)} %pad_maximum_fusion.4), channel_id=1, source_target_pairs={{0,1},{1,0},{2,3},{3,2},{4,5},{5,4},{6,7},{7,6},{8,9},{9,8},{10,11... | collective-permute-start | bytes 786440 | tf_op jit(solution)/shard_map/ppermute | solution.py:258
  4.7 0.1 collective-permute-start.1
  4.8 1.6 first_partial.1
  6.4 0.5 collective-permute-start
  6.9 0.0 copy-done
  6.9 0.1 fusion.8
  7.0 0.1 iota.9
  7.1 0.1 iota.10
  7.2 0.1 broadcast_in_dim.44
  7.3 0.5 collective-permute-done
  7.8 0.7 broadcast_in_dim.40
  8.5 3.3 %all-to-all-start = ((bf16[4,64,256]{2,1,0:T(8,128)(2,1)}), bf16[4,64,256]{2,1,0:T(8,128)(2,1)S(1)}, u32[]{:S(2)}, u32[]{:S(2)}) async-start(bf16[4,64,256]{2,1,0:T(8,128)(2,1)} %broadcast_in_dim.40), calls=%async_computation | async-start | bytes 262144 | tf_op jit(solution)/shard_map/all_to_all | solution.py:29
  11.8 0.0 collective-permute-done.2
  11.8 0.1 broadcast_select_fusion.1
  12.0 4.8 %collective-permute-start.3 = (bf16[64,2048]{1,0:T(8,128)(2,1)S(1)}, bf16[64,2048]{1,0:T(8,128)(2,1)S(1)}, u32[]{:S(2)}, u32[]{:S(2)}) collective-permute-start(bf16[64,2048]{1,0:T(8,128)(2,1)S(1)} %get-tuple-element.19), channel_id=1, source_target_pairs={{0,0},{1,5},{2,64},{3,69},{4,128},{5,133},{6,192},{7,197},{64,2},{... | collective-permute-start | bytes 786440 | tf_op jit(solution)/shard_map/ppermute | solution.py:263
  16.8 0.0 all-to-all-done
  16.9 1.8 collective-permute-start.5
  18.7 0.7 broadcast_in_dim.41
  19.4 8.2 %all-to-all-start.1 = ((bf16[8,64,256]{2,1,0:T(8,128)(2,1)}), bf16[8,64,256]{2,1,0:T(8,128)(2,1)S(1)}, u32[]{:S(2)}, u32[]{:S(2)}) async-start(bf16[8,64,256]{2,1,0:T(8,128)(2,1)} %broadcast_in_dim.41), calls=%async_computation.1 | async-start | bytes 524288 | tf_op jit(solution)/shard_map/all_to_all | solution.py:29
  27.6 0.0 collective-permute-done.3
  27.6 0.1 collective-permute-start.4
  27.7 0.0 collective-permute-done.5
  27.7 0.6 collective-permute-start.6
  28.3 0.0 collective-permute-done.1
  28.3 0.1 pad_maximum_fusion
  28.4 11.6 %all-to-all-done.1 = bf16[8,64,256]{2,1,0:T(8,128)(2,1)S(1)} async-done(((bf16[8,64,256]{2,1,0:T(8,128)(2,1)}), bf16[8,64,256]{2,1,0:T(8,128)(2,1)S(1)}, u32[]{:S(2)}, u32[]{:S(2)}) %all-to-all-start.1) | async-done | bytes 262176 | tf_op jit(solution)/shard_map/all_to_all | solution.py:29
  40.1 0.0 collective-permute-done.4
  40.1 0.0 collective-permute-done.6
  40.1 1.0 broadcast_select_fusion.4
  41.1 0.1 pad_maximum_fusion.1
  41.2 0.4 convolution_convert_fusion.6
  41.7 8.5 %all_to_all.75 = bf16[4,72,256]{2,1,0:T(8,128)(2,1)S(1)} all-to-all(bf16[4,72,256]{2,1,0:T(8,128)(2,1)S(1)} %broadcast_in_dim.47), channel_id=1, replica_groups=mesh['y'=4,'z'=8,'x'=4,'core'=2] {'y'}, dimensions={0} | all-to-all | bytes 294912 | tf_op jit(solution)/shard_map/all_to_all | solution.py:29
  50.2 0.3 convolution_convert_fusion.3
  50.6 11.9 %all_to_all.76 = bf16[8,64,256]{2,1,0:T(8,128)(2,1)S(1)} all-to-all(bf16[8,64,256]{2,1,0:T(8,128)(2,1)S(1)} %bitcast.77), channel_id=1, replica_groups=mesh['y'=4,'z'=8,'x'=4,'core'=2] {'z'}, dimensions={0} | all-to-all | bytes 524288 | tf_op jit(solution)/shard_map/all_to_all | solution.py:29
  62.6 7.2 %all_to_all.77 = bf16[4,64,256]{2,1,0:T(8,128)(2,1)S(1)} all-to-all(bf16[4,64,256]{2,1,0:T(8,128)(2,1)S(1)} %broadcast_in_dim.48), channel_id=1, replica_groups=mesh['y'=4,'z'=8,'x'=4,'core'=2] {'x'}, dimensions={0} | all-to-all | bytes 262144 | tf_op jit(solution)/shard_map/all_to_all | solution.py:29
  69.8 0.3 convolution_convert_fusion.2
  70.1 14.1 %all_to_all.78 = bf16[32,8,512]{2,1,0:T(8,128)(2,1)S(1)} all-to-all(bf16[32,8,512]{2,1,0:T(8,128)(2,1)S(1)} %bitcast.84), channel_id=1, replica_groups=mesh['y'=4,'z'=8,'x'=4,'core'=2] {'y','z'}, dimensions={0} | all-to-all | bytes 524288 | tf_op jit(solution)/shard_map/all_to_all | solution.py:29
  84.2 0.1 reduce_sum.117
  84.3 14.1 %all_to_all.79 = bf16[32,8,512]{2,1,0:T(8,128)(2,1)S(1)} all-to-all(bf16[32,8,512]{2,1,0:T(8,128)(2,1)S(1)} %broadcast_in_dim.49), channel_id=1, replica_groups=mesh['y'=4,'z'=8,'x'=4,'core'=2] {'y','z'}, dimensions={0} | all-to-all | bytes 524288 | tf_op jit(solution)/shard_map/all_to_all | solution.py:29
  98.4 0.4 convolution_convert_fusion.5
  98.9 0.2 reduce-precision_convert_fusion.1
  99.1 0.1 pad_maximum_fusion.5
  99.2 7.5 %all_to_all.80.arrived_ref = bf16[4,64,384]{2,1,0:T(8,128)(2,1)S(1)} all-to-all(bf16[4,64,384]{2,1,0:T(8,128)(2,1)S(1)} %broadcast_in_dim.50), channel_id=1, replica_groups=mesh['y'=4,'z'=8,'x'=4,'core'=2] {'x'}, dimensions={0} | all-to-all | bytes 393216 | tf_op jit(solution)/shard_map/all_to_all | solution.py:29
  106.7 1.7 normalized_forward.1
  108.5 12.5 %all_to_all.81 = bf16[8,64,256]{2,1,0:T(8,128)(2,1)S(1)} all-to-all(bf16[8,64,256]{2,1,0:T(8,128)(2,1)S(1)} %broadcast_in_dim.51), channel_id=1, replica_groups=mesh['y'=4,'z'=8,'x'=4,'core'=2] {'z'}, dimensions={0} | all-to-all | bytes 524288 | tf_op jit(solution)/shard_map/all_to_all | solution.py:29
  121.0 0.4 convolution_convert_fusion.4
  121.5 7.2 %all_to_all.82 = bf16[4,64,256]{2,1,0:T(8,128)(2,1)S(1)} all-to-all(bf16[4,64,256]{2,1,0:T(8,128)(2,1)S(1)} %broadcast_in_dim.52), channel_id=1, replica_groups=mesh['y'=4,'z'=8,'x'=4,'core'=2] {'y'}, dimensions={0} | all-to-all | bytes 262144 | tf_op jit(solution)/shard_map/all_to_all | solution.py:29
  128.7 0.3 convolution_convert_fusion.1
  129.0 11.7 %all_to_all.83 = bf16[8,64,256]{2,1,0:T(8,128)(2,1)S(1)} all-to-all(bf16[8,64,256]{2,1,0:T(8,128)(2,1)S(1)} %bitcast.79), channel_id=1, replica_groups=mesh['y'=4,'z'=8,'x'=4,'core'=2] {'z'}, dimensions={0} | all-to-all | bytes 524288 | tf_op jit(solution)/shard_map/all_to_all | solution.py:29
  140.8 7.2 %all_to_all.84 = bf16[4,64,256]{2,1,0:T(8,128)(2,1)S(1)} all-to-all(bf16[4,64,256]{2,1,0:T(8,128)(2,1)S(1)} %broadcast_in_dim.53), channel_id=1, replica_groups=mesh['y'=4,'z'=8,'x'=4,'core'=2] {'x'}, dimensions={0} | all-to-all | bytes 262144 | tf_op jit(solution)/shard_map/all_to_all | solution.py:29
  148.1 0.3 convolution_convert_fusion
  148.4 12.6 %all_to_all.85 = bf16[32,8,512]{2,1,0:T(8,128)(2,1)S(1)} all-to-all(bf16[32,8,512]{2,1,0:T(8,128)(2,1)S(1)} %bitcast.82), channel_id=1, replica_groups=mesh['y'=4,'z'=8,'x'=4,'core'=2] {'y','z'}, dimensions={0} | all-to-all | bytes 524288 | tf_op jit(solution)/shard_map/all_to_all | solution.py:29
  161.0 0.1 reduce_sum.121
  161.1 14.5 %all_to_all.86 = bf16[32,8,512]{2,1,0:T(8,128)(2,1)S(1)} all-to-all(bf16[32,8,512]{2,1,0:T(8,128)(2,1)S(1)} %broadcast_in_dim.54), channel_id=1, replica_groups=mesh['y'=4,'z'=8,'x'=4,'core'=2] {'y','z'}, dimensions={0} | all-to-all | bytes 524288 | tf_op jit(solution)/shard_map/all_to_all | solution.py:29
  175.6 0.2 reduce-precision_convert_fusion
  175.8 14.4 %collective-permute-start.7 = (bf16[64,1024]{1,0:T(8,128)(2,1)S(1)}, bf16[64,1024]{1,0:T(8,128)(2,1)S(1)}, u32[]{:S(2)}, u32[]{:S(2)}) collective-permute-start(bf16[64,1024]{1,0:T(8,128)(2,1)S(1)} %slice.55), channel_id=1, source_target_pairs={{0,1},{1,0},{2,3},{3,2},{4,5},{5,4},{6,7},{7,6},{8,9},{9,8},{10,11... | collective-permute-start | bytes 393224 | tf_op jit(solution)/shard_map/ppermute | solution.py:306
  190.2 0.1 pad_maximum_fusion.6
  190.3 7.6 %all_to_all.87.arrived_ref = bf16[8,64,128]{2,1,0:T(8,128)(2,1)S(1)} all-to-all(bf16[8,64,128]{2,1,0:T(8,128)(2,1)S(1)} %broadcast_in_dim.102), channel_id=1, replica_groups=mesh['y'=4,'z'=8,'x'=4,'core'=2] {'x','core'}, dimensions={0} | all-to-all | bytes 262144 | tf_op jit(solution)/shard_map/all_to_all | solution.py:29
  198.0 0.0 collective-permute-done.7.there_ref
  198.0 2.8 %normalized_panels.1 = f32[2,64,1024]{2,1,0:T(8,128)} custom-call(bf16[8,64,128]{2,1,0:T(8,128)(2,1)S(1)} %all_to_all.87.arrived_ref, bf16[64,2048]{1,0:T(8,128)(2,1)S(1)} %bitcast.73, bf16[64,1024]{1,0:T(8,128)(2,1)S(1)} %collective-permute-done.7.there_ref), custom_call_target="tpu_custom_call" | custom-call | tf_op jit(solution)/shard_map/normalized_panels/pallas_call | solution.py:197
  (35 shorter events, 0.7 us)
Async XLA Ops:
  1.3 5.6 %copy-start = (f32[2,2,256]{2,1,0:T(2,128)S(1)}, f32[2,2,256]{2,1,0:T(2,128)}, u32[]{:S(2)}) copy-start(f32[2,2,256]{2,1,0:T(2,128)} %param.4) | copy-start | bytes 12292
  1.4 10.5 %collective-permute-start.2 = (bf16[128,1024]{1,0:T(8,128)(2,1)S(1)}, bf16[128,1024]{1,0:T(8,128)(2,1)S(1)}, u32[]{:S(2)}, u32[]{:S(2)}) collective-permute-start(bf16[128,1024]{1,0:T(8,128)(2,1)S(1)} %pad_maximum_fusion.4), channel_id=1, source_target_pairs={{0,1},{1,0},{2,3},{3,2},{4,5},{5,4},{6,7},{7,6},{8,9},{9,8},{10,11... | collective-permute-start | bytes 786440 | tf_op jit(solution)/shard_map/ppermute | solution.py:258
  4.7 23.7 %collective-permute-start.1 = (bf16[256,1024]{1,0:T(8,128)(2,1)S(1)}, bf16[256,1024]{1,0:T(8,128)(2,1)S(1)}, u32[]{:S(2)}, u32[]{:S(2)}) collective-permute-start(bf16[256,1024]{1,0:T(8,128)(2,1)S(1)} %get-tuple-element.14), channel_id=1, source_target_pairs={{0,1},{1,0},{2,3},{3,2},{4,5},{5,4},{6,7},{7,6},{8,9},{9,8},{10,11... | collective-permute-start | bytes 1572872 | tf_op jit(solution)/shard_map/ppermute | solution.py:268
  6.4 1.4 collective-permute-start
  8.5 8.4 %all-to-all-start = ((bf16[4,64,256]{2,1,0:T(8,128)(2,1)}), bf16[4,64,256]{2,1,0:T(8,128)(2,1)S(1)}, u32[]{:S(2)}, u32[]{:S(2)}) async-start(bf16[4,64,256]{2,1,0:T(8,128)(2,1)} %broadcast_in_dim.40), calls=%async_computation | async-start | bytes 262144 | tf_op jit(solution)/shard_map/all_to_all | solution.py:29
  12.0 15.6 %collective-permute-start.3 = (bf16[64,2048]{1,0:T(8,128)(2,1)S(1)}, bf16[64,2048]{1,0:T(8,128)(2,1)S(1)}, u32[]{:S(2)}, u32[]{:S(2)}) collective-permute-start(bf16[64,2048]{1,0:T(8,128)(2,1)S(1)} %get-tuple-element.19), channel_id=1, source_target_pairs={{0,0},{1,5},{2,64},{3,69},{4,128},{5,133},{6,192},{7,197},{64,2},{... | collective-permute-start | bytes 786440 | tf_op jit(solution)/shard_map/ppermute | solution.py:263
  16.9 10.9 %collective-permute-start.5 = (bf16[64,2048]{1,0:T(8,128)(2,1)S(1)}, bf16[64,2048]{1,0:T(8,128)(2,1)S(1)}, u32[]{:S(2)}, u32[]{:S(2)}) collective-permute-start(bf16[64,2048]{1,0:T(8,128)(2,1)S(1)} %get-tuple-element.20), channel_id=1, source_target_pairs={{0,2},{1,7},{2,66},{3,71},{4,130},{5,135},{6,194},{7,199},{64,4},{... | collective-permute-start | bytes 786440 | tf_op jit(solution)/shard_map/ppermute | solution.py:263
  19.4 20.6 %all-to-all-start.1 = ((bf16[8,64,256]{2,1,0:T(8,128)(2,1)}), bf16[8,64,256]{2,1,0:T(8,128)(2,1)S(1)}, u32[]{:S(2)}, u32[]{:S(2)}) async-start(bf16[8,64,256]{2,1,0:T(8,128)(2,1)} %broadcast_in_dim.41), calls=%async_computation.1 | async-start | bytes 524288 | tf_op jit(solution)/shard_map/all_to_all | solution.py:29
  27.6 12.5 %collective-permute-start.4 = (bf16[64,2048]{1,0:T(8,128)(2,1)S(1)}, bf16[64,2048]{1,0:T(8,128)(2,1)S(1)}, u32[]{:S(2)}, u32[]{:S(2)}) collective-permute-start(bf16[64,2048]{1,0:T(8,128)(2,1)S(1)} %collective-permute-done.3), channel_id=1, source_target_pairs={{0,1},{1,0},{2,3},{3,2},{4,5},{5,4},{6,7},{7,6},{8,9},{9,8},{10,11... | collective-permute-start | bytes 786440 | tf_op jit(solution)/shard_map/ppermute | solution.py:264
  27.7 12.4 %collective-permute-start.6 = (bf16[64,2048]{1,0:T(8,128)(2,1)S(1)}, bf16[64,2048]{1,0:T(8,128)(2,1)}, u32[]{:S(2)}, u32[]{:S(2)}) collective-permute-start(bf16[64,2048]{1,0:T(8,128)(2,1)S(1)} %collective-permute-done.5), channel_id=1, source_target_pairs={{0,1},{1,0},{2,3},{3,2},{4,5},{5,4},{6,7},{7,6},{8,9},{9,8},{10,11... | collective-permute-start | bytes 786440 | tf_op jit(solution)/shard_map/ppermute | solution.py:264
  175.8 22.1 %collective-permute-start.7 = (bf16[64,1024]{1,0:T(8,128)(2,1)S(1)}, bf16[64,1024]{1,0:T(8,128)(2,1)S(1)}, u32[]{:S(2)}, u32[]{:S(2)}) collective-permute-start(bf16[64,1024]{1,0:T(8,128)(2,1)S(1)} %slice.55), channel_id=1, source_target_pairs={{0,1},{1,0},{2,3},{3,2},{4,5},{5,4},{6,7},{7,6},{8,9},{9,8},{10,11... | collective-permute-start | bytes 393224 | tf_op jit(solution)/shard_map/ppermute | solution.py:306
